TPU v7x, 512 devices: a 4x2x32 block of a 4x8x32 slice. The times are simulated.
512 devices in a mesh: group: 2 (over y), ctx: 32 (over z), head: 4 (over x), dec: 2 (over core).
Axes of the slice: x: 4, y: 2, z: 32, core: 2. Of those that a mesh axis runs over, the one named last changes fastest.
The devices are a block of a 4x8x32 slice.
Arguments:
- queries: bfloat16 [8192, 12288], P(('group', 'ctx'), ('head', 'dec')), parts along dimension 0, may hold values from -1100 to 1100
- latent_rows: bfloat16 [8192, 576], P(('group', 'ctx')), parts along dimension 0, may hold values from -8 to 8
- segments: int32 [8192], P('group'), parts along dimension 0, may hold values from 0 to 3, never falling along the last dimension, each value on 1 to 2048 neighbouring positions
- owners: int32 [8192, 1], P(('group', 'ctx')), parts along dimension 0, may hold values from 0 to 63; in each aligned block of 128 rows (0 to 127, 128 to 255, ...) at most 4 rows name the same one
- absorb_key: bfloat16 [64, 128, 512], P(('head', 'dec')), may hold values from -0.5 to 0.5
- absorb_value: bfloat16 [64, 512, 128], P(('head', 'dec')), may hold values from -0.25 to 0.25
Outputs:
- attended: bfloat16 [8192, 8192], P(('group', 'ctx'), ('head', 'dec')), parts along dimension 0
- kv_cache: bfloat16 [128, 32, 4, 576], P(('group', 'ctx', 'dec')), parts along dimension 0
There are 2 independent parts, one for each index of `group`. A program takes and returns all parts, laid end to end along the dimension named above; an argument that names none is the same for every part. Nothing has to cross between parts.
Inputs may be any that keep to these rules, and one draw needn't show every extreme that they name: `segments`: prompt numbers never fall along the tokens; each prompt has 1 to 2048 tokens and one has exactly 2048. `owners`: among the 128 tokens of one index of ctx no owner is named more than 4 times; some owner is named exactly 4 times in some of them; every owner is named somewhere.
All inputs are finite; a program needn't handle non-finite values.
Results may differ from a plain program's by a relative error of at most 0.0085.
Values may be sent and summed in bfloat16 or wider, within the bound.
No kernel may reach another device: no remote copies, remote signals or barrier semaphores. Data moves between devices by JAX's collectives and lax.ppermute only.
A program may use at most 128 MiB of HBM per device.

v0:
```python
import jax
import jax.numpy as jnp
from jax import lax
from jax.sharding import PartitionSpec as P

NOPE = 128
ROPE = 64
LATENT = 512
VDIM = 128


def rotate_pairs(rope_part, positions):
    half_rope = ROPE // 2
    frequency = 10000.0 ** (-jnp.arange(half_rope, dtype=jnp.float32) * 2.0 / ROPE)
    angles = positions.astype(jnp.float32)[:, None] * frequency[None, :]
    cosine = jnp.cos(angles)[:, None, :]
    sine_part = jnp.sin(angles)[:, None, :]
    first_part = rope_part[..., :half_rope]
    second = rope_part[..., half_rope:]
    return jnp.concatenate(
        [first_part * cosine - second * sine_part, first_part * sine_part + second * cosine],
        axis=-1,
    )


def ship_rows(latent_rows, owners):
    row_count = latent_rows.shape[0]
    ctx_count = lax.axis_size("ctx")
    dec_count = lax.axis_size("dec")
    core_index = lax.axis_index("dec")
    slots = max(2, 2 * row_count // (ctx_count * dec_count))
    owner_ids = owners[:, 0]
    row_order = jnp.arange(row_count, dtype=jnp.int32)
    earlier = row_order[None, :] < row_order[:, None]
    slot_rank = jnp.sum((owner_ids[:, None] == owner_ids[None, :]) & earlier, axis=1)
    target = owner_ids // dec_count * slots + slot_rank
    kept_rows = owner_ids % dec_count == core_index
    picker = (
        (jnp.arange(ctx_count * slots, dtype=jnp.int32)[:, None] == target[None, :])
        & kept_rows[None, :]
    ).astype(jnp.bfloat16)
    outgoing = jnp.dot(picker, latent_rows, preferred_element_type=jnp.float32).astype(jnp.bfloat16)
    outgoing = outgoing.reshape(ctx_count, slots, LATENT + ROPE)
    arrived = lax.all_to_all(outgoing, "ctx", split_axis=0, concat_axis=0, tiled=True)
    return arrived[None]


def on_device(queries, latent_rows, segments, owners, absorb_key, absorb_value):
    row_count = queries.shape[0]
    local_heads = absorb_key.shape[0]
    width = LATENT + ROPE
    ctx_index = lax.axis_index("ctx")
    scale = (NOPE + ROPE) ** (-0.5)
    shaped = queries.reshape(row_count, local_heads, NOPE + ROPE)
    offsets = jnp.arange(row_count, dtype=jnp.int32)
    query_pos = ctx_index * row_count + offsets
    query_seg = jnp.take(segments, query_pos)
    rotated = rotate_pairs(shaped[..., NOPE:].astype(jnp.float32), query_pos).astype(jnp.bfloat16)
    absorbed = jnp.einsum(
        "thn,hnc->thc", shaped[..., :NOPE], absorb_key, preferred_element_type=jnp.float32
    ).astype(jnp.bfloat16)
    full_query = jnp.concatenate([absorbed, rotated], axis=-1).reshape(
        row_count * local_heads, width
    )
    last_query = jnp.max(query_pos)
    lowest_seg = jnp.min(query_seg)
    highest_seg = jnp.max(query_seg)
    start_state = (
        jnp.full((row_count, local_heads), -1e30, jnp.float32),
        jnp.zeros((row_count, local_heads), jnp.float32),
        jnp.zeros((row_count, local_heads, LATENT), jnp.float32),
    )
    key_piece = lax.all_gather(latent_rows, "ctx", axis=0, tiled=True)
    count = key_piece.shape[0]
    key_pos = jnp.arange(count, dtype=jnp.int32)
    is_live = (
        (jnp.int32(0) <= last_query)
        & (segments[count - 1] >= lowest_seg)
        & (segments[0] <= highest_seg)
    )

    def update(carried):
        running_max, running_sum, running_out = carried
        scores = jnp.einsum("qw,kw->qk", full_query, key_piece, preferred_element_type=jnp.float32)
        scores = scores.reshape(row_count, local_heads, count) * scale
        allowed = (
            (key_pos[None, :] <= query_pos[:, None]) & (segments[None, :] == query_seg[:, None])
        )[:, None, :]
        masked = jnp.where(allowed, scores, -1e30)
        new_max = jnp.maximum(running_max, jnp.max(masked, axis=2))
        weights = jnp.where(allowed, jnp.exp(masked - new_max[..., None]), 0.0)
        new_sum = jnp.sum(weights, axis=2)
        mixed = jnp.dot(
            weights.astype(jnp.bfloat16).reshape(row_count * local_heads, count),
            key_piece[:, :LATENT],
            preferred_element_type=jnp.float32,
        )
        new_out = mixed.reshape(row_count, local_heads, LATENT)
        return (new_max, new_sum, new_out)

    final_state = lax.cond(is_live, update, lambda carried: carried, start_state)
    running_max, running_sum, running_out = final_state
    latent_out = (running_out / running_sum[..., None]).astype(jnp.bfloat16)
    answer = jnp.einsum(
        "thc,hcv->thv", latent_out, absorb_value, preferred_element_type=jnp.float32
    ).astype(jnp.bfloat16)
    answer = answer.reshape(row_count, local_heads * VDIM)
    kv_cache = ship_rows(latent_rows, owners)
    return (answer, kv_cache)


def solution(mesh):
    in_specs = (
        P(("group", "ctx"), ("head", "dec")),
        P(("group", "ctx"), None),
        P("group"),
        P(("group", "ctx"), None),
        P(("head", "dec"), None, None),
        P(("head", "dec"), None, None),
    )
    out_specs = (P(("group", "ctx"), ("head", "dec")), P(("group", "ctx", "dec"), None, None, None))
    return jax.shard_map(
        on_device, mesh=mesh, in_specs=in_specs, out_specs=out_specs, check_vma=False
    )
```

profile of v0, /device:TPU:44, one launch (start us, length us, event | category | flops | bytes accessed | tf_op | source)
XLA Modules:
  0.0 235.0 jit_solution(2218947732454641080)
XLA Ops:
  7.3 1.8 copy.31
  9.1 0.9 convert_reduce_fusion
  10.0 0.7 fusion.22
  10.7 0.7 multiply_add_fusion
  11.4 1.1 convolution_convert_fusion.2
  12.6 0.7 reshape.219
  13.4 45.8 %all-to-all-start = ((bf16[32,4,576]{2,1,0:T(4,128)(2,1)}), bf16[32,4,576]{2,1,0:T(4,128)(2,1)S(1)}, u32[]{:S(2)}, u32[]{:S(2)}) async-start(bf16[32,4,576]{2,1,0:T(4,128)(2,1)} %reshape.219), calls=%async_computation | async-start | bytes 327680 | tf_op jit(solution)/shard_map/all_to_all | solution.py:44
  59.2 1.6 gather_fusion
  60.8 0.7 fusion.24
  61.5 1.3 fusion.27
  62.9 0.7 fusion.26
  63.6 1.2 copy.28
  68.2 0.5 fusion.14
  68.7 1.1 pad_maximum_fusion
  69.8 24.9 %all-to-all-done = bf16[32,4,576]{2,1,0:T(4,128)(2,1)S(1)} async-done(((bf16[32,4,576]{2,1,0:T(4,128)(2,1)}), bf16[32,4,576]{2,1,0:T(4,128)(2,1)S(1)}, u32[]{:S(2)}, u32[]{:S(2)}) %all-to-all-start) | async-done | bytes 147488 | tf_op jit(solution)/shard_map/all_to_all | solution.py:44
  94.7 93.2 %all-gather.2.cloned.1.call-done = bf16[4096,576]{1,0:T(8,128)(2,1)} async-done(((bf16[128,576]{1,0:T(8,128)(2,1)}), bf16[4096,576]{1,0:T(8,128)(2,1)}) %all-gather.2.cloned.1.call-update) | async-done | bytes 4718608 | tf_op jit(solution)/shard_map/all_gather | solution.py:73
  187.9 36.4 %conditional.1 = (f32[128,8]{1,0:T(8,128)S(1)}, f32[128,8,512]{2,1,0:T(8,128)S(1)}) conditional(s32[]{:T(128)} %convert_element_type.40, () %tuple.16, (s32[4096]{0:T(1024)S(1)}, s32[128]{0:T(128)S(1)}, s32[4096]{0:T(1024)S(1)}, s32[128]{0:T(128)S(1)}, bf16[128,8,576]{0,2,1:T(8,128)(2,1)}, /*index=5*/bf16[4096,576]{1,0:T(8,128)(2,1)}) %tuple.39), branch_computations={%region_3.4_spmd, %region_4.0_spmd} | conditional | flops 9182903296 | bytes 71238728 | solution.py:101
  188.4 2.4 %copy.32 = bf16[128,8,576]{2,1,0:T(8,128)(2,1)S(1)} copy(bf16[128,8,576]{0,2,1:T(8,128)(2,1)} %get-tuple-element.45) | data formatting | bytes 2359296 | tf_op jit(solution)/shard_map
  190.8 13.9 %fusion = (f32[1024]{0:T(1024)S(1)}, f32[1024,4096]{1,0:T(8,128)}) fusion(pred[128,4096]{1,0:T(8,128)(4,1)S(1)} %compare_and_fusion, bf16[4096,576]{1,0:T(8,128)(2,1)} %get-tuple-element.18, bf16[128,8,576]{2,1,0:T(8,128)(2,1)S(1)} %copy.32), kind=kOutput, calls=%fused_computation.3 | convolution fusion | flops 4844420096 | bytes 23203840 | tf_op jit(solution)/shard_map/cond/branch_1_fun/qw,kw->qk/dot_general | solution.py:84
  204.7 10.4 %fusion.4 = f32[128,8,512]{2,1,0:T(8,128)S(1)} fusion(f32[1024,4096]{1,0:T(8,128)} %get-tuple-element.53, f32[1024]{0:T(1024)S(1)} %broadcast_maximum_fusion, pred[128,4096]{1,0:T(8,128)(4,1)} %copy-done.2, bf16[4096,576]{1,0:T(8,128)(2,1)} %get-tuple-element.18), kind=kOutput, calls=%fused_computation.7 | convolution fusion | flops 4315938816 | bytes 23597056 | tf_op jit(solution)/shard_map/cond/branch_1_fun/dot_general | solution.py:93
  215.1 9.1 %fusion.2 = f32[1024]{0:T(1024)S(1)} fusion(f32[1024,4096]{1,0:T(8,128)} %get-tuple-element.53, f32[1024]{0:T(1024)S(1)} %broadcast_maximum_fusion, pred[128,4096]{1,0:T(8,128)(4,1)S(1)} %copy-done.3), kind=kLoop, calls=%fused_computation.5 | loop fusion | flops 20970496 | bytes 17309696 | tf_op jit(solution)/shard_map/cond/branch_1_fun/reduce_sum | solution.py:92
  224.5 2.2 convolution_convert_fusion.1
  226.7 0.9 copy.36
  227.5 0.7 copy.47
  (22 shorter events, 1.3 us)
Async XLA Ops:
  7.2 61.0 %copy-start = (bf16[8,128,512]{2,1,0:T(8,128)(2,1)S(1)}, bf16[8,128,512]{2,1,0:T(8,128)(2,1)}, u32[]{:S(2)}) copy-start(bf16[8,128,512]{2,1,0:T(8,128)(2,1)} %param.12) | copy-start | bytes 3145732
  7.2 180.7 %copy-start.1 = (s32[4096]{0:T(1024)S(1)}, s32[4096]{0:T(1024)}, u32[]{:S(2)}) copy-start(s32[4096]{0:T(1024)} %param.10) | copy-start | bytes 49156
  7.2 180.7 %all-gather.2.cloned.1.call-start = ((), (), s32[]{:S(2)}) async-start(), calls=%async_computation.1 | async-start | bytes 5406720 | tf_op jit(solution)/shard_map/all_gather | solution.py:73
  13.4 81.3 %all-to-all-start = ((bf16[32,4,576]{2,1,0:T(4,128)(2,1)}), bf16[32,4,576]{2,1,0:T(4,128)(2,1)S(1)}, u32[]{:S(2)}, u32[]{:S(2)}) async-start(bf16[32,4,576]{2,1,0:T(4,128)(2,1)} %reshape.219), calls=%async_computation | async-start | bytes 327680 | tf_op jit(solution)/shard_map/all_to_all | solution.py:44
  188.4 16.3 %copy-start.2 = (pred[128,4096]{1,0:T(8,128)(4,1)}, pred[128,4096]{1,0:T(8,128)(4,1)S(1)}, u32[]{:S(2)}) copy-start(pred[128,4096]{1,0:T(8,128)(4,1)S(1)} %compare_and_fusion) | copy-start | bytes 1572868 | tf_op jit(solution)/shard_map/cond
  204.7 10.4 %copy-start.3 = (pred[128,4096]{1,0:T(8,128)(4,1)S(1)}, pred[128,4096]{1,0:T(8,128)(4,1)}, u32[]{:S(2)}) copy-start(pred[128,4096]{1,0:T(8,128)(4,1)} %copy-done.2) | copy-start | bytes 1572868 | tf_op jit(solution)/shard_map/cond
Sparse Core Ops, SparseCore 0:
  10.7 177.1 all-gather.1
where the time goes:
time: 236 us; the launch traced here: 235 us
  waiting for transfers between devices  118 us (50%)
  starting transfers between devices  45.8 us (19%)
  matrix products  28.1 us (12%)
  between operations  17.3 us (7%)
  other arithmetic  14.7 us (6%)
  local copies, waits for them, and re-layouts  10.9 us (5%)
    all_gather x1, waiting for transfers between devices, on_device(): key_piece = lax.all_gather(latent_rows, 'ctx', axis=0, tiled=True)  93.2 us
    all_to_all x1, starting transfers between devices, ship_rows(): lax.all_to_all(outgoing, 'ctx', split_axis=0, concat_axis=0, tiled=True)  45.8 us
    all_to_all x1, waiting for transfers between devices, ship_rows(): lax.all_to_all(outgoing, 'ctx', split_axis=0, concat_axis=0, tiled=True)  24.9 us
    dot_general x1, matrix products, update(): jnp.einsum('qw,kw->qk', full_query, key_piece, preferred_element_type=jnp...  13.9 us
    dot_general x1, matrix products, update(): jnp.dot(weights.astype(jnp.bfloat16).reshape(row_count * local_heads, cou...  10.4 us
    reduce_sum x1, other arithmetic, update(): new_sum = jnp.sum(weights, axis=2)  9.08 us
  transfers between devices with their start and end apart: 2, of which 2 were waited for; matrix products, arithmetic and copies ran while one was open for 5% of the time, Pallas kernels for 0%

commit v1 on v0

v1 whole, which is shorter than its diff:
```python
import jax
import jax.numpy as jnp
from jax import lax
from jax.experimental import pallas as pl
from jax.experimental.pallas import tpu as pltpu
from jax.sharding import PartitionSpec as P

NOPE = 128
ROPE = 64
LATENT = 512
VDIM = 128
WIDTH = LATENT + ROPE
HEAD_IN = NOPE + ROPE
PROMPT = 2048
NEG = -1e30
LOG2E = 1.4426950408889634
EVEN = (2, 10, 6, 14, 8, 4, 12)
ODD = (1, 9, 5, 13, 3, 11, 7, 15, 16)


def query_kernel(ctx_ref, q_ref, ak_ref, cos_ref, sin_ref, seg_ref, fq_ref, start_ref):
    heads = ak_ref.shape[0]
    rows = q_ref.shape[0]
    cos2 = cos_ref[...]
    sin2 = sin_ref[...]
    half = ROPE // 2
    for h in range(heads):
        piece = q_ref[:, h * HEAD_IN:(h + 1) * HEAD_IN]
        absorbed = jnp.dot(piece[:, :NOPE], ak_ref[h], preferred_element_type=jnp.float32)
        fq_ref[h, :, :LATENT] = absorbed.astype(jnp.bfloat16)
        x = piece[:, NOPE:].astype(jnp.float32)
        swapped = jnp.concatenate([x[:, half:], x[:, :half]], axis=1)
        fq_ref[h, :, LATENT:] = (x * cos2 + swapped * sin2).astype(jnp.bfloat16)
    own = seg_ref[pl.ds(ctx_ref[0], 1), :]
    own = jnp.broadcast_to(own, (rows, rows)).T
    below = jnp.zeros((rows, rows), jnp.int32)
    for b in range(seg_ref.shape[0]):
        below = below + (seg_ref[b:b + 1, :] < own).astype(jnp.int32)
    start = jnp.sum(below, axis=1, keepdims=True)
    start_ref[...] = jnp.broadcast_to(start, (rows, rows))


def pick_kernel(core_ref, owner_ref, latent_ref, out_ref, *, cores, slots):
    rows = latent_ref.shape[0]
    own = jnp.broadcast_to(owner_ref[...], (rows, rows))
    across = own.T
    down_id = lax.broadcasted_iota(jnp.int32, (rows, rows), 0)
    across_id = lax.broadcasted_iota(jnp.int32, (rows, rows), 1)
    hit = ((own == across) & (down_id < across_id)).astype(jnp.int32)
    rank = jnp.sum(hit, axis=0, keepdims=True)
    name = across[:1, :]
    target = name // cores * slots + rank
    target = jnp.where(name % cores == core_ref[0], target, -1)
    slot_id = lax.broadcasted_iota(jnp.int32, (out_ref.shape[0], rows), 0)
    picker = (slot_id == target).astype(jnp.float32).astype(jnp.bfloat16)
    out_ref[...] = jnp.dot(
        picker, latent_ref[...], preferred_element_type=jnp.float32
    ).astype(jnp.bfloat16)


def place(pieces, replicas, keys_ref, count):
    for piece, replica in zip(pieces, replicas):
        for b in range(count):
            at = pl.multiple_of(b * 128 + replica * 16, 16)
            keys_ref[pl.ds(at, 16), :] = piece[b * 16:(b + 1) * 16, :]


def fill_bias(bias_ref, start, ctx, dists, own_block):
    rows = start.shape[0]
    lane = lax.broadcasted_iota(jnp.int32, (rows, rows), 1)
    for b, dist in enumerate(dists):
        pos = (ctx - dist) * rows + lane
        bias_ref[:, b * rows:(b + 1) * rows] = jnp.where(pos >= start, 0.0, NEG)
    if own_block:
        b = len(dists)
        pos = ctx * rows + lane
        down = lax.broadcasted_iota(jnp.int32, (rows, rows), 0)
        bias_ref[:, b * rows:(b + 1) * rows] = jnp.where(
            (pos >= start) & (lane <= down), 0.0, NEG
        )


def score(fq_ref, h, n, keys_ref, bias_ref):
    rows = fq_ref.shape[1]
    q = fq_ref[h:h + n].reshape(n * rows, WIDTH)
    s = lax.dot_general(
        q, keys_ref[...], (((1,), (1,)), ((), ())), preferred_element_type=jnp.float32
    )
    return s.reshape(n, rows, -1) + bias_ref[...][None]


def first_kernel(meta_ref, fq_ref, start_ref, latent_ref, near_ref, far_ref,
                 max_ref, sum_ref, acc_ref, keys_ref, bias_ref, *, scale, group):
    count = len(EVEN)
    heads, rows = fq_ref.shape[0], fq_ref.shape[1]
    piece = count * 16
    for i in range(4):
        place([near_ref[i * piece:(i + 1) * piece, :], far_ref[i * piece:(i + 1) * piece, :]],
              [meta_ref[1 + i], meta_ref[5 + i]], keys_ref, count)
    keys_ref[count * rows:, :] = latent_ref[...]
    fill_bias(bias_ref, start_ref[...], meta_ref[0], EVEN, True)
    factor = scale * LOG2E
    for h in range(0, heads, group):
        s = score(fq_ref, h, group, keys_ref, bias_ref)
        top = jnp.max(s, axis=2, keepdims=True)
        p = jnp.exp2((s - top) * factor)
        total = jnp.sum(p, axis=2, keepdims=True)
        acc = jnp.dot(
            p.astype(jnp.bfloat16).reshape(group * rows, -1), keys_ref[:, :LATENT],
            preferred_element_type=jnp.float32,
        )
        acc_ref[h:h + group] = acc.reshape(group, rows, LATENT)
        max_ref[h:h + group] = jnp.broadcast_to(top, (group, rows, 128))
        sum_ref[h:h + group] = jnp.broadcast_to(total, (group, rows, 128))


def second_kernel(meta_ref, fq_ref, start_ref, max_ref, sum_ref, acc_ref, near_ref, far_ref,
                  av_ref, out_ref, keys_ref, bias_ref, *, scale, group):
    count = len(ODD)
    heads, rows = fq_ref.shape[0], fq_ref.shape[1]
    piece = count * 16
    for i in range(4):
        place([near_ref[i * piece:(i + 1) * piece, :], far_ref[i * piece:(i + 1) * piece, :]],
              [meta_ref[1 + i], meta_ref[5 + i]], keys_ref, count)
    fill_bias(bias_ref, start_ref[...], meta_ref[0], ODD, False)
    factor = scale * LOG2E
    for h in range(0, heads, group):
        s = score(fq_ref, h, group, keys_ref, bias_ref)
        before = max_ref[h:h + group][:, :, :1]
        top = jnp.maximum(before, jnp.max(s, axis=2, keepdims=True))
        p = jnp.exp2((s - top) * factor)
        keep = jnp.exp2((before - top) * factor)
        total = sum_ref[h:h + group][:, :, :1] * keep + jnp.sum(p, axis=2, keepdims=True)
        acc = jnp.dot(
            p.astype(jnp.bfloat16).reshape(group * rows, -1), keys_ref[:, :LATENT],
            preferred_element_type=jnp.float32,
        ).reshape(group, rows, LATENT)
        mixed = (acc + acc_ref[h:h + group] * keep) / total
        mixed = mixed.astype(jnp.bfloat16)
        for g in range(group):
            out_ref[:, (h + g) * VDIM:(h + g + 1) * VDIM] = jnp.dot(
                mixed[g], av_ref[h + g], preferred_element_type=jnp.float32
            ).astype(jnp.bfloat16)


def vmem(n):
    return [pl.BlockSpec(memory_space=pltpu.VMEM) for _ in range(n)]


SMEM = pl.BlockSpec(memory_space=pltpu.SMEM)


def on_device(queries, latent_rows, segments, owners, absorb_key, absorb_value):
    rows = queries.shape[0]
    heads = absorb_key.shape[0]
    ctx_count = lax.axis_size("ctx")
    head_count = lax.axis_size("head")
    dec_count = lax.axis_size("dec")
    ctx = lax.axis_index("ctx")
    head = lax.axis_index("head")
    core = lax.axis_index("dec")
    scale = (NOPE + ROPE) ** (-0.5)
    bf16 = jnp.bfloat16

    slots = max(2, 2 * rows // (ctx_count * dec_count))
    outgoing = pl.pallas_call(
        lambda *refs: pick_kernel(*refs, cores=dec_count, slots=slots),
        out_shape=jax.ShapeDtypeStruct((ctx_count * slots, WIDTH), bf16),
        in_specs=[SMEM] + vmem(2), out_specs=vmem(1)[0], name="pick",
    )(core[None], owners, latent_rows)
    outgoing = outgoing.reshape(ctx_count, slots, WIDTH)
    arrived = lax.all_to_all(outgoing, "ctx", split_axis=0, concat_axis=0, tiled=True)

    replica = head * dec_count + core
    share = rows // (head_count * dec_count)
    own = lax.dynamic_slice_in_dim(latent_rows, replica * share, share, 0)

    def shift(x, k):
        return lax.ppermute(x, "ctx", [(i, i + k) for i in range(ctx_count - k)])

    cat = lambda *xs: jnp.concatenate(xs, axis=0)
    d8 = shift(own, 8)
    d4 = shift(cat(own, d8), 4)
    four = cat(own, d8, d4)
    d2 = shift(four, 2)
    even = cat(d2, d8, d4)
    d1 = shift(cat(own, d8, d4, d2), 1)
    d16 = shift(d2[3 * share:], 2)
    odd = cat(d1, d16)

    def spread(x):
        ring = lambda k: [(i, (i + k) % head_count) for i in range(head_count)]
        near = cat(x, *[lax.ppermute(x, "head", ring(k)) for k in range(1, head_count)])
        far = lax.ppermute(near, "dec", [(i, (i + 1) % dec_count) for i in range(dec_count)])
        return near, far

    near_even, far_even = spread(even)
    near_odd, far_odd = spread(odd)

    half = ROPE // 2
    frequency = 10000.0 ** (-jnp.arange(half, dtype=jnp.float32) * 2.0 / ROPE)
    query_pos = ctx * rows + jnp.arange(rows, dtype=jnp.int32)
    angles = query_pos.astype(jnp.float32)[:, None] * frequency[None, :]
    cosine = jnp.cos(angles)
    sine = jnp.sin(angles)
    cos2 = jnp.concatenate([cosine, cosine], axis=1)
    sin2 = jnp.concatenate([-sine, sine], axis=1)
    full_query, start = pl.pallas_call(
        query_kernel,
        out_shape=(jax.ShapeDtypeStruct((heads, rows, WIDTH), bf16),
                   jax.ShapeDtypeStruct((rows, rows), jnp.int32)),
        in_specs=[SMEM] + vmem(5), out_specs=tuple(vmem(2)), name="query",
    )(ctx[None], queries, absorb_key, cos2, sin2, segments.reshape(-1, rows))

    from_head = [(head - k) % head_count for k in range(head_count)]
    meta = jnp.stack(
        [ctx] + [f * dec_count + core for f in from_head]
        + [f * dec_count + (1 - core) for f in from_head]
    )
    group = 2
    state = pl.pallas_call(
        lambda *refs: first_kernel(*refs, scale=scale, group=group),
        out_shape=(jax.ShapeDtypeStruct((heads, rows, 128), jnp.float32),
                   jax.ShapeDtypeStruct((heads, rows, 128), jnp.float32),
                   jax.ShapeDtypeStruct((heads, rows, LATENT), jnp.float32)),
        in_specs=[SMEM] + vmem(5), out_specs=tuple(vmem(3)),
        scratch_shapes=[pltpu.VMEM(((len(EVEN) + 1) * rows, WIDTH), bf16),
                        pltpu.VMEM((rows, (len(EVEN) + 1) * rows), jnp.float32)],
        name="first",
        cost_estimate=pl.CostEstimate(flops=5_000_000_000, bytes_accessed=6_000_000, transcendentals=1_000_000),
    )(meta, full_query, start, latent_rows, near_even, far_even)
    answer = pl.pallas_call(
        lambda *refs: second_kernel(*refs, scale=scale, group=group),
        out_shape=jax.ShapeDtypeStruct((rows, heads * VDIM), bf16),
        in_specs=[SMEM] + vmem(8), out_specs=vmem(1)[0],
        scratch_shapes=[pltpu.VMEM((len(ODD) * rows, WIDTH), bf16),
                        pltpu.VMEM((rows, len(ODD) * rows), jnp.float32)],
        name="second",
        cost_estimate=pl.CostEstimate(flops=5_000_000_000, bytes_accessed=6_000_000, transcendentals=1_000_000),
    )(meta, full_query, start, *state, near_odd, far_odd, absorb_value)
    return (answer, arrived[None])


def solution(mesh):
    in_specs = (
        P(("group", "ctx"), ("head", "dec")),
        P(("group", "ctx"), None),
        P("group"),
        P(("group", "ctx"), None),
        P(("head", "dec"), None, None),
        P(("head", "dec"), None, None),
    )
    out_specs = (P(("group", "ctx"), ("head", "dec")), P(("group", "ctx", "dec"), None, None, None))
    return jax.shard_map(
        on_device, mesh=mesh, in_specs=in_specs, out_specs=out_specs, check_vma=False
    )
```

time: 236 us -> 158 us (0.67)
  the two profiles are of different devices: /device:TPU:44 before, /device:TPU:33 now
where the time goes in v1:
time: 158 us; the launch traced here: 157 us
  starting transfers between devices  111 us (70%)
  Pallas kernels  22 us (14%)
  waiting for transfers between devices  14.7 us (9%)
  local copies, waits for them, and re-layouts  7.34 us (5%)
    ppermute x5, starting transfers between devices, shift(): return lax.ppermute(x, 'ctx', [(i, i + k) for i in range(ctx_count - k)])  51.8 us
    all_to_all x1, starting transfers between devices, on_device(): lax.all_to_all(outgoing, 'ctx', split_axis=0, concat_axis=0, tiled=True)  31.4 us
    ppermute x6, starting transfers between devices, spread(): lax.ppermute(x, 'head', ring(k))  19.5 us
    pallas_call x1, Pallas kernels, on_device(): pl.pallas_call(lambda *refs: second_kernel(*refs, scale=scale, group=grou...  9.74 us
    ppermute x5, waiting for transfers between devices, shift(): return lax.ppermute(x, 'ctx', [(i, i + k) for i in range(ctx_count - k)])  9.09 us
    ppermute x2, starting transfers between devices, spread(): lax.ppermute(near, 'dec', [(i, (i + 1) % dec_count) for i in range(dec_co...  8.39 us
    pallas_call x1, Pallas kernels, on_device(): pl.pallas_call(lambda *refs: first_kernel(*refs, scale=scale, group=group...  6.94 us
    ppermute x6, waiting for transfers between devices, spread(): lax.ppermute(x, 'head', ring(k))  5.61 us
  transfers between devices with their start and end apart: 14, of which 4 were waited for; matrix products, arithmetic and copies ran while one was open for 3% of the time, Pallas kernels for 14%

profile of v1, /device:TPU:33, one launch (start us, length us, event | category | flops | bytes accessed | tf_op | source)
XLA Modules:
  0.0 157.3 jit_solution(18223412305012584097)
XLA Ops:
  0.6 1.1 copy.18.refs_3_.refs_2_
  1.7 23.2 %collective-permute-start = (bf16[16,576]{1,0:T(8,128)(2,1)S(1)}, bf16[16,576]{1,0:T(8,128)(2,1)S(1)}, u32[]{:S(2)}, u32[]{:S(2)}) collective-permute-start(bf16[16,576]{1,0:T(8,128)(2,1)S(1)} %constant_dynamic-slice_fusion), channel_id=1, source_target_pairs={{0,64},{8,72},{16,80},{24,88},{32,96},{40,104},{48,112},{56,120},{... | collective-permute-start | bytes 55304 | tf_op jit(solution)/shard_map/ppermute | solution.py:179
  24.9 0.9 collective-permute-done
  25.8 12.3 %collective-permute-start.1 = (bf16[32,576]{1,0:T(8,128)(2,1)S(1)}, bf16[32,576]{1,0:T(8,128)(2,1)S(1)}, u32[]{:S(2)}, u32[]{:S(2)}) collective-permute-start(bf16[32,576]{1,0:T(8,128)(2,1)S(1)} %pad_maximum_fusion.4), channel_id=1, source_target_pairs={{0,32},{8,40},{16,48},{24,56},{32,64},{40,72},{48,80},{56,88},{64,... | collective-permute-start | bytes 110600 | tf_op jit(solution)/shard_map/ppermute | solution.py:179
  38.1 1.4 copy.19.refs_1_
  39.5 2.0 %pick.1 = bf16[128,576]{1,0:T(8,128)(2,1)} custom-call(s32[1]{0:T(128)} %bitcast.10.refs_0_, s32[128,1]{1,0:T(8,128)} %copy.19.refs_1_, bf16[128,576]{1,0:T(8,128)(2,1)} %copy-done), custom_call_target="tpu_custom_call" | custom-call | tf_op jit(solution)/shard_map/pick/pallas_call | solution.py:166
  41.4 1.6 %reshape.22 = bf16[32,4,576]{2,1,0:T(4,128)(2,1)} reshape(bf16[128,576]{1,0:T(8,128)(2,1)} %pick.1) | data formatting | bytes 294912 | tf_op jit(solution)/shard_map/reshape | solution.py:171
  43.1 31.4 %all-to-all-start = ((bf16[32,4,576]{2,1,0:T(4,128)(2,1)}), bf16[32,4,576]{2,1,0:T(4,128)(2,1)S(1)}, u32[]{:S(2)}, u32[]{:S(2)}) async-start(bf16[32,4,576]{2,1,0:T(4,128)(2,1)} %reshape.22), calls=%async_computation | async-start | bytes 327680 | tf_op jit(solution)/shard_map/all_to_all | solution.py:172
  74.5 3.6 %collective-permute-start.2 = (bf16[64,576]{1,0:T(8,128)(2,1)S(1)}, bf16[64,576]{1,0:T(8,128)(2,1)S(1)}, u32[]{:S(2)}, u32[]{:S(2)}) collective-permute-start(bf16[64,576]{1,0:T(8,128)(2,1)S(1)} %pad_maximum_fusion.1), channel_id=1, source_target_pairs={{0,16},{8,24},{16,32},{24,40},{32,48},{40,56},{48,64},{56,72},{64,... | collective-permute-start | bytes 221192 | tf_op jit(solution)/shard_map/ppermute | solution.py:179
  78.1 7.4 %collective-permute-done.2 = bf16[64,576]{1,0:T(8,128)(2,1)S(1)} collective-permute-done((bf16[64,576]{1,0:T(8,128)(2,1)S(1)}, bf16[64,576]{1,0:T(8,128)(2,1)S(1)}, u32[]{:S(2)}, u32[]{:S(2)}) %collective-permute-start.2) | collective-permute-done | bytes 73760 | tf_op jit(solution)/shard_map/ppermute | solution.py:179
  85.5 3.3 %collective-permute-start.3 = (bf16[112,576]{1,0:T(8,128)(2,1)S(1)}, bf16[112,576]{1,0:T(8,128)(2,1)S(1)}, u32[]{:S(2)}, u32[]{:S(2)}) collective-permute-start(bf16[112,576]{1,0:T(8,128)(2,1)S(1)} %get-tuple-element.16), channel_id=1, source_target_pairs={{0,2},{2,4},{4,6},{6,0},{1,3},{3,5},{5,7},{7,1},{8,10},{10,12},{12... | collective-permute-start | bytes 387080 | tf_op jit(solution)/shard_map/ppermute | solution.py:193
  88.9 7.1 %collective-permute-start.7 = (bf16[128,576]{1,0:T(8,128)(2,1)S(1)}, bf16[128,576]{1,0:T(8,128)(2,1)S(1)}, u32[]{:S(2)}, u32[]{:S(2)}) collective-permute-start(bf16[128,576]{1,0:T(8,128)(2,1)S(1)} %pad_maximum_fusion), channel_id=1, source_target_pairs={{0,8},{8,16},{16,24},{24,32},{32,40},{40,48},{48,56},{56,64},{64,7... | collective-permute-start | bytes 442376 | tf_op jit(solution)/shard_map/ppermute | solution.py:179
  96.0 4.7 %collective-permute-start.4 = (bf16[112,576]{1,0:T(8,128)(2,1)S(1)}, bf16[112,576]{1,0:T(8,128)(2,1)S(1)}, u32[]{:S(2)}, u32[]{:S(2)}) collective-permute-start(bf16[112,576]{1,0:T(8,128)(2,1)S(1)} %get-tuple-element.16), channel_id=1, source_target_pairs={{0,4},{2,6},{4,0},{6,2},{1,5},{3,7},{5,1},{7,3},{8,12},{10,14},{12... | collective-permute-start | bytes 387080 | tf_op jit(solution)/shard_map/ppermute | solution.py:193
  100.7 3.0 %collective-permute-start.5 = (bf16[112,576]{1,0:T(8,128)(2,1)S(1)}, bf16[112,576]{1,0:T(8,128)(2,1)S(1)}, u32[]{:S(2)}, u32[]{:S(2)}) collective-permute-start(bf16[112,576]{1,0:T(8,128)(2,1)S(1)} %get-tuple-element.16), channel_id=1, source_target_pairs={{0,6},{2,0},{4,2},{6,4},{1,7},{3,1},{5,3},{7,5},{8,14},{10,8},{12,... | collective-permute-start | bytes 387080 | tf_op jit(solution)/shard_map/ppermute | solution.py:193
  103.7 5.6 %collective-permute-start.8 = (bf16[16,576]{1,0:T(8,128)(2,1)S(1)}, bf16[16,576]{1,0:T(8,128)(2,1)S(1)}, u32[]{:S(2)}, u32[]{:S(2)}) collective-permute-start(bf16[16,576]{1,0:T(8,128)(2,1)S(1)} %slice.4), channel_id=1, source_target_pairs={{0,16},{8,24},{16,32},{24,40},{32,48},{40,56},{48,64},{56,72},{64,... | collective-permute-start | bytes 55304 | tf_op jit(solution)/shard_map/ppermute | solution.py:179
  110.2 2.4 %collective-permute-start.9 = (bf16[144,576]{1,0:T(8,128)(2,1)S(1)}, bf16[144,576]{1,0:T(8,128)(2,1)S(1)}, u32[]{:S(2)}, u32[]{:S(2)}) collective-permute-start(bf16[144,576]{1,0:T(8,128)(2,1)S(1)} %get-tuple-element.18), channel_id=1, source_target_pairs={{0,2},{2,4},{4,6},{6,0},{1,3},{3,5},{5,7},{7,1},{8,10},{10,12},{12... | collective-permute-start | bytes 497672 | tf_op jit(solution)/shard_map/ppermute | solution.py:193
  112.6 2.7 %collective-permute-start.10 = (bf16[144,576]{1,0:T(8,128)(2,1)S(1)}, bf16[144,576]{1,0:T(8,128)(2,1)S(1)}, u32[]{:S(2)}, u32[]{:S(2)}) collective-permute-start(bf16[144,576]{1,0:T(8,128)(2,1)S(1)} %get-tuple-element.18), channel_id=1, source_target_pairs={{0,4},{2,6},{4,0},{6,2},{1,5},{3,7},{5,1},{7,3},{8,12},{10,14},{12... | collective-permute-start | bytes 497672 | tf_op jit(solution)/shard_map/ppermute | solution.py:193
  115.3 5.7 %collective-permute-start.6 = (bf16[448,576]{1,0:T(8,128)(2,1)S(1)}, bf16[448,576]{1,0:T(8,128)(2,1)S(1)}, u32[]{:S(2)}, u32[]{:S(2)}) collective-permute-start(bf16[448,576]{1,0:T(8,128)(2,1)S(1)} %constant_dynamic-update-slice_fusion.3.refs_4_), channel_id=1, source_target_pairs={{0,1},{1,0},{2,3},{3,2},{4,5},{5,4},{6,7},{7,6},{8,9},{9,8},{10,11... | collective-permute-start | bytes 1548296 | tf_op jit(solution)/shard_map/ppermute | solution.py:194
  121.0 3.6 %collective-permute-start.11 = (bf16[144,576]{1,0:T(8,128)(2,1)S(1)}, bf16[144,576]{1,0:T(8,128)(2,1)S(1)}, u32[]{:S(2)}, u32[]{:S(2)}) collective-permute-start(bf16[144,576]{1,0:T(8,128)(2,1)S(1)} %get-tuple-element.18), channel_id=1, source_target_pairs={{0,6},{2,0},{4,2},{6,4},{1,7},{3,1},{5,3},{7,5},{8,14},{10,8},{12,... | collective-permute-start | bytes 497672 | tf_op jit(solution)/shard_map/ppermute | solution.py:193
  124.7 5.6 %collective-permute-done.11 = bf16[144,576]{1,0:T(8,128)(2,1)S(1)} collective-permute-done((bf16[144,576]{1,0:T(8,128)(2,1)S(1)}, bf16[144,576]{1,0:T(8,128)(2,1)S(1)}, u32[]{:S(2)}, u32[]{:S(2)}) %collective-permute-start.11) | collective-permute-done | bytes 165920 | tf_op jit(solution)/shard_map/ppermute | solution.py:193
  130.3 2.7 %collective-permute-start.12 = (bf16[576,576]{1,0:T(8,128)(2,1)S(1)}, bf16[576,576]{1,0:T(8,128)(2,1)S(1)}, u32[]{:S(2)}, u32[]{:S(2)}) collective-permute-start(bf16[576,576]{1,0:T(8,128)(2,1)S(1)} %constant_dynamic-update-slice_fusion.11.refs_6_), channel_id=1, source_target_pairs={{0,1},{1,0},{2,3},{3,2},{4,5},{5,4},{6,7},{7,6},{8,9},{9,8},{10,11... | collective-permute-start | bytes 1990664 | tf_op jit(solution)/shard_map/ppermute | solution.py:194
  134.2 3.4 %query.1 = (bf16[8,128,576]{2,1,0:T(8,128)(2,1)}, s32[128,128]{1,0:T(8,128)}) custom-call(s32[1]{0:T(128)} %bitcast.ctx_ref, bf16[128,1536]{1,0:T(8,128)(2,1)} %q_ref.1, bf16[8,128,512]{2,1,0:T(8,128)(2,1)} %ak_ref.1, f32[128,64]{1,0:T(8,128)} %get-tuple-element.25.cos_ref, f32[128,64]{1,0:T(8,128)} %get-tuple-element.26.sin_ref, s32[32,128]{1,0:T(8,128)} %bitcast.13), custom_call_target="tpu_custom_call" | custom-call | tf_op jit(solution)/shard_map/query/pallas_call | solution.py:208
  139.1 6.9 %first.1 = (f32[8,128,128]{2,1,0:T(8,128)}, f32[8,128,128]{2,1,0:T(8,128)}, f32[8,128,512]{2,1,0:T(8,128)}) custom-call(s32[9]{0:T(128)} %stack.39.refs_0_, bf16[8,128,576]{2,1,0:T(8,128)(2,1)} %get-tuple-element.7.refs_1_, s32[128,128]{1,0:T(8,128)} %get-tuple-element.8.refs_2_, bf16[128,576]{1,0:T(8,128)(2,1)} %copy-done, bf16[448,576]{1,0:T(8,128)(2,1)} %copy-done.2, ...), custom_call_target="tpu_custom_call" | custom-call | flops 5000000000 | bytes 6000000 | tf_op jit(solution)/shard_map/first/pallas_call | solution.py:221
  146.9 9.7 %second.1 = bf16[128,1024]{1,0:T(8,128)(2,1)} custom-call(s32[9]{0:T(128)} %stack.39.refs_0_, bf16[8,128,576]{2,1,0:T(8,128)(2,1)} %get-tuple-element.7.refs_1_, s32[128,128]{1,0:T(8,128)} %get-tuple-element.8.refs_2_, f32[8,128,128]{2,1,0:T(8,128)} %get-tuple-element.9.refs_3_, f32[8,128,128]{2,1,0:T(8,128)} %get-tuple-element.10.refs_4_, ...), custom_call_target="tpu_custom_call" | custom-call | flops 5000000000 | bytes 6000000 | tf_op jit(solution)/shard_map/second/pallas_call | solution.py:232
  (43 shorter events, 5.2 us)
Async XLA Ops:
  1.7 37.8 %copy-start = (bf16[128,576]{1,0:T(8,128)(2,1)}, bf16[128,576]{1,0:T(8,128)(2,1)S(1)}, u32[]{:S(2)}) copy-start(bf16[128,576]{1,0:T(8,128)(2,1)S(1)} %copy.18.refs_3_.refs_2_) | copy-start | bytes 442372
  1.7 24.1 %collective-permute-start = (bf16[16,576]{1,0:T(8,128)(2,1)S(1)}, bf16[16,576]{1,0:T(8,128)(2,1)S(1)}, u32[]{:S(2)}, u32[]{:S(2)}) collective-permute-start(bf16[16,576]{1,0:T(8,128)(2,1)S(1)} %constant_dynamic-slice_fusion), channel_id=1, source_target_pairs={{0,64},{8,72},{16,80},{24,88},{32,96},{40,104},{48,112},{56,120},{... | collective-permute-start | bytes 55304 | tf_op jit(solution)/shard_map/ppermute | solution.py:179
  25.8 48.6 %collective-permute-start.1 = (bf16[32,576]{1,0:T(8,128)(2,1)S(1)}, bf16[32,576]{1,0:T(8,128)(2,1)S(1)}, u32[]{:S(2)}, u32[]{:S(2)}) collective-permute-start(bf16[32,576]{1,0:T(8,128)(2,1)S(1)} %pad_maximum_fusion.4), channel_id=1, source_target_pairs={{0,32},{8,40},{16,48},{24,56},{32,64},{40,72},{48,80},{56,88},{64,... | collective-permute-start | bytes 110600 | tf_op jit(solution)/shard_map/ppermute | solution.py:179
  43.1 113.6 %all-to-all-start = ((bf16[32,4,576]{2,1,0:T(4,128)(2,1)}), bf16[32,4,576]{2,1,0:T(4,128)(2,1)S(1)}, u32[]{:S(2)}, u32[]{:S(2)}) async-start(bf16[32,4,576]{2,1,0:T(4,128)(2,1)} %reshape.22), calls=%async_computation | async-start | bytes 327680 | tf_op jit(solution)/shard_map/all_to_all | solution.py:172
  74.5 11.0 %collective-permute-start.2 = (bf16[64,576]{1,0:T(8,128)(2,1)S(1)}, bf16[64,576]{1,0:T(8,128)(2,1)S(1)}, u32[]{:S(2)}, u32[]{:S(2)}) collective-permute-start(bf16[64,576]{1,0:T(8,128)(2,1)S(1)} %pad_maximum_fusion.1), channel_id=1, source_target_pairs={{0,16},{8,24},{16,32},{24,40},{32,48},{40,56},{48,64},{56,72},{64,... | collective-permute-start | bytes 221192 | tf_op jit(solution)/shard_map/ppermute | solution.py:179
  85.5 23.7 %collective-permute-start.3 = (bf16[112,576]{1,0:T(8,128)(2,1)S(1)}, bf16[112,576]{1,0:T(8,128)(2,1)S(1)}, u32[]{:S(2)}, u32[]{:S(2)}) collective-permute-start(bf16[112,576]{1,0:T(8,128)(2,1)S(1)} %get-tuple-element.16), channel_id=1, source_target_pairs={{0,2},{2,4},{4,6},{6,0},{1,3},{3,5},{5,7},{7,1},{8,10},{10,12},{12... | collective-permute-start | bytes 387080 | tf_op jit(solution)/shard_map/ppermute | solution.py:193
  88.9 20.5 %collective-permute-start.7 = (bf16[128,576]{1,0:T(8,128)(2,1)S(1)}, bf16[128,576]{1,0:T(8,128)(2,1)S(1)}, u32[]{:S(2)}, u32[]{:S(2)}) collective-permute-start(bf16[128,576]{1,0:T(8,128)(2,1)S(1)} %pad_maximum_fusion), channel_id=1, source_target_pairs={{0,8},{8,16},{16,24},{24,32},{32,40},{40,48},{48,56},{56,64},{64,7... | collective-permute-start | bytes 442376 | tf_op jit(solution)/shard_map/ppermute | solution.py:179
  96.0 16.5 %collective-permute-start.4 = (bf16[112,576]{1,0:T(8,128)(2,1)S(1)}, bf16[112,576]{1,0:T(8,128)(2,1)S(1)}, u32[]{:S(2)}, u32[]{:S(2)}) collective-permute-start(bf16[112,576]{1,0:T(8,128)(2,1)S(1)} %get-tuple-element.16), channel_id=1, source_target_pairs={{0,4},{2,6},{4,0},{6,2},{1,5},{3,7},{5,1},{7,3},{8,12},{10,14},{12... | collective-permute-start | bytes 387080 | tf_op jit(solution)/shard_map/ppermute | solution.py:193
  100.7 14.6 %collective-permute-start.5 = (bf16[112,576]{1,0:T(8,128)(2,1)S(1)}, bf16[112,576]{1,0:T(8,128)(2,1)S(1)}, u32[]{:S(2)}, u32[]{:S(2)}) collective-permute-start(bf16[112,576]{1,0:T(8,128)(2,1)S(1)} %get-tuple-element.16), channel_id=1, source_target_pairs={{0,6},{2,0},{4,2},{6,4},{1,7},{3,1},{5,3},{7,5},{8,14},{10,8},{12,... | collective-permute-start | bytes 387080 | tf_op jit(solution)/shard_map/ppermute | solution.py:193
  103.7 6.5 %collective-permute-start.8 = (bf16[16,576]{1,0:T(8,128)(2,1)S(1)}, bf16[16,576]{1,0:T(8,128)(2,1)S(1)}, u32[]{:S(2)}, u32[]{:S(2)}) collective-permute-start(bf16[16,576]{1,0:T(8,128)(2,1)S(1)} %slice.4), channel_id=1, source_target_pairs={{0,16},{8,24},{16,32},{24,40},{32,48},{40,56},{48,64},{56,72},{64,... | collective-permute-start | bytes 55304 | tf_op jit(solution)/shard_map/ppermute | solution.py:179
  110.2 14.4 %collective-permute-start.9 = (bf16[144,576]{1,0:T(8,128)(2,1)S(1)}, bf16[144,576]{1,0:T(8,128)(2,1)S(1)}, u32[]{:S(2)}, u32[]{:S(2)}) collective-permute-start(bf16[144,576]{1,0:T(8,128)(2,1)S(1)} %get-tuple-element.18), channel_id=1, source_target_pairs={{0,2},{2,4},{4,6},{6,0},{1,3},{3,5},{5,7},{7,1},{8,10},{10,12},{12... | collective-permute-start | bytes 497672 | tf_op jit(solution)/shard_map/ppermute | solution.py:193
  112.6 12.1 %collective-permute-start.10 = (bf16[144,576]{1,0:T(8,128)(2,1)S(1)}, bf16[144,576]{1,0:T(8,128)(2,1)S(1)}, u32[]{:S(2)}, u32[]{:S(2)}) collective-permute-start(bf16[144,576]{1,0:T(8,128)(2,1)S(1)} %get-tuple-element.18), channel_id=1, source_target_pairs={{0,4},{2,6},{4,0},{6,2},{1,5},{3,7},{5,1},{7,3},{8,12},{10,14},{12... | collective-permute-start | bytes 497672 | tf_op jit(solution)/shard_map/ppermute | solution.py:193
  115.3 22.9 %copy-start.2 = (bf16[448,576]{1,0:T(8,128)(2,1)}, bf16[448,576]{1,0:T(8,128)(2,1)S(1)}, u32[]{:S(2)}) copy-start(bf16[448,576]{1,0:T(8,128)(2,1)S(1)} %constant_dynamic-update-slice_fusion.3.refs_4_) | copy-start | bytes 1548292
  115.3 22.9 %collective-permute-start.6 = (bf16[448,576]{1,0:T(8,128)(2,1)S(1)}, bf16[448,576]{1,0:T(8,128)(2,1)S(1)}, u32[]{:S(2)}, u32[]{:S(2)}) collective-permute-start(bf16[448,576]{1,0:T(8,128)(2,1)S(1)} %constant_dynamic-update-slice_fusion.3.refs_4_), channel_id=1, source_target_pairs={{0,1},{1,0},{2,3},{3,2},{4,5},{5,4},{6,7},{7,6},{8,9},{9,8},{10,11... | collective-permute-start | bytes 1548296 | tf_op jit(solution)/shard_map/ppermute | solution.py:194
  121.0 9.3 %collective-permute-start.11 = (bf16[144,576]{1,0:T(8,128)(2,1)S(1)}, bf16[144,576]{1,0:T(8,128)(2,1)S(1)}, u32[]{:S(2)}, u32[]{:S(2)}) collective-permute-start(bf16[144,576]{1,0:T(8,128)(2,1)S(1)} %get-tuple-element.18), channel_id=1, source_target_pairs={{0,6},{2,0},{4,2},{6,4},{1,7},{3,1},{5,3},{7,5},{8,14},{10,8},{12,... | collective-permute-start | bytes 497672 | tf_op jit(solution)/shard_map/ppermute | solution.py:193
  130.3 15.7 %copy-start.1 = (bf16[576,576]{1,0:T(8,128)(2,1)}, bf16[576,576]{1,0:T(8,128)(2,1)S(1)}, u32[]{:S(2)}) copy-start(bf16[576,576]{1,0:T(8,128)(2,1)S(1)} %constant_dynamic-update-slice_fusion.11.refs_6_) | copy-start | bytes 1990660
  130.3 15.7 %collective-permute-start.12 = (bf16[576,576]{1,0:T(8,128)(2,1)S(1)}, bf16[576,576]{1,0:T(8,128)(2,1)S(1)}, u32[]{:S(2)}, u32[]{:S(2)}) collective-permute-start(bf16[576,576]{1,0:T(8,128)(2,1)S(1)} %constant_dynamic-update-slice_fusion.11.refs_6_), channel_id=1, source_target_pairs={{0,1},{1,0},{2,3},{3,2},{4,5},{5,4},{6,7},{7,6},{8,9},{9,8},{10,11... | collective-permute-start | bytes 1990664 | tf_op jit(solution)/shard_map/ppermute | solution.py:194
  138.2 0.8 copy-start.4
  146.0 0.9 copy-start.3

commit v2 on v1

v2 whole, which is shorter than its diff:
```python
import jax
import jax.numpy as jnp
from jax import lax
from jax.experimental import pallas as pl
from jax.experimental.pallas import tpu as pltpu
from jax.experimental.layout import Layout, with_layout_constraint
from jax.sharding import PartitionSpec as P


NOPE = 128
ROPE = 64
LATENT = 512
VDIM = 128
WIDTH = LATENT + ROPE
HEAD_IN = NOPE + ROPE
NEG = -1e30
LOG2E = 1.4426950408889634
DISTANCES = (1, 9, 5, 13, 3, 11, 7, 15, 2, 10, 6, 14, 4, 12, 8, 16)


def query_kernel(ctx_ref, q_ref, ak_ref, cos_ref, sin_ref, seg_ref, fq_ref, start_ref):
    heads = ak_ref.shape[0]
    rows = q_ref.shape[0]
    cos2 = cos_ref[...]
    sin2 = sin_ref[...]
    half = ROPE // 2
    for h in range(heads):
        piece = q_ref[:, h * HEAD_IN:(h + 1) * HEAD_IN]
        absorbed = jnp.dot(piece[:, :NOPE], ak_ref[h], preferred_element_type=jnp.float32)
        fq_ref[h, :, :LATENT] = absorbed.astype(jnp.bfloat16)
        x = piece[:, NOPE:].astype(jnp.float32)
        swapped = jnp.concatenate([x[:, half:], x[:, :half]], axis=1)
        fq_ref[h, :, LATENT:] = (x * cos2 + swapped * sin2).astype(jnp.bfloat16)
    own = seg_ref[pl.ds(ctx_ref[0], 1), :]
    own = jnp.broadcast_to(own, (rows, rows)).T
    below = jnp.zeros((rows, rows), jnp.int32)
    for b in range(seg_ref.shape[0]):
        below = below + (seg_ref[b:b + 1, :] < own).astype(jnp.int32)
    start = jnp.sum(below, axis=1, keepdims=True)
    start_ref[...] = jnp.broadcast_to(start, (rows, rows))


def pick_kernel(core_ref, owner_ref, latent_ref, out_ref, *, cores, slots):
    rows = latent_ref.shape[0]
    own = jnp.broadcast_to(owner_ref[...], (rows, rows))
    across = own.T
    down_id = lax.broadcasted_iota(jnp.int32, (rows, rows), 0)
    across_id = lax.broadcasted_iota(jnp.int32, (rows, rows), 1)
    hit = ((own == across) & (down_id < across_id)).astype(jnp.int32)
    rank = jnp.sum(hit, axis=0, keepdims=True)
    name = across[:1, :]
    target = name // cores * slots + rank
    target = jnp.where(name % cores == core_ref[0], target, -1)
    slot_id = lax.broadcasted_iota(jnp.int32, (out_ref.shape[0], rows), 0)
    picker = (slot_id == target).astype(jnp.float32).astype(jnp.bfloat16)
    out_ref[...] = jnp.dot(
        picker, latent_ref[...], preferred_element_type=jnp.float32
    ).astype(jnp.bfloat16)


def attend_kernel(meta_ref, fq_ref, start_ref, latent_ref, near_ref, far_ref, av_ref,
                  out_ref, keys_ref, bias_ref, sems, *, scale, group):
    heads, rows = fq_ref.shape[0], fq_ref.shape[1]
    count = len(DISTANCES)
    quarters = near_ref.shape[0]
    copies = [pltpu.make_async_copy(latent_ref, keys_ref.at[count], sems.at[2 * quarters])]
    for i in range(quarters):
        copies.append(pltpu.make_async_copy(
            near_ref.at[i], keys_ref.at[pl.ds(0, count), meta_ref[1 + i]], sems.at[i]))
        copies.append(pltpu.make_async_copy(
            far_ref.at[i], keys_ref.at[pl.ds(0, count), meta_ref[1 + quarters + i]],
            sems.at[quarters + i]))
    for copy in copies:
        copy.start()
    start = start_ref[...]
    ctx = meta_ref[0]
    lane = lax.broadcasted_iota(jnp.int32, (rows, rows), 1)
    down = lax.broadcasted_iota(jnp.int32, (rows, rows), 0)
    for b, dist in enumerate(DISTANCES):
        seen = (ctx - dist) * rows + lane >= start
        bias_ref[:, b * rows:(b + 1) * rows] = jnp.where(seen, 0.0, NEG)
    seen = (ctx * rows + lane >= start) & (lane <= down)
    bias_ref[:, count * rows:] = jnp.where(seen, 0.0, NEG)
    for copy in copies:
        copy.wait()
    factor = scale * LOG2E
    total_keys = (count + 1) * rows
    for h in range(0, heads, group):
        q = fq_ref[h:h + group].reshape(group * rows, WIDTH)
        keys = keys_ref[...].reshape(total_keys, WIDTH)
        s = lax.dot_general(
            q, keys, (((1,), (1,)), ((), ())), preferred_element_type=jnp.float32
        )
        s = s.reshape(group, rows, total_keys) + bias_ref[...][None]
        top = jnp.max(s, axis=2, keepdims=True)
        p = jnp.exp2((s - top) * factor)
        total = jnp.sum(p, axis=2, keepdims=True)
        mixed = jnp.dot(
            p.astype(jnp.bfloat16).reshape(group * rows, total_keys), keys[:, :LATENT],
            preferred_element_type=jnp.float32,
        ).reshape(group, rows, LATENT)
        mixed = (mixed / total).astype(jnp.bfloat16)
        for g in range(group):
            out_ref[:, (h + g) * VDIM:(h + g + 1) * VDIM] = jnp.dot(
                mixed[g], av_ref[h + g], preferred_element_type=jnp.float32
            ).astype(jnp.bfloat16)


def vmem(n):
    return [pl.BlockSpec(memory_space=pltpu.VMEM) for _ in range(n)]


SMEM = pl.BlockSpec(memory_space=pltpu.SMEM)


def program(queries, latent_rows, segments, owners, absorb_key, absorb_value):
    rows = queries.shape[0]
    heads = absorb_key.shape[0]
    ctx_count = lax.axis_size("ctx")
    head_count = lax.axis_size("head")
    dec_count = lax.axis_size("dec")
    ctx = lax.axis_index("ctx")
    head = lax.axis_index("head")
    core = lax.axis_index("dec")
    scale = (NOPE + ROPE) ** (-0.5)
    bf16 = jnp.bfloat16

    half = ROPE // 2
    frequency = 10000.0 ** (-jnp.arange(half, dtype=jnp.float32) * 2.0 / ROPE)
    query_pos = ctx * rows + jnp.arange(rows, dtype=jnp.int32)
    angles = query_pos.astype(jnp.float32)[:, None] * frequency[None, :]
    cosine = jnp.cos(angles)
    sine = jnp.sin(angles)
    cos2 = jnp.concatenate([cosine, cosine], axis=1)
    sin2 = jnp.concatenate([-sine, sine], axis=1)
    full_query, start = pl.pallas_call(
        query_kernel,
        out_shape=(jax.ShapeDtypeStruct((heads, rows, WIDTH), bf16),
                   jax.ShapeDtypeStruct((rows, rows), jnp.int32)),
        in_specs=[SMEM] + vmem(5), out_specs=tuple(vmem(2)), name="query",
    )(ctx[None], queries, absorb_key, cos2, sin2, segments.reshape(-1, rows))
    from_head = [(head - k) % head_count for k in range(head_count)]
    meta = jnp.stack(
        [ctx] + [f * dec_count + core for f in from_head]
        + [f * dec_count + (1 - core) for f in from_head]
    )

    slots = max(2, 2 * rows // (ctx_count * dec_count))
    outgoing = pl.pallas_call(
        lambda *refs: pick_kernel(*refs, cores=dec_count, slots=slots),
        out_shape=jax.ShapeDtypeStruct((ctx_count * slots, WIDTH), bf16),
        in_specs=[SMEM] + vmem(2), out_specs=vmem(1)[0], name="pick",
    )(core[None], owners, latent_rows)
    outgoing = outgoing.reshape(ctx_count, slots, WIDTH)

    replica = head * dec_count + core
    share = rows // (head_count * dec_count)
    own = lax.dynamic_slice_in_dim(latent_rows, replica * share, share, 0)

    def shift(x, k):
        return lax.ppermute(x, "ctx", [(i, i + k) for i in range(ctx_count - k)])

    def row_major(x):
        return with_layout_constraint(x, Layout((0, 1)))

    def cat(*xs):
        return row_major(jnp.concatenate(xs, axis=0))

    two = cat(shift(own, 1), shift(own, 9))
    two, full_query, start, outgoing, meta = lax.optimization_barrier(
        (two, full_query, start, outgoing, meta))
    four = cat(two, shift(two, 4))
    eight = cat(four, shift(four, 2))
    eight, outgoing = lax.optimization_barrier((eight, outgoing))
    arrived = lax.all_to_all(outgoing, "ctx", split_axis=0, concat_axis=0, tiled=True)
    late = shift(eight, 1)
    window = cat(eight, late)

    ring = lambda k: [(i, (i + k) % head_count) for i in range(head_count)]
    others = [lax.ppermute(window, "head", ring(k)) for k in range(1, head_count)]
    near = cat(window, *others)
    far = row_major(lax.ppermute(near, "dec", [(i, (i + 1) % dec_count) for i in range(dec_count)]))

    blocks = len(DISTANCES)
    parts = head_count * dec_count
    by_share = lambda x: x.reshape(head_count, blocks, share, WIDTH)
    any_spec = pl.BlockSpec(memory_space=pl.ANY)
    answer = pl.pallas_call(
        lambda *refs: attend_kernel(*refs, scale=scale, group=2),
        out_shape=jax.ShapeDtypeStruct((rows, heads * VDIM), bf16),
        in_specs=[SMEM] + vmem(2) + [any_spec] * 3 + vmem(1), out_specs=vmem(1)[0],
        scratch_shapes=[pltpu.VMEM((blocks + 1, parts, share, WIDTH), bf16),
                        pltpu.VMEM((rows, (blocks + 1) * rows), jnp.float32),
                        pltpu.SemaphoreType.DMA((parts + 1,))],
        name="attend",
        cost_estimate=pl.CostEstimate(
            flops=10_000_000_000, bytes_accessed=6_000_000, transcendentals=2_000_000),
    )(meta, full_query, start, latent_rows.reshape(parts, share, WIDTH), by_share(near),
      by_share(far), absorb_value)
    return (answer, arrived[None])


def solution(mesh):
    in_specs = (
        P(("group", "ctx"), ("head", "dec")),
        P(("group", "ctx"), None),
        P("group"),
        P(("group", "ctx"), None),
        P(("head", "dec"), None, None),
        P(("head", "dec"), None, None),
    )
    out_specs = (P(("group", "ctx"), ("head", "dec")), P(("group", "ctx", "dec"), None, None, None))
    return jax.shard_map(
        program, mesh=mesh, in_specs=in_specs, out_specs=out_specs, check_vma=False
    )
```

time: 158 us -> 179 us (1.13)
  blocking collectives: 0 us -> 64.7 us
  starting transfers between devices: 111 us -> 67.9 us
  Pallas kernels: 22 us -> 18.5 us
  waiting for transfers between devices: 14.7 us -> 18 us
    all_to_all x0 -> x1, blocking collectives: none -> 64.7 us  [program(): lax.all_to_all(outgoing, 'ctx', split_axis=0, concat_axis=0, tiled=True)]
    all_to_all x1 -> x0, starting transfers between devices: 31.4 us -> none  [on_device(): lax.all_to_all(outgoing, 'ctx', split_axis=0, concat_axis=0, tiled=True)]
    ppermute x8 -> x4, starting transfers between devices: 27.9 us -> 14.1 us  [the longest x3 9.69 us: program(): lax.ppermute(window, 'head', ring(k))]
    ppermute x8 -> x4, waiting for transfers between devices: 5.61 us -> 13.2 us  [the longest x3 13.2 us: program(): lax.ppermute(window, 'head', ring(k))]
    ppermute x5, waiting for transfers between devices: 9.09 us -> 4.75 us  [shift(): return lax.ppermute(x, 'ctx', [(i, i + k) for i in range(ctx_count - k)])]
    pallas_call x4 -> x3, Pallas kernels: 22 us -> 18.5 us  [the longest x1 13.1 us: program(): pl.pallas_call(lambda *refs: attend_kernel(*refs, scale=scale, group=2),...]
    ppermute x5, starting transfers between devices: 51.8 us -> 53.8 us  [shift(): return lax.ppermute(x, 'ctx', [(i, i + k) for i in range(ctx_count - k)])]
    unnamed x20 -> x9, local copies, waits for them, and re-layouts: 4.97 us -> 3.14 us
  transfers between devices with their start and end apart: 14 -> 9, of which waited for: 4 -> 5; matrix products, arithmetic and copies ran while one was open for 3% -> 2% of each run, Pallas kernels for 14% -> 3%
where the time goes in v2:
time: 179 us
  starting transfers between devices  67.9 us (38%)
  blocking collectives  64.7 us (36%)
  Pallas kernels  18.5 us (10%)
  waiting for transfers between devices  18 us (10%)
  local copies, waits for them, and re-layouts  7.71 us (4%)
    all_to_all x1, blocking collectives, program(): lax.all_to_all(outgoing, 'ctx', split_axis=0, concat_axis=0, tiled=True)  64.7 us
    ppermute x5, starting transfers between devices, shift(): return lax.ppermute(x, 'ctx', [(i, i + k) for i in range(ctx_count - k)])  53.8 us
    ppermute x3, waiting for transfers between devices, program(): lax.ppermute(window, 'head', ring(k))  13.2 us
    pallas_call x1, Pallas kernels, program(): pl.pallas_call(lambda *refs: attend_kernel(*refs, scale=scale, group=2),...  13.1 us
    ppermute x3, starting transfers between devices, program(): lax.ppermute(window, 'head', ring(k))  9.69 us
    ppermute x5, waiting for transfers between devices, shift(): return lax.ppermute(x, 'ctx', [(i, i + k) for i in range(ctx_count - k)])  4.75 us
    ppermute x1, starting transfers between devices, program(): lax.ppermute(near, 'dec', [(i, (i + 1) % dec_count) for i in range(dec_co...  4.37 us
  transfers between devices with their start and end apart: 9, of which 5 were waited for; matrix products, arithmetic and copies ran while one was open for 2% of the time, Pallas kernels for 3%

profile of v2, /device:TPU:33, one launch (start us, length us, event | category | flops | bytes accessed | tf_op | source)
XLA Modules:
  0.0 178.8 jit_solution(7580179215374379735)
XLA Ops:
  0.6 1.1 copy.22.refs_2_
  1.7 25.4 %collective-permute-start.1 = (bf16[16,576]{1,0:T(8,128)(2,1)S(1)}, bf16[16,576]{1,0:T(8,128)(2,1)S(1)}, u32[]{:S(2)}, u32[]{:S(2)}) collective-permute-start(bf16[16,576]{1,0:T(8,128)(2,1)S(1)} %constant_dynamic-slice_fusion), channel_id=1, source_target_pairs={{0,72},{8,80},{16,88},{24,96},{32,104},{40,112},{48,120},{56,128},... | collective-permute-start | bytes 55304 | tf_op jit(solution)/shard_map/ppermute | solution.py:161
  27.1 4.4 %collective-permute-start = (bf16[16,576]{1,0:T(8,128)(2,1)S(1)}, bf16[16,576]{1,0:T(8,128)(2,1)S(1)}, u32[]{:S(2)}, u32[]{:S(2)}) collective-permute-start(bf16[16,576]{1,0:T(8,128)(2,1)S(1)} %constant_dynamic-slice_fusion), channel_id=1, source_target_pairs={{0,8},{8,16},{16,24},{24,32},{32,40},{40,48},{48,56},{56,64},{64,7... | collective-permute-start | bytes 55304 | tf_op jit(solution)/shard_map/ppermute | solution.py:161
  31.9 0.7 pad_maximum_fusion.2
  32.6 1.4 copy.24.refs_1_
  34.0 2.0 %pick.1 = bf16[128,576]{1,0:T(8,128)(2,1)} custom-call(s32[1]{0:T(128)} %bitcast.2.refs_0_, s32[128,1]{1,0:T(8,128)} %copy.24.refs_1_, bf16[128,576]{1,0:T(8,128)(2,1)} %copy-done.1), custom_call_target="tpu_custom_call" | custom-call | tf_op jit(solution)/shard_map/pick/pallas_call | solution.py:149
  36.0 1.0 reshape.31
  37.0 3.4 %query.1 = (bf16[8,128,576]{2,1,0:T(8,128)(2,1)}, s32[128,128]{1,0:T(8,128)}) custom-call(s32[1]{0:T(128)} %bitcast.ctx_ref, bf16[128,1536]{1,0:T(8,128)(2,1)} %q_ref.1, bf16[8,128,512]{2,1,0:T(8,128)(2,1)} %ak_ref.1, f32[128,64]{1,0:T(8,128)} %get-tuple-element.23.cos_ref, f32[128,64]{1,0:T(8,128)} %get-tuple-element.24.sin_ref, s32[32,128]{1,0:T(8,128)} %bitcast.19), custom_call_target="tpu_custom_call" | custom-call | tf_op jit(solution)/shard_map/query/pallas_call | solution.py:136
  41.1 12.3 %collective-permute-start.2 = (bf16[32,576]{1,0:T(8,128)(2,1)S(1)}, bf16[32,576]{1,0:T(8,128)(2,1)S(1)}, u32[]{:S(2)}, u32[]{:S(2)}) collective-permute-start(bf16[32,576]{1,0:T(8,128)(2,1)S(1)} %pad_maximum_fusion.4), channel_id=1, source_target_pairs={{0,32},{8,40},{16,48},{24,56},{32,64},{40,72},{48,80},{56,88},{64,... | collective-permute-start | bytes 110600 | tf_op jit(solution)/shard_map/ppermute | solution.py:161
  53.4 1.1 collective-permute-done.2
  54.4 7.8 %collective-permute-start.3 = (bf16[64,576]{1,0:T(8,128)(2,1)S(1)}, bf16[64,576]{1,0:T(8,128)(2,1)S(1)}, u32[]{:S(2)}, u32[]{:S(2)}) collective-permute-start(bf16[64,576]{1,0:T(8,128)(2,1)S(1)} %constant_dynamic-update-slice_fusion), channel_id=1, source_target_pairs={{0,16},{8,24},{16,32},{24,40},{32,48},{40,56},{48,64},{56,72},{64,... | collective-permute-start | bytes 221192 | tf_op jit(solution)/shard_map/ppermute | solution.py:161
  62.3 1.5 collective-permute-done.3
  63.8 3.9 %collective-permute-start.4 = (bf16[128,576]{1,0:T(8,128)(2,1)S(1)}, bf16[128,576]{1,0:T(8,128)(2,1)S(1)}, u32[]{:S(2)}, u32[]{:S(2)}) collective-permute-start(bf16[128,576]{1,0:T(8,128)(2,1)S(1)} %pad_maximum_fusion.1), channel_id=1, source_target_pairs={{0,8},{8,16},{16,24},{24,32},{32,40},{40,48},{48,56},{56,64},{64,7... | collective-permute-start | bytes 442376 | tf_op jit(solution)/shard_map/ppermute | solution.py:161
  67.7 2.2 %collective-permute-done.4 = bf16[128,576]{1,0:T(8,128)(2,1)S(1)} collective-permute-done((bf16[128,576]{1,0:T(8,128)(2,1)S(1)}, bf16[128,576]{1,0:T(8,128)(2,1)S(1)}, u32[]{:S(2)}, u32[]{:S(2)}) %collective-permute-start.4) | collective-permute-done | bytes 147488 | tf_op jit(solution)/shard_map/ppermute | solution.py:161
  69.9 4.8 %collective-permute-start.7 = (bf16[256,576]{1,0:T(8,128)(2,1)S(1)}, bf16[256,576]{1,0:T(8,128)(2,1)S(1)}, u32[]{:S(2)}, u32[]{:S(2)}) collective-permute-start(bf16[256,576]{1,0:T(8,128)(2,1)S(1)} %constant_dynamic-update-slice_fusion.2), channel_id=1, source_target_pairs={{0,6},{2,0},{4,2},{6,4},{1,7},{3,1},{5,3},{7,5},{8,14},{10,8},{12,... | collective-permute-start | bytes 884744 | tf_op jit(solution)/shard_map/ppermute | solution.py:180
  74.8 2.2 %collective-permute-start.6 = (bf16[256,576]{1,0:T(8,128)(2,1)S(1)}, bf16[256,576]{1,0:T(8,128)(2,1)S(1)}, u32[]{:S(2)}, u32[]{:S(2)}) collective-permute-start(bf16[256,576]{1,0:T(8,128)(2,1)S(1)} %constant_dynamic-update-slice_fusion.2), channel_id=1, source_target_pairs={{0,4},{2,6},{4,0},{6,2},{1,5},{3,7},{5,1},{7,3},{8,12},{10,14},{12... | collective-permute-start | bytes 884744 | tf_op jit(solution)/shard_map/ppermute | solution.py:180
  77.0 2.7 %collective-permute-start.5 = (bf16[256,576]{1,0:T(8,128)(2,1)S(1)}, bf16[256,576]{1,0:T(8,128)(2,1)S(1)}, u32[]{:S(2)}, u32[]{:S(2)}) collective-permute-start(bf16[256,576]{1,0:T(8,128)(2,1)S(1)} %constant_dynamic-update-slice_fusion.2), channel_id=1, source_target_pairs={{0,2},{2,4},{4,6},{6,0},{1,3},{3,5},{5,7},{7,1},{8,10},{10,12},{12... | collective-permute-start | bytes 884744 | tf_op jit(solution)/shard_map/ppermute | solution.py:180
  79.7 4.6 %collective-permute-done.6 = bf16[256,576]{1,0:T(8,128)(2,1)S(1)} collective-permute-done((bf16[256,576]{1,0:T(8,128)(2,1)S(1)}, bf16[256,576]{1,0:T(8,128)(2,1)S(1)}, u32[]{:S(2)}, u32[]{:S(2)}) %collective-permute-start.6) | collective-permute-done | bytes 294944 | tf_op jit(solution)/shard_map/ppermute | solution.py:180
  84.2 8.7 %collective-permute-done.5 = bf16[256,576]{1,0:T(8,128)(2,1)S(1)} collective-permute-done((bf16[256,576]{1,0:T(8,128)(2,1)S(1)}, bf16[256,576]{1,0:T(8,128)(2,1)S(1)}, u32[]{:S(2)}, u32[]{:S(2)}) %collective-permute-start.5) | collective-permute-done | bytes 294944 | tf_op jit(solution)/shard_map/ppermute | solution.py:180
  93.0 1.4 copy.27
  94.5 4.4 %collective-permute-start.8 = (bf16[1024,576]{0,1:T(8,128)(2,1)}, bf16[1024,576]{0,1:T(8,128)(2,1)S(1)}, u32[]{:S(2)}, u32[]{:S(2)}) collective-permute-start(bf16[1024,576]{0,1:T(8,128)(2,1)} %copy.27), channel_id=1, source_target_pairs={{0,1},{1,0},{2,3},{3,2},{4,5},{5,4},{6,7},{7,6},{8,9},{9,8},{10,11... | collective-permute-start | bytes 3538952 | tf_op jit(solution)/shard_map/ppermute | solution.py:182
  98.9 64.7 %all_to_all.5 = bf16[32,4,576]{2,1,0:T(4,128)(2,1)S(1)} all-to-all(bf16[32,4,576]{2,1,0:T(4,128)(2,1)S(1)} %reshape.31), channel_id=1, replica_groups=mesh['group'=2,'ctx'=32,'head'=4,'dec'=2] {'ctx'}, dimensions={0} | all-to-all | bytes 294912 | tf_op jit(solution)/shard_map/all_to_all | solution.py:175
  163.6 1.4 copy.28
  165.0 13.1 %attend.1 = bf16[128,1024]{1,0:T(8,128)(2,1)} custom-call(s32[9]{0:T(128)} %stack.36.refs_0_, bf16[8,128,576]{2,1,0:T(8,128)(2,1)} %get-tuple-element.14.refs_1_, s32[128,128]{1,0:T(8,128)} %get-tuple-element.15.refs_2_, bf16[8,16,576]{2,1,0:T(8,128)(2,1)} %bitcast.17, bf16[4,16,16,576]{3,2,1,0:T(8,128)(2,1)} %bitcast.15, bf16[4,16,16,576]{3,2,1,0:T(8,128)(2,1)} %bitcast.16, ...), custom_call_target="tpu_custom_call" | custom-call | flops 10000000000 | bytes 6000000 | tf_op jit(solution)/shard_map/attend/pallas_call | solution.py:188
  (21 shorter events, 1.9 us)
Async XLA Ops:
  1.7 32.3 %copy-start.1 = (bf16[128,576]{1,0:T(8,128)(2,1)}, bf16[128,576]{1,0:T(8,128)(2,1)S(1)}, u32[]{:S(2)}) copy-start(bf16[128,576]{1,0:T(8,128)(2,1)S(1)} %copy.22.refs_2_) | copy-start | bytes 442372
  1.7 39.3 %collective-permute-start.1 = (bf16[16,576]{1,0:T(8,128)(2,1)S(1)}, bf16[16,576]{1,0:T(8,128)(2,1)S(1)}, u32[]{:S(2)}, u32[]{:S(2)}) collective-permute-start(bf16[16,576]{1,0:T(8,128)(2,1)S(1)} %constant_dynamic-slice_fusion), channel_id=1, source_target_pairs={{0,72},{8,80},{16,88},{24,96},{32,104},{40,112},{48,120},{56,128},... | collective-permute-start | bytes 55304 | tf_op jit(solution)/shard_map/ppermute | solution.py:161
  27.1 13.9 %collective-permute-start = (bf16[16,576]{1,0:T(8,128)(2,1)S(1)}, bf16[16,576]{1,0:T(8,128)(2,1)S(1)}, u32[]{:S(2)}, u32[]{:S(2)}) collective-permute-start(bf16[16,576]{1,0:T(8,128)(2,1)S(1)} %constant_dynamic-slice_fusion), channel_id=1, source_target_pairs={{0,8},{8,16},{16,24},{24,32},{32,40},{40,48},{48,56},{56,64},{64,7... | collective-permute-start | bytes 55304 | tf_op jit(solution)/shard_map/ppermute | solution.py:161
  41.1 13.4 %collective-permute-start.2 = (bf16[32,576]{1,0:T(8,128)(2,1)S(1)}, bf16[32,576]{1,0:T(8,128)(2,1)S(1)}, u32[]{:S(2)}, u32[]{:S(2)}) collective-permute-start(bf16[32,576]{1,0:T(8,128)(2,1)S(1)} %pad_maximum_fusion.4), channel_id=1, source_target_pairs={{0,32},{8,40},{16,48},{24,56},{32,64},{40,72},{48,80},{56,88},{64,... | collective-permute-start | bytes 110600 | tf_op jit(solution)/shard_map/ppermute | solution.py:161
  54.4 9.3 %collective-permute-start.3 = (bf16[64,576]{1,0:T(8,128)(2,1)S(1)}, bf16[64,576]{1,0:T(8,128)(2,1)S(1)}, u32[]{:S(2)}, u32[]{:S(2)}) collective-permute-start(bf16[64,576]{1,0:T(8,128)(2,1)S(1)} %constant_dynamic-update-slice_fusion), channel_id=1, source_target_pairs={{0,16},{8,24},{16,32},{24,40},{32,48},{40,56},{48,64},{56,72},{64,... | collective-permute-start | bytes 221192 | tf_op jit(solution)/shard_map/ppermute | solution.py:161
  63.8 6.1 %collective-permute-start.4 = (bf16[128,576]{1,0:T(8,128)(2,1)S(1)}, bf16[128,576]{1,0:T(8,128)(2,1)S(1)}, u32[]{:S(2)}, u32[]{:S(2)}) collective-permute-start(bf16[128,576]{1,0:T(8,128)(2,1)S(1)} %pad_maximum_fusion.1), channel_id=1, source_target_pairs={{0,8},{8,16},{16,24},{24,32},{32,40},{40,48},{48,56},{56,64},{64,7... | collective-permute-start | bytes 442376 | tf_op jit(solution)/shard_map/ppermute | solution.py:161
  69.9 9.7 %collective-permute-start.7 = (bf16[256,576]{1,0:T(8,128)(2,1)S(1)}, bf16[256,576]{1,0:T(8,128)(2,1)S(1)}, u32[]{:S(2)}, u32[]{:S(2)}) collective-permute-start(bf16[256,576]{1,0:T(8,128)(2,1)S(1)} %constant_dynamic-update-slice_fusion.2), channel_id=1, source_target_pairs={{0,6},{2,0},{4,2},{6,4},{1,7},{3,1},{5,3},{7,5},{8,14},{10,8},{12,... | collective-permute-start | bytes 884744 | tf_op jit(solution)/shard_map/ppermute | solution.py:180
  74.8 9.5 %collective-permute-start.6 = (bf16[256,576]{1,0:T(8,128)(2,1)S(1)}, bf16[256,576]{1,0:T(8,128)(2,1)S(1)}, u32[]{:S(2)}, u32[]{:S(2)}) collective-permute-start(bf16[256,576]{1,0:T(8,128)(2,1)S(1)} %constant_dynamic-update-slice_fusion.2), channel_id=1, source_target_pairs={{0,4},{2,6},{4,0},{6,2},{1,5},{3,7},{5,1},{7,3},{8,12},{10,14},{12... | collective-permute-start | bytes 884744 | tf_op jit(solution)/shard_map/ppermute | solution.py:180
  77.0 15.9 %collective-permute-start.5 = (bf16[256,576]{1,0:T(8,128)(2,1)S(1)}, bf16[256,576]{1,0:T(8,128)(2,1)S(1)}, u32[]{:S(2)}, u32[]{:S(2)}) collective-permute-start(bf16[256,576]{1,0:T(8,128)(2,1)S(1)} %constant_dynamic-update-slice_fusion.2), channel_id=1, source_target_pairs={{0,2},{2,4},{4,6},{6,0},{1,3},{3,5},{5,7},{7,1},{8,10},{10,12},{12... | collective-permute-start | bytes 884744 | tf_op jit(solution)/shard_map/ppermute | solution.py:180
  93.0 70.6 %copy-start = (bf16[1024,576]{1,0:T(8,128)(2,1)}, bf16[1024,576]{1,0:T(8,128)(2,1)S(1)}, u32[]{:S(2)}) copy-start(bf16[1024,576]{1,0:T(8,128)(2,1)S(1)} %pad_maximum_fusion) | copy-start | bytes 3538948
  94.5 69.1 %collective-permute-start.8 = (bf16[1024,576]{0,1:T(8,128)(2,1)}, bf16[1024,576]{0,1:T(8,128)(2,1)S(1)}, u32[]{:S(2)}, u32[]{:S(2)}) collective-permute-start(bf16[1024,576]{0,1:T(8,128)(2,1)} %copy.27), channel_id=1, source_target_pairs={{0,1},{1,0},{2,3},{3,2},{4,5},{5,4},{6,7},{7,6},{8,9},{9,8},{10,11... | collective-permute-start | bytes 3538952 | tf_op jit(solution)/shard_map/ppermute | solution.py:182

commit v3 on v2

--- a/solution.py
+++ b/solution.py
@@ -58,8 +58,8 @@
     ).astype(jnp.bfloat16)
 
 
-def attend_kernel(meta_ref, fq_ref, start_ref, latent_ref, near_ref, far_ref, av_ref,
-                  out_ref, keys_ref, bias_ref, sems, *, scale, group):
+def attend_kernel(meta_ref, start_ref, fq_hbm, latent_ref, near_ref, far_ref, av_hbm,
+                  out_ref, keys_ref, bias_ref, fq_ref, av_ref, sems, *, scale, group):
     heads, rows = fq_ref.shape[0], fq_ref.shape[1]
     count = len(DISTANCES)
     quarters = near_ref.shape[0]
@@ -70,7 +70,13 @@
         copies.append(pltpu.make_async_copy(
             far_ref.at[i], keys_ref.at[pl.ds(0, count), meta_ref[1 + quarters + i]],
             sems.at[quarters + i]))
-    for copy in copies:
+    queries = [
+        pltpu.make_async_copy(fq_hbm.at[pl.ds(h, group)], fq_ref.at[pl.ds(h, group)],
+                              sems.at[2 * quarters + 1 + h // group])
+        for h in range(0, heads, group)
+    ]
+    values = pltpu.make_async_copy(av_hbm, av_ref, sems.at[2 * quarters + 1 + heads // group])
+    for copy in queries[:1] + copies + queries[1:] + [values]:
         copy.start()
     start = start_ref[...]
     ctx = meta_ref[0]
@@ -86,6 +92,7 @@
     factor = scale * LOG2E
     total_keys = (count + 1) * rows
     for h in range(0, heads, group):
+        queries[h // group].wait()
         q = fq_ref[h:h + group].reshape(group * rows, WIDTH)
         keys = keys_ref[...].reshape(total_keys, WIDTH)
         s = lax.dot_general(
@@ -100,6 +107,8 @@
             preferred_element_type=jnp.float32,
         ).reshape(group, rows, LATENT)
         mixed = (mixed / total).astype(jnp.bfloat16)
+        if h == 0:
+            values.wait()
         for g in range(group):
             out_ref[:, (h + g) * VDIM:(h + g + 1) * VDIM] = jnp.dot(
                 mixed[g], av_ref[h + g], preferred_element_type=jnp.float32
@@ -166,37 +175,36 @@
     def cat(*xs):
         return row_major(jnp.concatenate(xs, axis=0))
 
-    two = cat(shift(own, 1), shift(own, 9))
-    two, full_query, start, outgoing, meta = lax.optimization_barrier(
-        (two, full_query, start, outgoing, meta))
+    ninth = shift(own, 9)
+    two = cat(shift(own, 1), ninth)
     four = cat(two, shift(two, 4))
     eight = cat(four, shift(four, 2))
-    eight, outgoing = lax.optimization_barrier((eight, outgoing))
     arrived = lax.all_to_all(outgoing, "ctx", split_axis=0, concat_axis=0, tiled=True)
     late = shift(eight, 1)
     window = cat(eight, late)
 
     ring = lambda k: [(i, (i + k) % head_count) for i in range(head_count)]
     others = [lax.ppermute(window, "head", ring(k)) for k in range(1, head_count)]
-    near = cat(window, *others)
-    far = row_major(lax.ppermute(near, "dec", [(i, (i + 1) % dec_count) for i in range(dec_count)]))
-
     blocks = len(DISTANCES)
     parts = head_count * dec_count
-    by_share = lambda x: x.reshape(head_count, blocks, share, WIDTH)
+    group = 2
+    near = cat(window, *others).reshape(head_count, blocks, share, WIDTH)
+    far = lax.ppermute(near, "dec", [(i, (i + 1) % dec_count) for i in range(dec_count)])
     any_spec = pl.BlockSpec(memory_space=pl.ANY)
     answer = pl.pallas_call(
-        lambda *refs: attend_kernel(*refs, scale=scale, group=2),
+        lambda *refs: attend_kernel(*refs, scale=scale, group=group),
         out_shape=jax.ShapeDtypeStruct((rows, heads * VDIM), bf16),
-        in_specs=[SMEM] + vmem(2) + [any_spec] * 3 + vmem(1), out_specs=vmem(1)[0],
+        in_specs=[SMEM] + vmem(1) + [any_spec] * 5, out_specs=vmem(1)[0],
         scratch_shapes=[pltpu.VMEM((blocks + 1, parts, share, WIDTH), bf16),
                         pltpu.VMEM((rows, (blocks + 1) * rows), jnp.float32),
-                        pltpu.SemaphoreType.DMA((parts + 1,))],
+                        pltpu.VMEM(full_query.shape, bf16),
+                        pltpu.VMEM(absorb_value.shape, bf16),
+                        pltpu.SemaphoreType.DMA((parts + 2 + heads // group,))],
         name="attend",
         cost_estimate=pl.CostEstimate(
             flops=10_000_000_000, bytes_accessed=6_000_000, transcendentals=2_000_000),
-    )(meta, full_query, start, latent_rows.reshape(parts, share, WIDTH), by_share(near),
-      by_share(far), absorb_value)
+    )(meta, start, full_query, latent_rows.reshape(parts, share, WIDTH), near, far,
+      absorb_value)
     return (answer, arrived[None])
 
 

time: 179 us -> 171 us (0.955)
  the two profiles are of different devices: /device:TPU:33 before, /device:TPU:34 now
where the time goes in v3:
time: 171 us
  starting transfers between devices  98.6 us (58%)
  waiting for transfers between devices  45.7 us (27%)
  Pallas kernels  18.4 us (11%)
  local copies, waits for them, and re-layouts  5.83 us (3%)
    ppermute x5, starting transfers between devices, shift(): return lax.ppermute(x, 'ctx', [(i, i + k) for i in range(ctx_count - k)])  54.4 us
    all_to_all x1, starting transfers between devices, program(): lax.all_to_all(outgoing, 'ctx', split_axis=0, concat_axis=0, tiled=True)  31.3 us
    all_to_all x1, waiting for transfers between devices, program(): lax.all_to_all(outgoing, 'ctx', split_axis=0, concat_axis=0, tiled=True)  29 us
    pallas_call x1, Pallas kernels, program(): pl.pallas_call(lambda *refs: attend_kernel(*refs, scale=scale, group=grou...  13.1 us
    ppermute x3, starting transfers between devices, program(): lax.ppermute(window, 'head', ring(k))  10.8 us
    ppermute x3, waiting for transfers between devices, program(): lax.ppermute(window, 'head', ring(k))  8.7 us
    ppermute x5, waiting for transfers between devices, shift(): return lax.ppermute(x, 'ctx', [(i, i + k) for i in range(ctx_count - k)])  7.95 us
    unnamed x12, local copies, waits for them, and re-layouts  3.54 us
  transfers between devices with their start and end apart: 10, of which 8 were waited for; matrix products, arithmetic and copies ran while one was open for 2% of the time, Pallas kernels for 3%

profile of v3, /device:TPU:34, one launch (start us, length us, event | category | flops | bytes accessed | tf_op | source)
XLA Modules:
  0.0 170.6 jit_solution(1302309016598505398)
XLA Ops:
  0.6 1.1 copy.17.refs_2_
  1.7 4.7 %collective-permute-start = (bf16[16,576]{1,0:T(8,128)(2,1)S(1)}, bf16[16,576]{1,0:T(8,128)(2,1)S(1)}, u32[]{:S(2)}, u32[]{:S(2)}) collective-permute-start(bf16[16,576]{1,0:T(8,128)(2,1)S(1)} %constant_dynamic-slice_fusion), channel_id=1, source_target_pairs={{0,8},{8,16},{16,24},{24,32},{32,40},{40,48},{48,56},{56,64},{64,7... | collective-permute-start | bytes 55304 | tf_op jit(solution)/shard_map/ppermute | solution.py:170
  6.5 24.8 %collective-permute-start.1 = (bf16[16,576]{1,0:T(8,128)(2,1)S(1)}, bf16[16,576]{1,0:T(8,128)(2,1)S(1)}, u32[]{:S(2)}, u32[]{:S(2)}) collective-permute-start(bf16[16,576]{1,0:T(8,128)(2,1)S(1)} %constant_dynamic-slice_fusion), channel_id=1, source_target_pairs={{0,72},{8,80},{16,88},{24,96},{32,104},{40,112},{48,120},{56,128},... | collective-permute-start | bytes 55304 | tf_op jit(solution)/shard_map/ppermute | solution.py:170
  31.3 1.4 collective-permute-done.1
  32.8 12.5 %collective-permute-start.2 = (bf16[32,576]{1,0:T(8,128)(2,1)S(1)}, bf16[32,576]{1,0:T(8,128)(2,1)S(1)}, u32[]{:S(2)}, u32[]{:S(2)}) collective-permute-start(bf16[32,576]{1,0:T(8,128)(2,1)S(1)} %constant_dynamic-update-slice_fusion), channel_id=1, source_target_pairs={{0,32},{8,40},{16,48},{24,56},{32,64},{40,72},{48,80},{56,88},{64,... | collective-permute-start | bytes 110600 | tf_op jit(solution)/shard_map/ppermute | solution.py:170
  45.3 1.7 collective-permute-done.2
  47.0 8.1 %collective-permute-start.3 = (bf16[64,576]{1,0:T(8,128)(2,1)S(1)}, bf16[64,576]{1,0:T(8,128)(2,1)S(1)}, u32[]{:S(2)}, u32[]{:S(2)}) collective-permute-start(bf16[64,576]{1,0:T(8,128)(2,1)S(1)} %pad_maximum_fusion.3), channel_id=1, source_target_pairs={{0,16},{8,24},{16,32},{24,40},{32,48},{40,56},{48,64},{56,72},{64,... | collective-permute-start | bytes 221192 | tf_op jit(solution)/shard_map/ppermute | solution.py:170
  55.1 2.0 %collective-permute-done.3 = bf16[64,576]{1,0:T(8,128)(2,1)S(1)} collective-permute-done((bf16[64,576]{1,0:T(8,128)(2,1)S(1)}, bf16[64,576]{1,0:T(8,128)(2,1)S(1)}, u32[]{:S(2)}, u32[]{:S(2)}) %collective-permute-start.3) | collective-permute-done | bytes 73760 | tf_op jit(solution)/shard_map/ppermute | solution.py:170
  57.2 4.2 %collective-permute-start.4 = (bf16[128,576]{1,0:T(8,128)(2,1)S(1)}, bf16[128,576]{1,0:T(8,128)(2,1)S(1)}, u32[]{:S(2)}, u32[]{:S(2)}) collective-permute-start(bf16[128,576]{1,0:T(8,128)(2,1)S(1)} %pad_maximum_fusion.2), channel_id=1, source_target_pairs={{0,8},{8,16},{16,24},{24,32},{32,40},{40,48},{48,56},{56,64},{64,7... | collective-permute-start | bytes 442376 | tf_op jit(solution)/shard_map/ppermute | solution.py:170
  61.4 2.8 %collective-permute-done.4 = bf16[128,576]{1,0:T(8,128)(2,1)S(1)} collective-permute-done((bf16[128,576]{1,0:T(8,128)(2,1)S(1)}, bf16[128,576]{1,0:T(8,128)(2,1)S(1)}, u32[]{:S(2)}, u32[]{:S(2)}) %collective-permute-start.4) | collective-permute-done | bytes 147488 | tf_op jit(solution)/shard_map/ppermute | solution.py:170
  64.3 3.6 %collective-permute-start.5 = (bf16[256,576]{1,0:T(8,128)(2,1)S(1)}, bf16[256,576]{1,0:T(8,128)(2,1)S(1)}, u32[]{:S(2)}, u32[]{:S(2)}) collective-permute-start(bf16[256,576]{1,0:T(8,128)(2,1)S(1)} %pad_maximum_fusion.1), channel_id=1, source_target_pairs={{0,2},{2,4},{4,6},{6,0},{1,3},{3,5},{5,7},{7,1},{8,10},{10,12},{12... | collective-permute-start | bytes 884744 | tf_op jit(solution)/shard_map/ppermute | solution.py:187
  67.8 2.8 %collective-permute-start.6 = (bf16[256,576]{1,0:T(8,128)(2,1)S(1)}, bf16[256,576]{1,0:T(8,128)(2,1)S(1)}, u32[]{:S(2)}, u32[]{:S(2)}) collective-permute-start(bf16[256,576]{1,0:T(8,128)(2,1)S(1)} %pad_maximum_fusion.1), channel_id=1, source_target_pairs={{0,4},{2,6},{4,0},{6,2},{1,5},{3,7},{5,1},{7,3},{8,12},{10,14},{12... | collective-permute-start | bytes 884744 | tf_op jit(solution)/shard_map/ppermute | solution.py:187
  70.6 4.5 %collective-permute-start.7 = (bf16[256,576]{1,0:T(8,128)(2,1)S(1)}, bf16[256,576]{1,0:T(8,128)(2,1)S(1)}, u32[]{:S(2)}, u32[]{:S(2)}) collective-permute-start(bf16[256,576]{1,0:T(8,128)(2,1)S(1)} %pad_maximum_fusion.1), channel_id=1, source_target_pairs={{0,6},{2,0},{4,2},{6,4},{1,7},{3,1},{5,3},{7,5},{8,14},{10,8},{12,... | collective-permute-start | bytes 884744 | tf_op jit(solution)/shard_map/ppermute | solution.py:187
  75.1 1.5 collective-permute-done.5
  76.7 3.8 %collective-permute-done.6 = bf16[256,576]{1,0:T(8,128)(2,1)S(1)} collective-permute-done((bf16[256,576]{1,0:T(8,128)(2,1)S(1)}, bf16[256,576]{1,0:T(8,128)(2,1)S(1)}, u32[]{:S(2)}, u32[]{:S(2)}) %collective-permute-start.6) | collective-permute-done | bytes 294944 | tf_op jit(solution)/shard_map/ppermute | solution.py:187
  80.5 3.4 %collective-permute-done.7 = bf16[256,576]{1,0:T(8,128)(2,1)S(1)} collective-permute-done((bf16[256,576]{1,0:T(8,128)(2,1)S(1)}, bf16[256,576]{1,0:T(8,128)(2,1)S(1)}, u32[]{:S(2)}, u32[]{:S(2)}) %collective-permute-start.7) | collective-permute-done | bytes 294944 | tf_op jit(solution)/shard_map/ppermute | solution.py:187
  84.0 2.0 %collective-permute-start.8 = (bf16[4,16,16,576]{3,2,1,0:T(8,128)(2,1)S(1)}, bf16[4,16,16,576]{3,2,1,0:T(8,128)(2,1)S(1)}, u32[]{:S(2)}, u32[]{:S(2)}) collective-permute-start(bf16[4,16,16,576]{3,2,1,0:T(8,128)(2,1)S(1)} %bitcast.14), channel_id=1, source_target_pairs={{0,1},{1,0},{2,3},{3,2},{4,5},{5,4},{6,7},{7,6},{8,9},{9,8},{10,11... | collective-permute-start | bytes 3538952 | tf_op jit(solution)/shard_map/ppermute | solution.py:192
  86.7 2.0 %pick.1 = bf16[128,576]{1,0:T(8,128)(2,1)} custom-call(s32[1]{0:T(128)} %bitcast.12.refs_0_, s32[128,1]{1,0:T(8,128)} %copy.19.refs_1_, bf16[128,576]{1,0:T(8,128)(2,1)} %copy-done.1), custom_call_target="tpu_custom_call" | custom-call | tf_op jit(solution)/shard_map/pick/pallas_call | solution.py:158
  88.6 1.6 reshape.30
  90.3 31.3 %all-to-all-start = ((bf16[32,4,576]{2,1,0:T(4,128)(2,1)}), bf16[32,4,576]{2,1,0:T(4,128)(2,1)S(1)}, u32[]{:S(2)}, u32[]{:S(2)}) async-start(bf16[32,4,576]{2,1,0:T(4,128)(2,1)} %reshape.30), calls=%async_computation | async-start | bytes 327680 | tf_op jit(solution)/shard_map/all_to_all | solution.py:182
  122.8 3.4 %query.1 = (bf16[8,128,576]{2,1,0:T(8,128)(2,1)}, s32[128,128]{1,0:T(8,128)}) custom-call(s32[1]{0:T(128)} %bitcast.ctx_ref, bf16[128,1536]{1,0:T(8,128)(2,1)} %q_ref.1, bf16[8,128,512]{2,1,0:T(8,128)(2,1)} %ak_ref.1, f32[128,64]{1,0:T(8,128)} %get-tuple-element.9.cos_ref, f32[128,64]{1,0:T(8,128)} %get-tuple-element.10.sin_ref, s32[32,128]{1,0:T(8,128)} %bitcast.18), custom_call_target="tpu_custom_call" | custom-call | tf_op jit(solution)/shard_map/query/pallas_call | solution.py:145
  126.8 29.0 %all-to-all-done = bf16[32,4,576]{2,1,0:T(4,128)(2,1)S(1)} async-done(((bf16[32,4,576]{2,1,0:T(4,128)(2,1)}), bf16[32,4,576]{2,1,0:T(4,128)(2,1)S(1)}, u32[]{:S(2)}, u32[]{:S(2)}) %all-to-all-start) | async-done | bytes 147488 | tf_op jit(solution)/shard_map/all_to_all | solution.py:182
  155.8 1.1 copy-done.3
  156.9 13.1 %attend.1 = bf16[128,1024]{1,0:T(8,128)(2,1)} custom-call(s32[9]{0:T(128)} %stack.39.refs_0_, s32[128,128]{1,0:T(8,128)} %get-tuple-element.4.refs_1_, bf16[8,128,576]{2,1,0:T(8,128)(2,1)} %get-tuple-element.5.refs_2_, bf16[8,16,576]{2,1,0:T(8,128)(2,1)} %bitcast.16, bf16[4,16,16,576]{3,2,1,0:T(8,128)(2,1)} %bitcast.15, bf16[4,16,16,576]{3,2,1,0:T(8,128)(2,1)} %copy-done.3, ...), custom_call_target="tpu_custom_call" | custom-call | flops 10000000000 | bytes 6000000 | tf_op jit(solution)/shard_map/attend/pallas_call | solution.py:194
  (23 shorter events, 3.3 us)
Async XLA Ops:
  1.7 82.2 %copy-start.1 = (bf16[128,576]{1,0:T(8,128)(2,1)}, bf16[128,576]{1,0:T(8,128)(2,1)S(1)}, u32[]{:S(2)}) copy-start(bf16[128,576]{1,0:T(8,128)(2,1)S(1)} %copy.17.refs_2_) | copy-start | bytes 442372
  1.7 29.6 %collective-permute-start = (bf16[16,576]{1,0:T(8,128)(2,1)S(1)}, bf16[16,576]{1,0:T(8,128)(2,1)S(1)}, u32[]{:S(2)}, u32[]{:S(2)}) collective-permute-start(bf16[16,576]{1,0:T(8,128)(2,1)S(1)} %constant_dynamic-slice_fusion), channel_id=1, source_target_pairs={{0,8},{8,16},{16,24},{24,32},{32,40},{40,48},{48,56},{56,64},{64,7... | collective-permute-start | bytes 55304 | tf_op jit(solution)/shard_map/ppermute | solution.py:170
  6.5 26.3 %collective-permute-start.1 = (bf16[16,576]{1,0:T(8,128)(2,1)S(1)}, bf16[16,576]{1,0:T(8,128)(2,1)S(1)}, u32[]{:S(2)}, u32[]{:S(2)}) collective-permute-start(bf16[16,576]{1,0:T(8,128)(2,1)S(1)} %constant_dynamic-slice_fusion), channel_id=1, source_target_pairs={{0,72},{8,80},{16,88},{24,96},{32,104},{40,112},{48,120},{56,128},... | collective-permute-start | bytes 55304 | tf_op jit(solution)/shard_map/ppermute | solution.py:170
  32.8 14.2 %collective-permute-start.2 = (bf16[32,576]{1,0:T(8,128)(2,1)S(1)}, bf16[32,576]{1,0:T(8,128)(2,1)S(1)}, u32[]{:S(2)}, u32[]{:S(2)}) collective-permute-start(bf16[32,576]{1,0:T(8,128)(2,1)S(1)} %constant_dynamic-update-slice_fusion), channel_id=1, source_target_pairs={{0,32},{8,40},{16,48},{24,56},{32,64},{40,72},{48,80},{56,88},{64,... | collective-permute-start | bytes 110600 | tf_op jit(solution)/shard_map/ppermute | solution.py:170
  47.0 10.2 %collective-permute-start.3 = (bf16[64,576]{1,0:T(8,128)(2,1)S(1)}, bf16[64,576]{1,0:T(8,128)(2,1)S(1)}, u32[]{:S(2)}, u32[]{:S(2)}) collective-permute-start(bf16[64,576]{1,0:T(8,128)(2,1)S(1)} %pad_maximum_fusion.3), channel_id=1, source_target_pairs={{0,16},{8,24},{16,32},{24,40},{32,48},{40,56},{48,64},{56,72},{64,... | collective-permute-start | bytes 221192 | tf_op jit(solution)/shard_map/ppermute | solution.py:170
  57.2 7.0 %collective-permute-start.4 = (bf16[128,576]{1,0:T(8,128)(2,1)S(1)}, bf16[128,576]{1,0:T(8,128)(2,1)S(1)}, u32[]{:S(2)}, u32[]{:S(2)}) collective-permute-start(bf16[128,576]{1,0:T(8,128)(2,1)S(1)} %pad_maximum_fusion.2), channel_id=1, source_target_pairs={{0,8},{8,16},{16,24},{24,32},{32,40},{40,48},{48,56},{56,64},{64,7... | collective-permute-start | bytes 442376 | tf_op jit(solution)/shard_map/ppermute | solution.py:170
  64.2 21.7 %copy-start.2 = (s32[128,1]{0,1:T(1,128)S(1)}, s32[128,1]{0,1:T(1,128)}, u32[]{:S(2)}) copy-start(s32[128,1]{0,1:T(1,128)} %param.9) | copy-start | bytes 1540
  64.3 12.4 %collective-permute-start.5 = (bf16[256,576]{1,0:T(8,128)(2,1)S(1)}, bf16[256,576]{1,0:T(8,128)(2,1)S(1)}, u32[]{:S(2)}, u32[]{:S(2)}) collective-permute-start(bf16[256,576]{1,0:T(8,128)(2,1)S(1)} %pad_maximum_fusion.1), channel_id=1, source_target_pairs={{0,2},{2,4},{4,6},{6,0},{1,3},{3,5},{5,7},{7,1},{8,10},{10,12},{12... | collective-permute-start | bytes 884744 | tf_op jit(solution)/shard_map/ppermute | solution.py:187
  67.8 12.6 %collective-permute-start.6 = (bf16[256,576]{1,0:T(8,128)(2,1)S(1)}, bf16[256,576]{1,0:T(8,128)(2,1)S(1)}, u32[]{:S(2)}, u32[]{:S(2)}) collective-permute-start(bf16[256,576]{1,0:T(8,128)(2,1)S(1)} %pad_maximum_fusion.1), channel_id=1, source_target_pairs={{0,4},{2,6},{4,0},{6,2},{1,5},{3,7},{5,1},{7,3},{8,12},{10,14},{12... | collective-permute-start | bytes 884744 | tf_op jit(solution)/shard_map/ppermute | solution.py:187
  70.6 13.2 %collective-permute-start.7 = (bf16[256,576]{1,0:T(8,128)(2,1)S(1)}, bf16[256,576]{1,0:T(8,128)(2,1)S(1)}, u32[]{:S(2)}, u32[]{:S(2)}) collective-permute-start(bf16[256,576]{1,0:T(8,128)(2,1)S(1)} %pad_maximum_fusion.1), channel_id=1, source_target_pairs={{0,6},{2,0},{4,2},{6,4},{1,7},{3,1},{5,3},{7,5},{8,14},{10,8},{12,... | collective-permute-start | bytes 884744 | tf_op jit(solution)/shard_map/ppermute | solution.py:187
  84.0 42.2 %copy-start = (bf16[1024,576]{1,0:T(8,128)(2,1)}, bf16[1024,576]{1,0:T(8,128)(2,1)S(1)}, u32[]{:S(2)}) copy-start(bf16[1024,576]{1,0:T(8,128)(2,1)S(1)} %pad_maximum_fusion) | copy-start | bytes 3538948
  84.0 71.8 %collective-permute-start.8 = (bf16[4,16,16,576]{3,2,1,0:T(8,128)(2,1)S(1)}, bf16[4,16,16,576]{3,2,1,0:T(8,128)(2,1)S(1)}, u32[]{:S(2)}, u32[]{:S(2)}) collective-permute-start(bf16[4,16,16,576]{3,2,1,0:T(8,128)(2,1)S(1)} %bitcast.14), channel_id=1, source_target_pairs={{0,1},{1,0},{2,3},{3,2},{4,5},{5,4},{6,7},{7,6},{8,9},{9,8},{10,11... | collective-permute-start | bytes 3538952 | tf_op jit(solution)/shard_map/ppermute | solution.py:192
  90.3 65.5 %all-to-all-start = ((bf16[32,4,576]{2,1,0:T(4,128)(2,1)}), bf16[32,4,576]{2,1,0:T(4,128)(2,1)S(1)}, u32[]{:S(2)}, u32[]{:S(2)}) async-start(bf16[32,4,576]{2,1,0:T(4,128)(2,1)} %reshape.30), calls=%async_computation | async-start | bytes 327680 | tf_op jit(solution)/shard_map/all_to_all | solution.py:182
  155.8 1.1 copy-start.3

commit v4 on v3

--- a/solution.py
+++ b/solution.py
@@ -1,5 +1,6 @@
 import jax
 import jax.numpy as jnp
+import numpy as np
 from jax import lax
 from jax.experimental import pallas as pl
 from jax.experimental.pallas import tpu as pltpu
@@ -15,7 +16,8 @@
 HEAD_IN = NOPE + ROPE
 NEG = -1e30
 LOG2E = 1.4426950408889634
-DISTANCES = (1, 9, 5, 13, 3, 11, 7, 15, 2, 10, 6, 14, 4, 12, 8, 16)
+EARLY = (1, 9, 5, 13, 3, 11, 7, 15)
+LATE = (2, 10, 6, 14, 4, 12, 8, 16)
 
 
 def query_kernel(ctx_ref, q_ref, ak_ref, cos_ref, sin_ref, seg_ref, fq_ref, start_ref):
@@ -58,55 +60,51 @@
     ).astype(jnp.bfloat16)
 
 
-def attend_kernel(meta_ref, start_ref, fq_hbm, latent_ref, near_ref, far_ref, av_hbm,
-                  out_ref, keys_ref, bias_ref, fq_ref, av_ref, sems, *, scale, group):
+def attend_kernel(meta_ref, start_ref, offset_ref, fq_ref, latent_ref, near_early_ref,
+                  near_late_ref, far_early_ref, far_late_ref, av_hbm, out_ref, bias_ref, av_ref,
+                  sem, *, scale, group):
     heads, rows = fq_ref.shape[0], fq_ref.shape[1]
-    count = len(DISTANCES)
-    quarters = near_ref.shape[0]
-    copies = [pltpu.make_async_copy(latent_ref, keys_ref.at[count], sems.at[2 * quarters])]
-    for i in range(quarters):
-        copies.append(pltpu.make_async_copy(
-            near_ref.at[i], keys_ref.at[pl.ds(0, count), meta_ref[1 + i]], sems.at[i]))
-        copies.append(pltpu.make_async_copy(
-            far_ref.at[i], keys_ref.at[pl.ds(0, count), meta_ref[1 + quarters + i]],
-            sems.at[quarters + i]))
-    queries = [
-        pltpu.make_async_copy(fq_hbm.at[pl.ds(h, group)], fq_ref.at[pl.ds(h, group)],
-                              sems.at[2 * quarters + 1 + h // group])
-        for h in range(0, heads, group)
-    ]
-    values = pltpu.make_async_copy(av_hbm, av_ref, sems.at[2 * quarters + 1 + heads // group])
-    for copy in queries[:1] + copies + queries[1:] + [values]:
-        copy.start()
+    parts = (near_early_ref, near_late_ref, far_early_ref, far_late_ref)
+    wide = near_early_ref.shape[0]
+    pieces = wide // rows
+    values = pltpu.make_async_copy(av_hbm, av_ref, sem)
+    values.start()
     start = start_ref[...]
-    ctx = meta_ref[0]
+    base = meta_ref[0] * rows
+    for n in range(len(parts)):
+        offset = offset_ref[n % 2:n % 2 + 1, :]
+        for i in range(pieces):
+            share_start = meta_ref[1 + (n // 2) * pieces + i] * (rows // (2 * pieces))
+            seen = base + share_start + offset >= start
+            at = n * wide + i * rows
+            bias_ref[:, at:at + rows] = jnp.where(seen, 0.0, NEG)
     lane = lax.broadcasted_iota(jnp.int32, (rows, rows), 1)
     down = lax.broadcasted_iota(jnp.int32, (rows, rows), 0)
-    for b, dist in enumerate(DISTANCES):
-        seen = (ctx - dist) * rows + lane >= start
-        bias_ref[:, b * rows:(b + 1) * rows] = jnp.where(seen, 0.0, NEG)
-    seen = (ctx * rows + lane >= start) & (lane <= down)
-    bias_ref[:, count * rows:] = jnp.where(seen, 0.0, NEG)
-    for copy in copies:
-        copy.wait()
+    bias_ref[:, len(parts) * wide:] = jnp.where(
+        (base + lane >= start) & (lane <= down), 0.0, NEG)
     factor = scale * LOG2E
-    total_keys = (count + 1) * rows
+    parts = parts + (latent_ref,)
     for h in range(0, heads, group):
-        queries[h // group].wait()
         q = fq_ref[h:h + group].reshape(group * rows, WIDTH)
-        keys = keys_ref[...].reshape(total_keys, WIDTH)
-        s = lax.dot_general(
-            q, keys, (((1,), (1,)), ((), ())), preferred_element_type=jnp.float32
-        )
-        s = s.reshape(group, rows, total_keys) + bias_ref[...][None]
+        scores = []
+        for n, part in enumerate(parts):
+            s = lax.dot_general(
+                q, part[...], (((1,), (1,)), ((), ())), preferred_element_type=jnp.float32
+            )
+            bias = bias_ref[:, n * wide:n * wide + part.shape[0]]
+            scores.append(s.reshape(group, rows, -1) + bias[None])
+        s = jnp.concatenate(scores, axis=2)
         top = jnp.max(s, axis=2, keepdims=True)
         p = jnp.exp2((s - top) * factor)
         total = jnp.sum(p, axis=2, keepdims=True)
-        mixed = jnp.dot(
-            p.astype(jnp.bfloat16).reshape(group * rows, total_keys), keys[:, :LATENT],
-            preferred_element_type=jnp.float32,
-        ).reshape(group, rows, LATENT)
-        mixed = (mixed / total).astype(jnp.bfloat16)
+        p = p.astype(jnp.bfloat16).reshape(group * rows, -1)
+        mixed = jnp.zeros((group * rows, LATENT), jnp.float32)
+        for n, part in enumerate(parts):
+            mixed = mixed + jnp.dot(
+                p[:, n * wide:n * wide + part.shape[0]], part[:, :LATENT],
+                preferred_element_type=jnp.float32,
+            )
+        mixed = (mixed.reshape(group, rows, LATENT) / total).astype(jnp.bfloat16)
         if h == 0:
             values.wait()
         for g in range(group):
@@ -117,6 +115,10 @@
 
 def vmem(n):
     return [pl.BlockSpec(memory_space=pltpu.VMEM) for _ in range(n)]
+
+
+def KEEP(x):
+    return pltpu.with_memory_space_constraint(x, pltpu.VMEM)
 
 
 SMEM = pl.BlockSpec(memory_space=pltpu.SMEM)
@@ -144,9 +146,9 @@
     sin2 = jnp.concatenate([-sine, sine], axis=1)
     full_query, start = pl.pallas_call(
         query_kernel,
-        out_shape=(jax.ShapeDtypeStruct((heads, rows, WIDTH), bf16),
-                   jax.ShapeDtypeStruct((rows, rows), jnp.int32)),
-        in_specs=[SMEM] + vmem(5), out_specs=tuple(vmem(2)), name="query",
+        out_shape=(pltpu.VMEM((heads, rows, WIDTH), bf16),
+                   pltpu.VMEM((rows, rows), jnp.int32)),
+        in_specs=[SMEM] + vmem(5), out_specs=tuple(vmem(2)), name="query", compiler_params=pltpu.CompilerParams(vmem_limit_bytes=16 << 20),
     )(ctx[None], queries, absorb_key, cos2, sin2, segments.reshape(-1, rows))
     from_head = [(head - k) % head_count for k in range(head_count)]
     meta = jnp.stack(
@@ -158,7 +160,7 @@
     outgoing = pl.pallas_call(
         lambda *refs: pick_kernel(*refs, cores=dec_count, slots=slots),
         out_shape=jax.ShapeDtypeStruct((ctx_count * slots, WIDTH), bf16),
-        in_specs=[SMEM] + vmem(2), out_specs=vmem(1)[0], name="pick",
+        in_specs=[SMEM] + vmem(2), out_specs=vmem(1)[0], name="pick", compiler_params=pltpu.CompilerParams(vmem_limit_bytes=8 << 20),
     )(core[None], owners, latent_rows)
     outgoing = outgoing.reshape(ctx_count, slots, WIDTH)
 
@@ -181,30 +183,36 @@
     eight = cat(four, shift(four, 2))
     arrived = lax.all_to_all(outgoing, "ctx", split_axis=0, concat_axis=0, tiled=True)
     late = shift(eight, 1)
-    window = cat(eight, late)
-
-    ring = lambda k: [(i, (i + k) % head_count) for i in range(head_count)]
-    others = [lax.ppermute(window, "head", ring(k)) for k in range(1, head_count)]
-    blocks = len(DISTANCES)
-    parts = head_count * dec_count
+
+    def spread(x):
+        others = [
+            lax.ppermute(x, "head", [(i, (i + k) % head_count) for i in range(head_count)])
+            for k in range(1, head_count)
+        ]
+        near = cat(x, *others)
+        flat = near.reshape(head_count, -1, share, WIDTH)
+        far = lax.ppermute(flat, "dec", [(i, (i + 1) % dec_count) for i in range(dec_count)])
+        return near, far.reshape(near.shape)
+
+    near_early, far_early = spread(eight)
+    near_late, far_late = spread(late)
+    offset = jnp.asarray(np.array(
+        [[r % share - rows * d[r // share] for r in range(rows)] for d in (EARLY, LATE)], np.int32))
     group = 2
-    near = cat(window, *others).reshape(head_count, blocks, share, WIDTH)
-    far = lax.ppermute(near, "dec", [(i, (i + 1) % dec_count) for i in range(dec_count)])
-    any_spec = pl.BlockSpec(memory_space=pl.ANY)
     answer = pl.pallas_call(
         lambda *refs: attend_kernel(*refs, scale=scale, group=group),
         out_shape=jax.ShapeDtypeStruct((rows, heads * VDIM), bf16),
-        in_specs=[SMEM] + vmem(1) + [any_spec] * 5, out_specs=vmem(1)[0],
-        scratch_shapes=[pltpu.VMEM((blocks + 1, parts, share, WIDTH), bf16),
-                        pltpu.VMEM((rows, (blocks + 1) * rows), jnp.float32),
-                        pltpu.VMEM(full_query.shape, bf16),
-                        pltpu.VMEM(absorb_value.shape, bf16),
-                        pltpu.SemaphoreType.DMA((parts + 2 + heads // group,))],
-        name="attend",
+        in_specs=[SMEM] + vmem(8) + [pl.BlockSpec(memory_space=pltpu.HBM)],
+        out_specs=vmem(1)[0],
+        scratch_shapes=[
+            pltpu.VMEM((rows, (1 + len(EARLY) + len(LATE)) * rows), jnp.float32),
+            pltpu.VMEM(absorb_value.shape, bf16), pltpu.SemaphoreType.DMA],
+        name="attend", compiler_params=pltpu.CompilerParams(vmem_limit_bytes=20 << 20),
         cost_estimate=pl.CostEstimate(
             flops=10_000_000_000, bytes_accessed=6_000_000, transcendentals=2_000_000),
-    )(meta, start, full_query, latent_rows.reshape(parts, share, WIDTH), near, far,
-      absorb_value)
+    )(meta, KEEP(start), offset, KEEP(full_query), KEEP(latent_rows), KEEP(near_early),
+      KEEP(near_late), KEEP(far_early), KEEP(far_late),
+      pltpu.with_memory_space_constraint(absorb_value, pltpu.HBM))
     return (answer, arrived[None])
 
 

time: 171 us -> 162 us (0.947)
  the two profiles are of different devices: /device:TPU:34 before, /device:TPU:33 now
where the time goes in v4:
time: 162 us
  starting transfers between devices  112 us (69%)
  waiting for transfers between devices  30.3 us (19%)
  Pallas kernels  12.3 us (8%)
  local copies, waits for them, and re-layouts  5.15 us (3%)
    ppermute x5, starting transfers between devices, shift(): return lax.ppermute(x, 'ctx', [(i, i + k) for i in range(ctx_count - k)])  54.3 us
    all_to_all x1, starting transfers between devices, program(): lax.all_to_all(outgoing, 'ctx', split_axis=0, concat_axis=0, tiled=True)  30.4 us
    ppermute x6, starting transfers between devices, spread(): lax.ppermute(x, 'head', [(i, (i + k) % head_count) for i in range(head_co...  19.1 us
    all_to_all x1, waiting for transfers between devices, program(): lax.all_to_all(outgoing, 'ctx', split_axis=0, concat_axis=0, tiled=True)  18.3 us
    pallas_call x1, Pallas kernels, program(): pl.pallas_call(lambda *refs: attend_kernel(*refs, scale=scale, group=grou...  11 us
    ppermute x6, waiting for transfers between devices, spread(): lax.ppermute(x, 'head', [(i, (i + k) % head_count) for i in range(head_co...  8.65 us
    ppermute x2, starting transfers between devices, spread(): lax.ppermute(flat, 'dec', [(i, (i + 1) % dec_count) for i in range(dec_co...  8.38 us
    unnamed x21, local copies, waits for them, and re-layouts  4.3 us
  transfers between devices with their start and end apart: 14, of which 7 were waited for; matrix products, arithmetic and copies ran while one was open for 1% of the time, Pallas kernels for 8%

profile of v4, /device:TPU:33, one launch (start us, length us, event | category | flops | bytes accessed | tf_op | source)
XLA Modules:
  0.0 161.6 jit_solution(7865461326572969017)
XLA Ops:
  0.6 1.1 copy.19.refs_4_.refs_2_
  1.7 5.2 %collective-permute-start = (bf16[16,576]{1,0:T(8,128)(2,1)S(1)}, bf16[16,576]{1,0:T(8,128)(2,1)S(1)}, u32[]{:S(2)}, u32[]{:S(2)}) collective-permute-start(bf16[16,576]{1,0:T(8,128)(2,1)S(1)} %constant_dynamic-slice_fusion), channel_id=1, source_target_pairs={{0,8},{8,16},{16,24},{24,32},{32,40},{40,48},{48,56},{56,64},{64,7... | collective-permute-start | bytes 55304 | tf_op jit(solution)/shard_map/ppermute | solution.py:172
  7.0 24.6 %collective-permute-start.1 = (bf16[16,576]{1,0:T(8,128)(2,1)S(1)}, bf16[16,576]{1,0:T(8,128)(2,1)S(1)}, u32[]{:S(2)}, u32[]{:S(2)}) collective-permute-start(bf16[16,576]{1,0:T(8,128)(2,1)S(1)} %constant_dynamic-slice_fusion), channel_id=1, source_target_pairs={{0,72},{8,80},{16,88},{24,96},{32,104},{40,112},{48,120},{56,128},... | collective-permute-start | bytes 55304 | tf_op jit(solution)/shard_map/ppermute | solution.py:172
  32.4 12.5 %collective-permute-start.2 = (bf16[32,576]{1,0:T(8,128)(2,1)S(1)}, bf16[32,576]{1,0:T(8,128)(2,1)S(1)}, u32[]{:S(2)}, u32[]{:S(2)}) collective-permute-start(bf16[32,576]{1,0:T(8,128)(2,1)S(1)} %constant_dynamic-update-slice_fusion), channel_id=1, source_target_pairs={{0,32},{8,40},{16,48},{24,56},{32,64},{40,72},{48,80},{56,88},{64,... | collective-permute-start | bytes 110600 | tf_op jit(solution)/shard_map/ppermute | solution.py:172
  44.9 1.1 collective-permute-done.2
  46.0 8.1 %collective-permute-start.3 = (bf16[64,576]{1,0:T(8,128)(2,1)S(1)}, bf16[64,576]{1,0:T(8,128)(2,1)S(1)}, u32[]{:S(2)}, u32[]{:S(2)}) collective-permute-start(bf16[64,576]{1,0:T(8,128)(2,1)S(1)} %pad_maximum_fusion.2), channel_id=1, source_target_pairs={{0,16},{8,24},{16,32},{24,40},{32,48},{40,56},{48,64},{56,72},{64,... | collective-permute-start | bytes 221192 | tf_op jit(solution)/shard_map/ppermute | solution.py:172
  54.1 1.5 collective-permute-done.3
  55.6 3.9 %collective-permute-start.7 = (bf16[128,576]{1,0:T(8,128)(2,1)S(1)}, bf16[128,576]{1,0:T(8,128)(2,1)S(1)}, u32[]{:S(2)}, u32[]{:S(2)}) collective-permute-start(bf16[128,576]{1,0:T(8,128)(2,1)S(1)} %pad_maximum_fusion.1), channel_id=1, source_target_pairs={{0,8},{8,16},{16,24},{24,32},{32,40},{40,48},{48,56},{56,64},{64,7... | collective-permute-start | bytes 442376 | tf_op jit(solution)/shard_map/ppermute | solution.py:172
  59.5 2.8 %collective-permute-start.4 = (bf16[128,576]{1,0:T(8,128)(2,1)S(1)}, bf16[128,576]{1,0:T(8,128)(2,1)S(1)}, u32[]{:S(2)}, u32[]{:S(2)}) collective-permute-start(bf16[128,576]{1,0:T(8,128)(2,1)S(1)} %pad_maximum_fusion.1), channel_id=1, source_target_pairs={{0,2},{2,4},{4,6},{6,0},{1,3},{3,5},{5,7},{7,1},{8,10},{10,12},{12... | collective-permute-start | bytes 442376 | tf_op jit(solution)/shard_map/ppermute | solution.py:189
  62.4 4.7 %collective-permute-start.5 = (bf16[128,576]{1,0:T(8,128)(2,1)S(1)}, bf16[128,576]{1,0:T(8,128)(2,1)S(1)}, u32[]{:S(2)}, u32[]{:S(2)}) collective-permute-start(bf16[128,576]{1,0:T(8,128)(2,1)S(1)} %pad_maximum_fusion.1), channel_id=1, source_target_pairs={{0,4},{2,6},{4,0},{6,2},{1,5},{3,7},{5,1},{7,3},{8,12},{10,14},{12... | collective-permute-start | bytes 442376 | tf_op jit(solution)/shard_map/ppermute | solution.py:189
  67.1 3.0 %collective-permute-start.6 = (bf16[128,576]{1,0:T(8,128)(2,1)S(1)}, bf16[128,576]{1,0:T(8,128)(2,1)S(1)}, u32[]{:S(2)}, u32[]{:S(2)}) collective-permute-start(bf16[128,576]{1,0:T(8,128)(2,1)S(1)} %pad_maximum_fusion.1), channel_id=1, source_target_pairs={{0,6},{2,0},{4,2},{6,4},{1,7},{3,1},{5,3},{7,5},{8,14},{10,8},{12,... | collective-permute-start | bytes 442376 | tf_op jit(solution)/shard_map/ppermute | solution.py:189
  70.0 2.4 %collective-permute-start.8 = (bf16[128,576]{1,0:T(8,128)(2,1)S(1)}, bf16[128,576]{1,0:T(8,128)(2,1)S(1)}, u32[]{:S(2)}, u32[]{:S(2)}) collective-permute-start(bf16[128,576]{1,0:T(8,128)(2,1)S(1)} %collective-permute-done.7), channel_id=1, source_target_pairs={{0,2},{2,4},{4,6},{6,0},{1,3},{3,5},{5,7},{7,1},{8,10},{10,12},{12... | collective-permute-start | bytes 442376 | tf_op jit(solution)/shard_map/ppermute | solution.py:189
  72.4 2.5 %collective-permute-done.6 = bf16[128,576]{1,0:T(8,128)(2,1)S(1)} collective-permute-done((bf16[128,576]{1,0:T(8,128)(2,1)S(1)}, bf16[128,576]{1,0:T(8,128)(2,1)S(1)}, u32[]{:S(2)}, u32[]{:S(2)}) %collective-permute-start.6) | collective-permute-done | bytes 147488 | tf_op jit(solution)/shard_map/ppermute | solution.py:189
  75.0 5.6 %collective-permute-start.11 = (bf16[4,8,16,576]{3,2,1,0:T(8,128)(2,1)S(1)}, bf16[4,8,16,576]{3,2,1,0:T(8,128)(2,1)}, u32[]{:S(2)}, u32[]{:S(2)}) collective-permute-start(bf16[4,8,16,576]{3,2,1,0:T(8,128)(2,1)S(1)} %bitcast.16), channel_id=1, source_target_pairs={{0,1},{1,0},{2,3},{3,2},{4,5},{5,4},{6,7},{7,6},{8,9},{9,8},{10,11... | collective-permute-start | bytes 1769480 | tf_op jit(solution)/shard_map/ppermute | solution.py:194
  80.6 2.4 %collective-permute-start.9 = (bf16[128,576]{1,0:T(8,128)(2,1)S(1)}, bf16[128,576]{1,0:T(8,128)(2,1)S(1)}, u32[]{:S(2)}, u32[]{:S(2)}) collective-permute-start(bf16[128,576]{1,0:T(8,128)(2,1)S(1)} %collective-permute-done.7), channel_id=1, source_target_pairs={{0,4},{2,6},{4,0},{6,2},{1,5},{3,7},{5,1},{7,3},{8,12},{10,14},{12... | collective-permute-start | bytes 442376 | tf_op jit(solution)/shard_map/ppermute | solution.py:189
  83.1 3.8 %collective-permute-start.10 = (bf16[128,576]{1,0:T(8,128)(2,1)S(1)}, bf16[128,576]{1,0:T(8,128)(2,1)S(1)}, u32[]{:S(2)}, u32[]{:S(2)}) collective-permute-start(bf16[128,576]{1,0:T(8,128)(2,1)S(1)} %collective-permute-done.7), channel_id=1, source_target_pairs={{0,6},{2,0},{4,2},{6,4},{1,7},{3,1},{5,3},{7,5},{8,14},{10,8},{12,... | collective-permute-start | bytes 442376 | tf_op jit(solution)/shard_map/ppermute | solution.py:189
  87.0 2.8 %collective-permute-done.9 = bf16[128,576]{1,0:T(8,128)(2,1)S(1)} collective-permute-done((bf16[128,576]{1,0:T(8,128)(2,1)S(1)}, bf16[128,576]{1,0:T(8,128)(2,1)S(1)}, u32[]{:S(2)}, u32[]{:S(2)}) %collective-permute-start.9) | collective-permute-done | bytes 147488 | tf_op jit(solution)/shard_map/ppermute | solution.py:189
  89.8 3.3 %collective-permute-done.10 = bf16[128,576]{1,0:T(8,128)(2,1)S(1)} collective-permute-done((bf16[128,576]{1,0:T(8,128)(2,1)S(1)}, bf16[128,576]{1,0:T(8,128)(2,1)S(1)}, u32[]{:S(2)}, u32[]{:S(2)}) %collective-permute-start.10) | collective-permute-done | bytes 147488 | tf_op jit(solution)/shard_map/ppermute | solution.py:189
  93.1 2.8 %collective-permute-start.12 = (bf16[4,8,16,576]{3,2,1,0:T(8,128)(2,1)S(1)}, bf16[4,8,16,576]{3,2,1,0:T(8,128)(2,1)}, u32[]{:S(2)}, u32[]{:S(2)}) collective-permute-start(bf16[4,8,16,576]{3,2,1,0:T(8,128)(2,1)S(1)} %bitcast.17), channel_id=1, source_target_pairs={{0,1},{1,0},{2,3},{3,2},{4,5},{5,4},{6,7},{7,6},{8,9},{9,8},{10,11... | collective-permute-start | bytes 1769480 | tf_op jit(solution)/shard_map/ppermute | solution.py:194
  97.2 30.4 %all-to-all-start = ((bf16[32,4,576]{2,1,0:T(4,128)(2,1)}), bf16[32,4,576]{2,1,0:T(4,128)(2,1)S(1)}, u32[]{:S(2)}, u32[]{:S(2)}) async-start(bf16[32,4,576]{2,1,0:T(4,128)(2,1)} %reshape.38), calls=%async_computation | async-start | bytes 327680 | tf_op jit(solution)/shard_map/all_to_all | solution.py:184
  129.1 1.1 copy-done.3
  130.3 1.3 copy-done.4
  131.6 11.0 %attend.1 = bf16[128,1024]{1,0:T(8,128)(2,1)} custom-call(s32[9]{0:T(128)S(1)} %stack.39.refs_0_, s32[128,128]{1,0:T(8,128)S(1)} %get-tuple-element.4.refs_1_, s32[2,128]{1,0:T(2,128)S(1)} %copy-done.5, bf16[8,128,576]{2,1,0:T(8,128)(2,1)S(1)} %copy-done.4, bf16[128,576]{1,0:T(8,128)(2,1)S(1)} %copy.19.refs_4_.refs_2_, ...), custom_call_target="tpu_custom_call" | custom-call | flops 10000000000 | bytes 6000000 | tf_op jit(solution)/shard_map/attend/pallas_call | solution.py:202
  142.7 18.3 %all-to-all-done = bf16[32,4,576]{2,1,0:T(4,128)(2,1)S(1)} async-done(((bf16[32,4,576]{2,1,0:T(4,128)(2,1)}), bf16[32,4,576]{2,1,0:T(4,128)(2,1)S(1)}, u32[]{:S(2)}, u32[]{:S(2)}) %all-to-all-start) | async-done | bytes 147488 | tf_op jit(solution)/shard_map/all_to_all | solution.py:184
  (40 shorter events, 4.4 us)
Async XLA Ops:
  1.7 29.8 %collective-permute-start = (bf16[16,576]{1,0:T(8,128)(2,1)S(1)}, bf16[16,576]{1,0:T(8,128)(2,1)S(1)}, u32[]{:S(2)}, u32[]{:S(2)}) collective-permute-start(bf16[16,576]{1,0:T(8,128)(2,1)S(1)} %constant_dynamic-slice_fusion), channel_id=1, source_target_pairs={{0,8},{8,16},{16,24},{24,32},{32,40},{40,48},{48,56},{56,64},{64,7... | collective-permute-start | bytes 55304 | tf_op jit(solution)/shard_map/ppermute | solution.py:172
  7.0 25.5 %collective-permute-start.1 = (bf16[16,576]{1,0:T(8,128)(2,1)S(1)}, bf16[16,576]{1,0:T(8,128)(2,1)S(1)}, u32[]{:S(2)}, u32[]{:S(2)}) collective-permute-start(bf16[16,576]{1,0:T(8,128)(2,1)S(1)} %constant_dynamic-slice_fusion), channel_id=1, source_target_pairs={{0,72},{8,80},{16,88},{24,96},{32,104},{40,112},{48,120},{56,128},... | collective-permute-start | bytes 55304 | tf_op jit(solution)/shard_map/ppermute | solution.py:172
  32.4 13.5 %collective-permute-start.2 = (bf16[32,576]{1,0:T(8,128)(2,1)S(1)}, bf16[32,576]{1,0:T(8,128)(2,1)S(1)}, u32[]{:S(2)}, u32[]{:S(2)}) collective-permute-start(bf16[32,576]{1,0:T(8,128)(2,1)S(1)} %constant_dynamic-update-slice_fusion), channel_id=1, source_target_pairs={{0,32},{8,40},{16,48},{24,56},{32,64},{40,72},{48,80},{56,88},{64,... | collective-permute-start | bytes 110600 | tf_op jit(solution)/shard_map/ppermute | solution.py:172
  46.0 9.6 %collective-permute-start.3 = (bf16[64,576]{1,0:T(8,128)(2,1)S(1)}, bf16[64,576]{1,0:T(8,128)(2,1)S(1)}, u32[]{:S(2)}, u32[]{:S(2)}) collective-permute-start(bf16[64,576]{1,0:T(8,128)(2,1)S(1)} %pad_maximum_fusion.2), channel_id=1, source_target_pairs={{0,16},{8,24},{16,32},{24,40},{32,48},{40,56},{48,64},{56,72},{64,... | collective-permute-start | bytes 221192 | tf_op jit(solution)/shard_map/ppermute | solution.py:172
  55.6 40.4 %copy-start.6 = (s32[128,1]{0,1:T(1,128)S(1)}, s32[128,1]{0,1:T(1,128)}, u32[]{:S(2)}) copy-start(s32[128,1]{0,1:T(1,128)} %param.10) | copy-start | bytes 1540
  55.6 14.4 %collective-permute-start.7 = (bf16[128,576]{1,0:T(8,128)(2,1)S(1)}, bf16[128,576]{1,0:T(8,128)(2,1)S(1)}, u32[]{:S(2)}, u32[]{:S(2)}) collective-permute-start(bf16[128,576]{1,0:T(8,128)(2,1)S(1)} %pad_maximum_fusion.1), channel_id=1, source_target_pairs={{0,8},{8,16},{16,24},{24,32},{32,40},{40,48},{48,56},{56,64},{64,7... | collective-permute-start | bytes 442376 | tf_op jit(solution)/shard_map/ppermute | solution.py:172
  59.5 12.9 %collective-permute-start.4 = (bf16[128,576]{1,0:T(8,128)(2,1)S(1)}, bf16[128,576]{1,0:T(8,128)(2,1)S(1)}, u32[]{:S(2)}, u32[]{:S(2)}) collective-permute-start(bf16[128,576]{1,0:T(8,128)(2,1)S(1)} %pad_maximum_fusion.1), channel_id=1, source_target_pairs={{0,2},{2,4},{4,6},{6,0},{1,3},{3,5},{5,7},{7,1},{8,10},{10,12},{12... | collective-permute-start | bytes 442376 | tf_op jit(solution)/shard_map/ppermute | solution.py:189
  62.4 10.1 %collective-permute-start.5 = (bf16[128,576]{1,0:T(8,128)(2,1)S(1)}, bf16[128,576]{1,0:T(8,128)(2,1)S(1)}, u32[]{:S(2)}, u32[]{:S(2)}) collective-permute-start(bf16[128,576]{1,0:T(8,128)(2,1)S(1)} %pad_maximum_fusion.1), channel_id=1, source_target_pairs={{0,4},{2,6},{4,0},{6,2},{1,5},{3,7},{5,1},{7,3},{8,12},{10,14},{12... | collective-permute-start | bytes 442376 | tf_op jit(solution)/shard_map/ppermute | solution.py:189
  67.1 7.9 %collective-permute-start.6 = (bf16[128,576]{1,0:T(8,128)(2,1)S(1)}, bf16[128,576]{1,0:T(8,128)(2,1)S(1)}, u32[]{:S(2)}, u32[]{:S(2)}) collective-permute-start(bf16[128,576]{1,0:T(8,128)(2,1)S(1)} %pad_maximum_fusion.1), channel_id=1, source_target_pairs={{0,6},{2,0},{4,2},{6,4},{1,7},{3,1},{5,3},{7,5},{8,14},{10,8},{12,... | collective-permute-start | bytes 442376 | tf_op jit(solution)/shard_map/ppermute | solution.py:189
  70.0 16.9 %collective-permute-start.8 = (bf16[128,576]{1,0:T(8,128)(2,1)S(1)}, bf16[128,576]{1,0:T(8,128)(2,1)S(1)}, u32[]{:S(2)}, u32[]{:S(2)}) collective-permute-start(bf16[128,576]{1,0:T(8,128)(2,1)S(1)} %collective-permute-done.7), channel_id=1, source_target_pairs={{0,2},{2,4},{4,6},{6,0},{1,3},{3,5},{5,7},{7,1},{8,10},{10,12},{12... | collective-permute-start | bytes 442376 | tf_op jit(solution)/shard_map/ppermute | solution.py:189
  75.0 55.2 %collective-permute-start.11 = (bf16[4,8,16,576]{3,2,1,0:T(8,128)(2,1)S(1)}, bf16[4,8,16,576]{3,2,1,0:T(8,128)(2,1)}, u32[]{:S(2)}, u32[]{:S(2)}) collective-permute-start(bf16[4,8,16,576]{3,2,1,0:T(8,128)(2,1)S(1)} %bitcast.16), channel_id=1, source_target_pairs={{0,1},{1,0},{2,3},{3,2},{4,5},{5,4},{6,7},{7,6},{8,9},{9,8},{10,11... | collective-permute-start | bytes 1769480 | tf_op jit(solution)/shard_map/ppermute | solution.py:194
  80.6 9.2 %collective-permute-start.9 = (bf16[128,576]{1,0:T(8,128)(2,1)S(1)}, bf16[128,576]{1,0:T(8,128)(2,1)S(1)}, u32[]{:S(2)}, u32[]{:S(2)}) collective-permute-start(bf16[128,576]{1,0:T(8,128)(2,1)S(1)} %collective-permute-done.7), channel_id=1, source_target_pairs={{0,4},{2,6},{4,0},{6,2},{1,5},{3,7},{5,1},{7,3},{8,12},{10,14},{12... | collective-permute-start | bytes 442376 | tf_op jit(solution)/shard_map/ppermute | solution.py:189
  83.0 45.1 %copy-start = (bf16[8,128,512]{2,1,0:T(8,128)(2,1)S(1)}, bf16[8,128,512]{2,1,0:T(8,128)(2,1)}, u32[]{:S(2)}) copy-start(bf16[8,128,512]{2,1,0:T(8,128)(2,1)} %ak_ref.1) | copy-start | bytes 3145732
  83.0 45.1 %copy-start.1 = (bf16[128,1536]{1,0:T(8,128)(2,1)S(1)}, bf16[128,1536]{1,0:T(8,128)(2,1)}, u32[]{:S(2)}) copy-start(bf16[128,1536]{1,0:T(8,128)(2,1)} %q_ref.1) | copy-start | bytes 1179652
  83.1 45.1 %copy-start.2 = (s32[4096]{0:T(1024)S(1)}, s32[4096]{0:T(1024)}, u32[]{:S(2)}) copy-start(s32[4096]{0:T(1024)} %param.9) | copy-start | bytes 49156
  83.1 10.0 %collective-permute-start.10 = (bf16[128,576]{1,0:T(8,128)(2,1)S(1)}, bf16[128,576]{1,0:T(8,128)(2,1)S(1)}, u32[]{:S(2)}, u32[]{:S(2)}) collective-permute-start(bf16[128,576]{1,0:T(8,128)(2,1)S(1)} %collective-permute-done.7), channel_id=1, source_target_pairs={{0,6},{2,0},{4,2},{6,4},{1,7},{3,1},{5,3},{7,5},{8,14},{10,8},{12,... | collective-permute-start | bytes 442376 | tf_op jit(solution)/shard_map/ppermute | solution.py:189
  93.1 37.1 %collective-permute-start.12 = (bf16[4,8,16,576]{3,2,1,0:T(8,128)(2,1)S(1)}, bf16[4,8,16,576]{3,2,1,0:T(8,128)(2,1)}, u32[]{:S(2)}, u32[]{:S(2)}) collective-permute-start(bf16[4,8,16,576]{3,2,1,0:T(8,128)(2,1)S(1)} %bitcast.17), channel_id=1, source_target_pairs={{0,1},{1,0},{2,3},{3,2},{4,5},{5,4},{6,7},{7,6},{8,9},{9,8},{10,11... | collective-permute-start | bytes 1769480 | tf_op jit(solution)/shard_map/ppermute | solution.py:194
  97.2 33.1 %copy-start.5 = (s32[2,128]{1,0:T(2,128)S(1)}, s32[2,128]{1,0:T(2,128)}, u32[]{:S(2)}) copy-start(s32[2,128]{1,0:T(2,128)} %constant.63.clone.refs_2_) | copy-start | bytes 3076
  97.2 63.8 %all-to-all-start = ((bf16[32,4,576]{2,1,0:T(4,128)(2,1)}), bf16[32,4,576]{2,1,0:T(4,128)(2,1)S(1)}, u32[]{:S(2)}, u32[]{:S(2)}) async-start(bf16[32,4,576]{2,1,0:T(4,128)(2,1)} %reshape.38), calls=%async_computation | async-start | bytes 327680 | tf_op jit(solution)/shard_map/all_to_all | solution.py:184
  129.1 1.1 copy-start.3
  130.3 1.3 copy-start.4

commit v5 on v4

--- a/solution.py
+++ b/solution.py
@@ -60,24 +60,23 @@
     ).astype(jnp.bfloat16)
 
 
-def attend_kernel(meta_ref, start_ref, offset_ref, fq_ref, latent_ref, near_early_ref,
-                  near_late_ref, far_early_ref, far_late_ref, av_hbm, out_ref, bias_ref, av_ref,
-                  sem, *, scale, group):
+def attend_kernel(meta_ref, start_ref, offset_ref, fq_ref, latent_ref, near_ref, far_ref,
+                  av_hbm, out_ref, bias_ref, av_ref, sem, *, scale, group):
     heads, rows = fq_ref.shape[0], fq_ref.shape[1]
-    parts = (near_early_ref, near_late_ref, far_early_ref, far_late_ref)
-    wide = near_early_ref.shape[0]
-    pieces = wide // rows
+    parts = (near_ref, far_ref)
+    wide = near_ref.shape[0]
+    pieces = wide // (2 * rows)
     values = pltpu.make_async_copy(av_hbm, av_ref, sem)
     values.start()
     start = start_ref[...]
     base = meta_ref[0] * rows
     for n in range(len(parts)):
-        offset = offset_ref[n % 2:n % 2 + 1, :]
         for i in range(pieces):
-            share_start = meta_ref[1 + (n // 2) * pieces + i] * (rows // (2 * pieces))
-            seen = base + share_start + offset >= start
-            at = n * wide + i * rows
-            bias_ref[:, at:at + rows] = jnp.where(seen, 0.0, NEG)
+            share_start = meta_ref[1 + n * pieces + i] * (rows // (2 * pieces))
+            for k in range(2):
+                seen = base + share_start + offset_ref[k:k + 1, :] >= start
+                at = n * wide + (2 * i + k) * rows
+                bias_ref[:, at:at + rows] = jnp.where(seen, 0.0, NEG)
     lane = lax.broadcasted_iota(jnp.int32, (rows, rows), 1)
     down = lax.broadcasted_iota(jnp.int32, (rows, rows), 0)
     bias_ref[:, len(parts) * wide:] = jnp.where(
@@ -184,25 +183,22 @@
     arrived = lax.all_to_all(outgoing, "ctx", split_axis=0, concat_axis=0, tiled=True)
     late = shift(eight, 1)
 
-    def spread(x):
-        others = [
-            lax.ppermute(x, "head", [(i, (i + k) % head_count) for i in range(head_count)])
-            for k in range(1, head_count)
-        ]
-        near = cat(x, *others)
-        flat = near.reshape(head_count, -1, share, WIDTH)
-        far = lax.ppermute(flat, "dec", [(i, (i + 1) % dec_count) for i in range(dec_count)])
-        return near, far.reshape(near.shape)
-
-    near_early, far_early = spread(eight)
-    near_late, far_late = spread(late)
+    window = cat(eight, late)
+    others = [
+        lax.ppermute(window, "head", [(i, (i + k) % head_count) for i in range(head_count)])
+        for k in range(1, head_count)
+    ]
+    near = cat(window, *others)
+    near = near.reshape(head_count, 2 * len(EARLY), share, WIDTH)
+    far = lax.ppermute(near, "dec", [(i, (i + 1) % dec_count) for i in range(dec_count)])
+    keys = lambda x: KEEP(x.reshape(head_count * 2 * rows, WIDTH))
     offset = jnp.asarray(np.array(
         [[r % share - rows * d[r // share] for r in range(rows)] for d in (EARLY, LATE)], np.int32))
     group = 2
     answer = pl.pallas_call(
         lambda *refs: attend_kernel(*refs, scale=scale, group=group),
         out_shape=jax.ShapeDtypeStruct((rows, heads * VDIM), bf16),
-        in_specs=[SMEM] + vmem(8) + [pl.BlockSpec(memory_space=pltpu.HBM)],
+        in_specs=[SMEM] + vmem(6) + [pl.BlockSpec(memory_space=pltpu.HBM)],
         out_specs=vmem(1)[0],
         scratch_shapes=[
             pltpu.VMEM((rows, (1 + len(EARLY) + len(LATE)) * rows), jnp.float32),
@@ -210,8 +206,7 @@
         name="attend", compiler_params=pltpu.CompilerParams(vmem_limit_bytes=20 << 20),
         cost_estimate=pl.CostEstimate(
             flops=10_000_000_000, bytes_accessed=6_000_000, transcendentals=2_000_000),
-    )(meta, KEEP(start), offset, KEEP(full_query), KEEP(latent_rows), KEEP(near_early),
-      KEEP(near_late), KEEP(far_early), KEEP(far_late),
+    )(meta, KEEP(start), offset, KEEP(full_query), KEEP(latent_rows), keys(near), keys(far),
       pltpu.with_memory_space_constraint(absorb_value, pltpu.HBM))
     return (answer, arrived[None])
 

time: 162 us -> 167 us (1.031)
  the two profiles are of different devices: /device:TPU:33 before, /device:TPU:42 now
where the time goes in v5:
time: 167 us; the launch traced here: 166 us
  starting transfers between devices  98.8 us (59%)
  waiting for transfers between devices  48.2 us (29%)
  Pallas kernels  12.4 us (7%)
  local copies, waits for them, and re-layouts  5.07 us (3%)
    ppermute x5, starting transfers between devices, shift(): return lax.ppermute(x, 'ctx', [(i, i + k) for i in range(ctx_count - k)])  54.4 us
    all_to_all x1, waiting for transfers between devices, program(): lax.all_to_all(outgoing, 'ctx', split_axis=0, concat_axis=0, tiled=True)  31.5 us
    all_to_all x1, starting transfers between devices, program(): lax.all_to_all(outgoing, 'ctx', split_axis=0, concat_axis=0, tiled=True)  31.5 us
    pallas_call x1, Pallas kernels, program(): pl.pallas_call(lambda *refs: attend_kernel(*refs, scale=scale, group=grou...  11.1 us
    ppermute x3, starting transfers between devices, program(): lax.ppermute(window, 'head', [(i, (i + k) % head_count) for i in range(he...  10.8 us
    ppermute x3, waiting for transfers between devices, program(): lax.ppermute(window, 'head', [(i, (i + k) % head_count) for i in range(he...  8.7 us
    ppermute x5, waiting for transfers between devices, shift(): return lax.ppermute(x, 'ctx', [(i, i + k) for i in range(ctx_count - k)])  7.95 us
    unnamed x18, local copies, waits for them, and re-layouts  4.25 us
  transfers between devices with their start and end apart: 10, of which 8 were waited for; matrix products, arithmetic and copies ran while one was open for 1% of the time, Pallas kernels for 1%

profile of v5, /device:TPU:42, one launch (start us, length us, event | category | flops | bytes accessed | tf_op | source)
XLA Modules:
  0.0 166.0 jit_solution(3720356796237658301)
XLA Ops:
  0.6 1.1 copy.19.refs_4_.refs_2_
  1.7 4.7 %collective-permute-start = (bf16[16,576]{1,0:T(8,128)(2,1)S(1)}, bf16[16,576]{1,0:T(8,128)(2,1)S(1)}, u32[]{:S(2)}, u32[]{:S(2)}) collective-permute-start(bf16[16,576]{1,0:T(8,128)(2,1)S(1)} %constant_dynamic-slice_fusion), channel_id=1, source_target_pairs={{0,8},{8,16},{16,24},{24,32},{32,40},{40,48},{48,56},{56,64},{64,7... | collective-permute-start | bytes 55304 | tf_op jit(solution)/shard_map/ppermute | solution.py:171
  6.4 24.8 %collective-permute-start.1 = (bf16[16,576]{1,0:T(8,128)(2,1)S(1)}, bf16[16,576]{1,0:T(8,128)(2,1)S(1)}, u32[]{:S(2)}, u32[]{:S(2)}) collective-permute-start(bf16[16,576]{1,0:T(8,128)(2,1)S(1)} %constant_dynamic-slice_fusion), channel_id=1, source_target_pairs={{0,72},{8,80},{16,88},{24,96},{32,104},{40,112},{48,120},{56,128},... | collective-permute-start | bytes 55304 | tf_op jit(solution)/shard_map/ppermute | solution.py:171
  31.3 1.4 collective-permute-done.1
  32.8 12.5 %collective-permute-start.2 = (bf16[32,576]{1,0:T(8,128)(2,1)S(1)}, bf16[32,576]{1,0:T(8,128)(2,1)S(1)}, u32[]{:S(2)}, u32[]{:S(2)}) collective-permute-start(bf16[32,576]{1,0:T(8,128)(2,1)S(1)} %constant_dynamic-update-slice_fusion), channel_id=1, source_target_pairs={{0,32},{8,40},{16,48},{24,56},{32,64},{40,72},{48,80},{56,88},{64,... | collective-permute-start | bytes 110600 | tf_op jit(solution)/shard_map/ppermute | solution.py:171
  45.3 1.7 collective-permute-done.2
  47.0 8.1 %collective-permute-start.3 = (bf16[64,576]{1,0:T(8,128)(2,1)S(1)}, bf16[64,576]{1,0:T(8,128)(2,1)S(1)}, u32[]{:S(2)}, u32[]{:S(2)}) collective-permute-start(bf16[64,576]{1,0:T(8,128)(2,1)S(1)} %pad_maximum_fusion.3), channel_id=1, source_target_pairs={{0,16},{8,24},{16,32},{24,40},{32,48},{40,56},{48,64},{56,72},{64,... | collective-permute-start | bytes 221192 | tf_op jit(solution)/shard_map/ppermute | solution.py:171
  55.1 2.0 %collective-permute-done.3 = bf16[64,576]{1,0:T(8,128)(2,1)S(1)} collective-permute-done((bf16[64,576]{1,0:T(8,128)(2,1)S(1)}, bf16[64,576]{1,0:T(8,128)(2,1)S(1)}, u32[]{:S(2)}, u32[]{:S(2)}) %collective-permute-start.3) | collective-permute-done | bytes 73760 | tf_op jit(solution)/shard_map/ppermute | solution.py:171
  57.2 4.2 %collective-permute-start.4 = (bf16[128,576]{1,0:T(8,128)(2,1)S(1)}, bf16[128,576]{1,0:T(8,128)(2,1)S(1)}, u32[]{:S(2)}, u32[]{:S(2)}) collective-permute-start(bf16[128,576]{1,0:T(8,128)(2,1)S(1)} %pad_maximum_fusion.2), channel_id=1, source_target_pairs={{0,8},{8,16},{16,24},{24,32},{32,40},{40,48},{48,56},{56,64},{64,7... | collective-permute-start | bytes 442376 | tf_op jit(solution)/shard_map/ppermute | solution.py:171
  61.4 2.8 %collective-permute-done.4 = bf16[128,576]{1,0:T(8,128)(2,1)S(1)} collective-permute-done((bf16[128,576]{1,0:T(8,128)(2,1)S(1)}, bf16[128,576]{1,0:T(8,128)(2,1)S(1)}, u32[]{:S(2)}, u32[]{:S(2)}) %collective-permute-start.4) | collective-permute-done | bytes 147488 | tf_op jit(solution)/shard_map/ppermute | solution.py:171
  64.2 3.6 %collective-permute-start.5 = (bf16[256,576]{1,0:T(8,128)(2,1)S(1)}, bf16[256,576]{1,0:T(8,128)(2,1)S(1)}, u32[]{:S(2)}, u32[]{:S(2)}) collective-permute-start(bf16[256,576]{1,0:T(8,128)(2,1)S(1)} %pad_maximum_fusion.1), channel_id=1, source_target_pairs={{0,2},{2,4},{4,6},{6,0},{1,3},{3,5},{5,7},{7,1},{8,10},{10,12},{12... | collective-permute-start | bytes 884744 | tf_op jit(solution)/shard_map/ppermute | solution.py:188
  67.8 2.8 %collective-permute-start.6 = (bf16[256,576]{1,0:T(8,128)(2,1)S(1)}, bf16[256,576]{1,0:T(8,128)(2,1)S(1)}, u32[]{:S(2)}, u32[]{:S(2)}) collective-permute-start(bf16[256,576]{1,0:T(8,128)(2,1)S(1)} %pad_maximum_fusion.1), channel_id=1, source_target_pairs={{0,4},{2,6},{4,0},{6,2},{1,5},{3,7},{5,1},{7,3},{8,12},{10,14},{12... | collective-permute-start | bytes 884744 | tf_op jit(solution)/shard_map/ppermute | solution.py:188
  70.6 4.5 %collective-permute-start.7 = (bf16[256,576]{1,0:T(8,128)(2,1)S(1)}, bf16[256,576]{1,0:T(8,128)(2,1)S(1)}, u32[]{:S(2)}, u32[]{:S(2)}) collective-permute-start(bf16[256,576]{1,0:T(8,128)(2,1)S(1)} %pad_maximum_fusion.1), channel_id=1, source_target_pairs={{0,6},{2,0},{4,2},{6,4},{1,7},{3,1},{5,3},{7,5},{8,14},{10,8},{12,... | collective-permute-start | bytes 884744 | tf_op jit(solution)/shard_map/ppermute | solution.py:188
  75.1 1.5 collective-permute-done.5
  76.7 3.8 %collective-permute-done.6 = bf16[256,576]{1,0:T(8,128)(2,1)S(1)} collective-permute-done((bf16[256,576]{1,0:T(8,128)(2,1)S(1)}, bf16[256,576]{1,0:T(8,128)(2,1)S(1)}, u32[]{:S(2)}, u32[]{:S(2)}) %collective-permute-start.6) | collective-permute-done | bytes 294944 | tf_op jit(solution)/shard_map/ppermute | solution.py:188
  80.4 3.4 %collective-permute-done.7 = bf16[256,576]{1,0:T(8,128)(2,1)S(1)} collective-permute-done((bf16[256,576]{1,0:T(8,128)(2,1)S(1)}, bf16[256,576]{1,0:T(8,128)(2,1)S(1)}, u32[]{:S(2)}, u32[]{:S(2)}) %collective-permute-start.7) | collective-permute-done | bytes 294944 | tf_op jit(solution)/shard_map/ppermute | solution.py:188
  84.0 2.1 %collective-permute-start.8 = (bf16[4,16,16,576]{3,2,1,0:T(8,128)(2,1)S(1)}, bf16[4,16,16,576]{3,2,1,0:T(8,128)(2,1)}, u32[]{:S(2)}, u32[]{:S(2)}) collective-permute-start(bf16[4,16,16,576]{3,2,1,0:T(8,128)(2,1)S(1)} %bitcast.14), channel_id=1, source_target_pairs={{0,1},{1,0},{2,3},{3,2},{4,5},{5,4},{6,7},{7,6},{8,9},{9,8},{10,11... | collective-permute-start | bytes 3538952 | tf_op jit(solution)/shard_map/ppermute | solution.py:193
  86.5 0.7 reshape.30
  87.3 31.5 %all-to-all-start = ((bf16[32,4,576]{2,1,0:T(4,128)(2,1)}), bf16[32,4,576]{2,1,0:T(4,128)(2,1)S(1)}, u32[]{:S(2)}, u32[]{:S(2)}) async-start(bf16[32,4,576]{2,1,0:T(4,128)(2,1)} %reshape.30), calls=%async_computation | async-start | bytes 327680 | tf_op jit(solution)/shard_map/all_to_all | solution.py:183
  119.3 0.9 query.1
  120.3 1.1 copy-done.3
  121.4 31.5 %all-to-all-done = bf16[32,4,576]{2,1,0:T(4,128)(2,1)S(1)} async-done(((bf16[32,4,576]{2,1,0:T(4,128)(2,1)}), bf16[32,4,576]{2,1,0:T(4,128)(2,1)S(1)}, u32[]{:S(2)}, u32[]{:S(2)}) %all-to-all-start) | async-done | bytes 147488 | tf_op jit(solution)/shard_map/all_to_all | solution.py:183
  152.9 1.3 copy-done.4
  154.3 11.1 %attend.1 = bf16[128,1024]{1,0:T(8,128)(2,1)} custom-call(s32[9]{0:T(128)S(1)} %stack.39.refs_0_, s32[128,128]{1,0:T(8,128)S(1)} %get-tuple-element.4.refs_1_, s32[2,128]{1,0:T(2,128)S(1)} %copy-done.5, bf16[8,128,576]{2,1,0:T(8,128)(2,1)S(1)} %copy-done.4, bf16[128,576]{1,0:T(8,128)(2,1)S(1)} %copy.19.refs_4_.refs_2_, ...), custom_call_target="tpu_custom_call" | custom-call | flops 10000000000 | bytes 6000000 | tf_op jit(solution)/shard_map/attend/pallas_call | solution.py:198
  (29 shorter events, 1.9 us)
Async XLA Ops:
  1.7 29.6 %collective-permute-start = (bf16[16,576]{1,0:T(8,128)(2,1)S(1)}, bf16[16,576]{1,0:T(8,128)(2,1)S(1)}, u32[]{:S(2)}, u32[]{:S(2)}) collective-permute-start(bf16[16,576]{1,0:T(8,128)(2,1)S(1)} %constant_dynamic-slice_fusion), channel_id=1, source_target_pairs={{0,8},{8,16},{16,24},{24,32},{32,40},{40,48},{48,56},{56,64},{64,7... | collective-permute-start | bytes 55304 | tf_op jit(solution)/shard_map/ppermute | solution.py:171
  6.4 26.3 %collective-permute-start.1 = (bf16[16,576]{1,0:T(8,128)(2,1)S(1)}, bf16[16,576]{1,0:T(8,128)(2,1)S(1)}, u32[]{:S(2)}, u32[]{:S(2)}) collective-permute-start(bf16[16,576]{1,0:T(8,128)(2,1)S(1)} %constant_dynamic-slice_fusion), channel_id=1, source_target_pairs={{0,72},{8,80},{16,88},{24,96},{32,104},{40,112},{48,120},{56,128},... | collective-permute-start | bytes 55304 | tf_op jit(solution)/shard_map/ppermute | solution.py:171
  32.8 14.2 %collective-permute-start.2 = (bf16[32,576]{1,0:T(8,128)(2,1)S(1)}, bf16[32,576]{1,0:T(8,128)(2,1)S(1)}, u32[]{:S(2)}, u32[]{:S(2)}) collective-permute-start(bf16[32,576]{1,0:T(8,128)(2,1)S(1)} %constant_dynamic-update-slice_fusion), channel_id=1, source_target_pairs={{0,32},{8,40},{16,48},{24,56},{32,64},{40,72},{48,80},{56,88},{64,... | collective-permute-start | bytes 110600 | tf_op jit(solution)/shard_map/ppermute | solution.py:171
  47.0 10.2 %collective-permute-start.3 = (bf16[64,576]{1,0:T(8,128)(2,1)S(1)}, bf16[64,576]{1,0:T(8,128)(2,1)S(1)}, u32[]{:S(2)}, u32[]{:S(2)}) collective-permute-start(bf16[64,576]{1,0:T(8,128)(2,1)S(1)} %pad_maximum_fusion.3), channel_id=1, source_target_pairs={{0,16},{8,24},{16,32},{24,40},{32,48},{40,56},{48,64},{56,72},{64,... | collective-permute-start | bytes 221192 | tf_op jit(solution)/shard_map/ppermute | solution.py:171
  57.2 7.0 %collective-permute-start.4 = (bf16[128,576]{1,0:T(8,128)(2,1)S(1)}, bf16[128,576]{1,0:T(8,128)(2,1)S(1)}, u32[]{:S(2)}, u32[]{:S(2)}) collective-permute-start(bf16[128,576]{1,0:T(8,128)(2,1)S(1)} %pad_maximum_fusion.2), channel_id=1, source_target_pairs={{0,8},{8,16},{16,24},{24,32},{32,40},{40,48},{48,56},{56,64},{64,7... | collective-permute-start | bytes 442376 | tf_op jit(solution)/shard_map/ppermute | solution.py:171
  64.2 21.8 %copy-start.6 = (s32[128,1]{0,1:T(1,128)S(1)}, s32[128,1]{0,1:T(1,128)}, u32[]{:S(2)}) copy-start(s32[128,1]{0,1:T(1,128)} %param.10) | copy-start | bytes 1540
  64.2 12.4 %collective-permute-start.5 = (bf16[256,576]{1,0:T(8,128)(2,1)S(1)}, bf16[256,576]{1,0:T(8,128)(2,1)S(1)}, u32[]{:S(2)}, u32[]{:S(2)}) collective-permute-start(bf16[256,576]{1,0:T(8,128)(2,1)S(1)} %pad_maximum_fusion.1), channel_id=1, source_target_pairs={{0,2},{2,4},{4,6},{6,0},{1,3},{3,5},{5,7},{7,1},{8,10},{10,12},{12... | collective-permute-start | bytes 884744 | tf_op jit(solution)/shard_map/ppermute | solution.py:188
  67.8 12.6 %collective-permute-start.6 = (bf16[256,576]{1,0:T(8,128)(2,1)S(1)}, bf16[256,576]{1,0:T(8,128)(2,1)S(1)}, u32[]{:S(2)}, u32[]{:S(2)}) collective-permute-start(bf16[256,576]{1,0:T(8,128)(2,1)S(1)} %pad_maximum_fusion.1), channel_id=1, source_target_pairs={{0,4},{2,6},{4,0},{6,2},{1,5},{3,7},{5,1},{7,3},{8,12},{10,14},{12... | collective-permute-start | bytes 884744 | tf_op jit(solution)/shard_map/ppermute | solution.py:188
  70.6 13.2 %collective-permute-start.7 = (bf16[256,576]{1,0:T(8,128)(2,1)S(1)}, bf16[256,576]{1,0:T(8,128)(2,1)S(1)}, u32[]{:S(2)}, u32[]{:S(2)}) collective-permute-start(bf16[256,576]{1,0:T(8,128)(2,1)S(1)} %pad_maximum_fusion.1), channel_id=1, source_target_pairs={{0,6},{2,0},{4,2},{6,4},{1,7},{3,1},{5,3},{7,5},{8,14},{10,8},{12,... | collective-permute-start | bytes 884744 | tf_op jit(solution)/shard_map/ppermute | solution.py:188
  83.9 35.3 %copy-start = (bf16[8,128,512]{2,1,0:T(8,128)(2,1)S(1)}, bf16[8,128,512]{2,1,0:T(8,128)(2,1)}, u32[]{:S(2)}) copy-start(bf16[8,128,512]{2,1,0:T(8,128)(2,1)} %ak_ref.1) | copy-start | bytes 3145732
  83.9 35.3 %copy-start.1 = (bf16[128,1536]{1,0:T(8,128)(2,1)S(1)}, bf16[128,1536]{1,0:T(8,128)(2,1)}, u32[]{:S(2)}) copy-start(bf16[128,1536]{1,0:T(8,128)(2,1)} %q_ref.1) | copy-start | bytes 1179652
  84.0 35.3 %copy-start.2 = (s32[4096]{0:T(1024)S(1)}, s32[4096]{0:T(1024)}, u32[]{:S(2)}) copy-start(s32[4096]{0:T(1024)} %param.9) | copy-start | bytes 49156
  84.0 69.0 %collective-permute-start.8 = (bf16[4,16,16,576]{3,2,1,0:T(8,128)(2,1)S(1)}, bf16[4,16,16,576]{3,2,1,0:T(8,128)(2,1)}, u32[]{:S(2)}, u32[]{:S(2)}) collective-permute-start(bf16[4,16,16,576]{3,2,1,0:T(8,128)(2,1)S(1)} %bitcast.14), channel_id=1, source_target_pairs={{0,1},{1,0},{2,3},{3,2},{4,5},{5,4},{6,7},{7,6},{8,9},{9,8},{10,11... | collective-permute-start | bytes 3538952 | tf_op jit(solution)/shard_map/ppermute | solution.py:193
  87.3 65.7 %copy-start.5 = (s32[2,128]{1,0:T(2,128)S(1)}, s32[2,128]{1,0:T(2,128)}, u32[]{:S(2)}) copy-start(s32[2,128]{1,0:T(2,128)} %constant.63.clone.refs_2_) | copy-start | bytes 3076
  87.3 65.7 %all-to-all-start = ((bf16[32,4,576]{2,1,0:T(4,128)(2,1)}), bf16[32,4,576]{2,1,0:T(4,128)(2,1)S(1)}, u32[]{:S(2)}, u32[]{:S(2)}) async-start(bf16[32,4,576]{2,1,0:T(4,128)(2,1)} %reshape.30), calls=%async_computation | async-start | bytes 327680 | tf_op jit(solution)/shard_map/all_to_all | solution.py:183
  120.3 1.1 copy-start.3
  152.9 1.3 copy-start.4

commit v6 on v5

--- a/solution.py
+++ b/solution.py
@@ -60,29 +60,35 @@
     ).astype(jnp.bfloat16)
 
 
-def attend_kernel(meta_ref, start_ref, offset_ref, fq_ref, latent_ref, near_ref, far_ref,
-                  av_hbm, out_ref, bias_ref, av_ref, sem, *, scale, group):
+def attend_kernel(meta_ref, start_ref, offset_ref, fq_ref, *refs, scale, group, shares, skip, own, last):
     heads, rows = fq_ref.shape[0], fq_ref.shape[1]
-    parts = (near_ref, far_ref)
-    wide = near_ref.shape[0]
-    pieces = wide // (2 * rows)
-    values = pltpu.make_async_copy(av_hbm, av_ref, sem)
-    values.start()
+    refs = list(refs)
+    keys_ref = refs.pop(0)
+    parts = [keys_ref.at[pl.ds(skip, keys_ref.shape[0] - skip)]]
+    if own:
+        parts.append(refs.pop(0))
+    else:
+        max_ref, sum_ref, acc_ref = refs.pop(0), refs.pop(0), refs.pop(0)
+    if last:
+        av_hbm, out_ref, bias_ref, av_ref, sem = refs
+        values = pltpu.make_async_copy(av_hbm, av_ref, sem)
+        values.start()
+    else:
+        new_max_ref, new_sum_ref, new_acc_ref, bias_ref = refs
     start = start_ref[...]
     base = meta_ref[0] * rows
-    for n in range(len(parts)):
-        for i in range(pieces):
-            share_start = meta_ref[1 + n * pieces + i] * (rows // (2 * pieces))
-            for k in range(2):
-                seen = base + share_start + offset_ref[k:k + 1, :] >= start
-                at = n * wide + (2 * i + k) * rows
-                bias_ref[:, at:at + rows] = jnp.where(seen, 0.0, NEG)
-    lane = lax.broadcasted_iota(jnp.int32, (rows, rows), 1)
-    down = lax.broadcasted_iota(jnp.int32, (rows, rows), 0)
-    bias_ref[:, len(parts) * wide:] = jnp.where(
-        (base + lane >= start) & (lane <= down), 0.0, NEG)
+    for i, slot in enumerate(shares):
+        share_start = meta_ref[slot]
+        for k in range(2):
+            seen = base + share_start + offset_ref[k:k + 1, :] >= start
+            at = (2 * i + k) * rows
+            bias_ref[:, at:at + rows] = jnp.where(seen, 0.0, NEG)
+    wide = parts[0].shape[0]
+    if own:
+        lane = lax.broadcasted_iota(jnp.int32, (rows, rows), 1)
+        down = lax.broadcasted_iota(jnp.int32, (rows, rows), 0)
+        bias_ref[:, wide:] = jnp.where((base + lane >= start) & (lane <= down), 0.0, NEG)
     factor = scale * LOG2E
-    parts = parts + (latent_ref,)
     for h in range(0, heads, group):
         q = fq_ref[h:h + group].reshape(group * rows, WIDTH)
         scores = []
@@ -94,16 +100,27 @@
             scores.append(s.reshape(group, rows, -1) + bias[None])
         s = jnp.concatenate(scores, axis=2)
         top = jnp.max(s, axis=2, keepdims=True)
+        if not own:
+            before = max_ref[h:h + group][:, :, :1]
+            top = jnp.maximum(before, top)
         p = jnp.exp2((s - top) * factor)
         total = jnp.sum(p, axis=2, keepdims=True)
         p = p.astype(jnp.bfloat16).reshape(group * rows, -1)
-        mixed = jnp.zeros((group * rows, LATENT), jnp.float32)
-        for n, part in enumerate(parts):
+        mixed = jnp.dot(p[:, :wide], parts[0][:, :LATENT], preferred_element_type=jnp.float32)
+        if own:
             mixed = mixed + jnp.dot(
-                p[:, n * wide:n * wide + part.shape[0]], part[:, :LATENT],
-                preferred_element_type=jnp.float32,
-            )
-        mixed = (mixed.reshape(group, rows, LATENT) / total).astype(jnp.bfloat16)
+                p[:, wide:], parts[1][:, :LATENT], preferred_element_type=jnp.float32)
+        mixed = mixed.reshape(group, rows, LATENT)
+        if not own:
+            keep = jnp.exp2((before - top) * factor)
+            total = total + sum_ref[h:h + group][:, :, :1] * keep
+            mixed = mixed + acc_ref[h:h + group] * keep
+        if not last:
+            new_max_ref[h:h + group] = jnp.broadcast_to(top, (group, rows, 128))
+            new_sum_ref[h:h + group] = jnp.broadcast_to(total, (group, rows, 128))
+            new_acc_ref[h:h + group] = mixed
+            continue
+        mixed = (mixed / total).astype(jnp.bfloat16)
         if h == 0:
             values.wait()
         for g in range(group):
@@ -149,10 +166,11 @@
                    pltpu.VMEM((rows, rows), jnp.int32)),
         in_specs=[SMEM] + vmem(5), out_specs=tuple(vmem(2)), name="query", compiler_params=pltpu.CompilerParams(vmem_limit_bytes=16 << 20),
     )(ctx[None], queries, absorb_key, cos2, sin2, segments.reshape(-1, rows))
+    share = rows // (head_count * dec_count)
     from_head = [(head - k) % head_count for k in range(head_count)]
     meta = jnp.stack(
-        [ctx] + [f * dec_count + core for f in from_head]
-        + [f * dec_count + (1 - core) for f in from_head]
+        [ctx] + [(f * dec_count + core) * share for f in from_head]
+        + [(f * dec_count + 1 - core) * share for f in from_head]
     )
 
     slots = max(2, 2 * rows // (ctx_count * dec_count))
@@ -188,26 +206,43 @@
         lax.ppermute(window, "head", [(i, (i + k) % head_count) for i in range(head_count)])
         for k in range(1, head_count)
     ]
-    near = cat(window, *others)
-    near = near.reshape(head_count, 2 * len(EARLY), share, WIDTH)
+    near_flat = cat(window, *others)
+    near = near_flat.reshape(head_count, 2 * len(EARLY), share, WIDTH)
     far = lax.ppermute(near, "dec", [(i, (i + 1) % dec_count) for i in range(dec_count)])
-    keys = lambda x: KEEP(x.reshape(head_count * 2 * rows, WIDTH))
     offset = jnp.asarray(np.array(
         [[r % share - rows * d[r // share] for r in range(rows)] for d in (EARLY, LATE)], np.int32))
     group = 2
-    answer = pl.pallas_call(
-        lambda *refs: attend_kernel(*refs, scale=scale, group=group),
-        out_shape=jax.ShapeDtypeStruct((rows, heads * VDIM), bf16),
-        in_specs=[SMEM] + vmem(6) + [pl.BlockSpec(memory_space=pltpu.HBM)],
-        out_specs=vmem(1)[0],
-        scratch_shapes=[
-            pltpu.VMEM((rows, (1 + len(EARLY) + len(LATE)) * rows), jnp.float32),
-            pltpu.VMEM(absorb_value.shape, bf16), pltpu.SemaphoreType.DMA],
-        name="attend", compiler_params=pltpu.CompilerParams(vmem_limit_bytes=20 << 20),
-        cost_estimate=pl.CostEstimate(
-            flops=10_000_000_000, bytes_accessed=6_000_000, transcendentals=2_000_000),
-    )(meta, KEEP(start), offset, KEEP(full_query), KEEP(latent_rows), keys(near), keys(far),
-      pltpu.with_memory_space_constraint(absorb_value, pltpu.HBM))
+    state_shape = (pltpu.VMEM((heads, rows, 128), jnp.float32),
+                   pltpu.VMEM((heads, rows, 128), jnp.float32),
+                   pltpu.VMEM((heads, rows, LATENT), jnp.float32))
+
+    def attend(keys, shares, skip=0, state=(), own=(), values=()):
+        count = keys.shape[0] - skip + sum(x.shape[0] for x in own)
+        inputs = [KEEP(start), offset, KEEP(full_query), KEEP(keys)]
+        inputs += [KEEP(x) for x in own] + [KEEP(x) for x in state]
+        scratch = [pltpu.VMEM((rows, count), jnp.float32)]
+        if values:
+            scratch += [pltpu.VMEM(values[0].shape, bf16), pltpu.SemaphoreType.DMA]
+        specs = [SMEM] + vmem(len(inputs)) + [pl.BlockSpec(memory_space=pltpu.HBM) for _ in values]
+        inputs += [pltpu.with_memory_space_constraint(x, pltpu.HBM) for x in values]
+        out = jax.ShapeDtypeStruct((rows, heads * VDIM), bf16)
+        return pl.pallas_call(
+            lambda *refs: attend_kernel(*refs, scale=scale, group=group, shares=shares,
+                                        skip=skip, own=bool(own), last=bool(values)),
+            out_shape=out if values else state_shape,
+            in_specs=specs, out_specs=vmem(1)[0] if values else tuple(vmem(3)),
+            scratch_shapes=scratch,
+            compiler_params=pltpu.CompilerParams(vmem_limit_bytes=20 << 20),
+            cost_estimate=pl.CostEstimate(
+                flops=2_300_000 * count, bytes_accessed=6_000_000,
+                transcendentals=1000 * count),
+        )(meta, *inputs)
+
+    state = attend(window, (1,), own=(latent_rows,))
+    wide = window.shape[0]
+    state = attend(near_flat, (2, 3, 4), skip=wide, state=state)
+    answer = attend(far.reshape(near_flat.shape), (5, 6, 7, 8), state=state,
+                    values=(absorb_value,))
     return (answer, arrived[None])
 
 
@@ -221,6 +256,4 @@
         P(("head", "dec"), None, None),
     )
     out_specs = (P(("group", "ctx"), ("head", "dec")), P(("group", "ctx", "dec"), None, None, None))
-    return jax.shard_map(
-        program, mesh=mesh, in_specs=in_specs, out_specs=out_specs, check_vma=False
-    )
+    return jax.shard_map(program, mesh=mesh, in_specs=in_specs, out_specs=out_specs, check_vma=False)

time: 167 us -> 165 us (0.988)
  the two profiles are of different devices: /device:TPU:42 before, /device:TPU:34 now
where the time goes in v6:
time: 165 us
  starting transfers between devices  98.9 us (60%)
  waiting for transfers between devices  37.8 us (23%)
  Pallas kernels  16.1 us (10%)
  local copies, waits for them, and re-layouts  10.3 us (6%)
    ppermute x5, starting transfers between devices, shift(): return lax.ppermute(x, 'ctx', [(i, i + k) for i in range(ctx_count - k)])  54.4 us
    all_to_all x1, starting transfers between devices, program(): lax.all_to_all(outgoing, 'ctx', split_axis=0, concat_axis=0, tiled=True)  31.5 us
    all_to_all x1, waiting for transfers between devices, program(): lax.all_to_all(outgoing, 'ctx', split_axis=0, concat_axis=0, tiled=True)  21.1 us
    pallas_call x3, Pallas kernels, attend(): pl.pallas_call(lambda *refs: attend_kernel(*refs, scale=scale, group=grou...  14.8 us
    ppermute x3, starting transfers between devices, program(): lax.ppermute(window, 'head', [(i, (i + k) % head_count) for i in range(he...  11 us
    unnamed x24, local copies, waits for them, and re-layouts  9.47 us
    ppermute x3, waiting for transfers between devices, program(): lax.ppermute(window, 'head', [(i, (i + k) % head_count) for i in range(he...  8.7 us
    ppermute x5, waiting for transfers between devices, shift(): return lax.ppermute(x, 'ctx', [(i, i + k) for i in range(ctx_count - k)])  7.95 us
  transfers between devices with their start and end apart: 10, of which 8 were waited for; matrix products, arithmetic and copies ran while one was open for 1% of the time, Pallas kernels for 5%

profile of v6, /device:TPU:34, one launch (start us, length us, event | category | flops | bytes accessed | tf_op | source)
XLA Modules:
  0.0 164.7 jit_solution(1651608232218906378)
XLA Ops:
  1.7 4.7 %collective-permute-start = (bf16[16,576]{1,0:T(8,128)(2,1)S(1)}, bf16[16,576]{1,0:T(8,128)(2,1)S(1)}, u32[]{:S(2)}, u32[]{:S(2)}) collective-permute-start(bf16[16,576]{1,0:T(8,128)(2,1)S(1)} %constant_dynamic-slice_fusion), channel_id=1, source_target_pairs={{0,8},{8,16},{16,24},{24,32},{32,40},{40,48},{48,56},{56,64},{64,7... | collective-permute-start | bytes 55304 | tf_op jit(solution)/shard_map/ppermute | solution.py:189
  6.5 24.8 %collective-permute-start.1 = (bf16[16,576]{1,0:T(8,128)(2,1)S(1)}, bf16[16,576]{1,0:T(8,128)(2,1)S(1)}, u32[]{:S(2)}, u32[]{:S(2)}) collective-permute-start(bf16[16,576]{1,0:T(8,128)(2,1)S(1)} %constant_dynamic-slice_fusion), channel_id=1, source_target_pairs={{0,72},{8,80},{16,88},{24,96},{32,104},{40,112},{48,120},{56,128},... | collective-permute-start | bytes 55304 | tf_op jit(solution)/shard_map/ppermute | solution.py:189
  31.3 1.4 collective-permute-done.1
  32.8 12.5 %collective-permute-start.2 = (bf16[32,576]{1,0:T(8,128)(2,1)S(1)}, bf16[32,576]{1,0:T(8,128)(2,1)S(1)}, u32[]{:S(2)}, u32[]{:S(2)}) collective-permute-start(bf16[32,576]{1,0:T(8,128)(2,1)S(1)} %constant_dynamic-update-slice_fusion), channel_id=1, source_target_pairs={{0,32},{8,40},{16,48},{24,56},{32,64},{40,72},{48,80},{56,88},{64,... | collective-permute-start | bytes 110600 | tf_op jit(solution)/shard_map/ppermute | solution.py:189
  45.3 1.7 %collective-permute-done.2 = bf16[32,576]{1,0:T(8,128)(2,1)S(1)} collective-permute-done((bf16[32,576]{1,0:T(8,128)(2,1)S(1)}, bf16[32,576]{1,0:T(8,128)(2,1)S(1)}, u32[]{:S(2)}, u32[]{:S(2)}) %collective-permute-start.2) | collective-permute-done | bytes 36896 | tf_op jit(solution)/shard_map/ppermute | solution.py:189
  47.0 8.1 %collective-permute-start.3 = (bf16[64,576]{1,0:T(8,128)(2,1)S(1)}, bf16[64,576]{1,0:T(8,128)(2,1)S(1)}, u32[]{:S(2)}, u32[]{:S(2)}) collective-permute-start(bf16[64,576]{1,0:T(8,128)(2,1)S(1)} %pad_maximum_fusion.3), channel_id=1, source_target_pairs={{0,16},{8,24},{16,32},{24,40},{32,48},{40,56},{48,64},{56,72},{64,... | collective-permute-start | bytes 221192 | tf_op jit(solution)/shard_map/ppermute | solution.py:189
  55.1 2.0 %collective-permute-done.3 = bf16[64,576]{1,0:T(8,128)(2,1)S(1)} collective-permute-done((bf16[64,576]{1,0:T(8,128)(2,1)S(1)}, bf16[64,576]{1,0:T(8,128)(2,1)S(1)}, u32[]{:S(2)}, u32[]{:S(2)}) %collective-permute-start.3) | collective-permute-done | bytes 73760 | tf_op jit(solution)/shard_map/ppermute | solution.py:189
  57.2 4.2 %collective-permute-start.4 = (bf16[128,576]{1,0:T(8,128)(2,1)S(1)}, bf16[128,576]{1,0:T(8,128)(2,1)S(1)}, u32[]{:S(2)}, u32[]{:S(2)}) collective-permute-start(bf16[128,576]{1,0:T(8,128)(2,1)S(1)} %pad_maximum_fusion.2), channel_id=1, source_target_pairs={{0,8},{8,16},{16,24},{24,32},{32,40},{40,48},{48,56},{56,64},{64,7... | collective-permute-start | bytes 442376 | tf_op jit(solution)/shard_map/ppermute | solution.py:189
  61.4 2.8 %collective-permute-done.4 = bf16[128,576]{1,0:T(8,128)(2,1)S(1)} collective-permute-done((bf16[128,576]{1,0:T(8,128)(2,1)S(1)}, bf16[128,576]{1,0:T(8,128)(2,1)S(1)}, u32[]{:S(2)}, u32[]{:S(2)}) %collective-permute-start.4) | collective-permute-done | bytes 147488 | tf_op jit(solution)/shard_map/ppermute | solution.py:189
  64.3 3.7 %collective-permute-start.5 = (bf16[256,576]{1,0:T(8,128)(2,1)S(1)}, bf16[256,576]{1,0:T(8,128)(2,1)S(1)}, u32[]{:S(2)}, u32[]{:S(2)}) collective-permute-start(bf16[256,576]{1,0:T(8,128)(2,1)S(1)} %pad_maximum_fusion.1.refs_4_), channel_id=1, source_target_pairs={{0,2},{2,4},{4,6},{6,0},{1,3},{3,5},{5,7},{7,1},{8,10},{10,12},{12... | collective-permute-start | bytes 884744 | tf_op jit(solution)/shard_map/ppermute | solution.py:206
  68.0 2.8 %collective-permute-start.6 = (bf16[256,576]{1,0:T(8,128)(2,1)S(1)}, bf16[256,576]{1,0:T(8,128)(2,1)S(1)}, u32[]{:S(2)}, u32[]{:S(2)}) collective-permute-start(bf16[256,576]{1,0:T(8,128)(2,1)S(1)} %pad_maximum_fusion.1.refs_4_), channel_id=1, source_target_pairs={{0,4},{2,6},{4,0},{6,2},{1,5},{3,7},{5,1},{7,3},{8,12},{10,14},{12... | collective-permute-start | bytes 884744 | tf_op jit(solution)/shard_map/ppermute | solution.py:206
  70.8 4.5 %collective-permute-start.7 = (bf16[256,576]{1,0:T(8,128)(2,1)S(1)}, bf16[256,576]{1,0:T(8,128)(2,1)S(1)}, u32[]{:S(2)}, u32[]{:S(2)}) collective-permute-start(bf16[256,576]{1,0:T(8,128)(2,1)S(1)} %pad_maximum_fusion.1.refs_4_), channel_id=1, source_target_pairs={{0,6},{2,0},{4,2},{6,4},{1,7},{3,1},{5,3},{7,5},{8,14},{10,8},{12,... | collective-permute-start | bytes 884744 | tf_op jit(solution)/shard_map/ppermute | solution.py:206
  75.3 1.5 collective-permute-done.5
  76.8 3.8 %collective-permute-done.6 = bf16[256,576]{1,0:T(8,128)(2,1)S(1)} collective-permute-done((bf16[256,576]{1,0:T(8,128)(2,1)S(1)}, bf16[256,576]{1,0:T(8,128)(2,1)S(1)}, u32[]{:S(2)}, u32[]{:S(2)}) %collective-permute-start.6) | collective-permute-done | bytes 294944 | tf_op jit(solution)/shard_map/ppermute | solution.py:206
  80.6 3.4 %collective-permute-done.7 = bf16[256,576]{1,0:T(8,128)(2,1)S(1)} collective-permute-done((bf16[256,576]{1,0:T(8,128)(2,1)S(1)}, bf16[256,576]{1,0:T(8,128)(2,1)S(1)}, u32[]{:S(2)}, u32[]{:S(2)}) %collective-permute-start.7) | collective-permute-done | bytes 294944 | tf_op jit(solution)/shard_map/ppermute | solution.py:206
  84.1 2.0 %collective-permute-start.8 = (bf16[4,16,16,576]{3,2,1,0:T(8,128)(2,1)S(1)}, bf16[4,16,16,576]{3,2,1,0:T(8,128)(2,1)}, u32[]{:S(2)}, u32[]{:S(2)}) collective-permute-start(bf16[4,16,16,576]{3,2,1,0:T(8,128)(2,1)S(1)} %bitcast.14), channel_id=1, source_target_pairs={{0,1},{1,0},{2,3},{3,2},{4,5},{5,4},{6,7},{7,6},{8,9},{9,8},{10,11... | collective-permute-start | bytes 3538952 | tf_op jit(solution)/shard_map/ppermute | solution.py:211
  87.3 31.5 %all-to-all-start = ((bf16[32,4,576]{2,1,0:T(4,128)(2,1)}), bf16[32,4,576]{2,1,0:T(4,128)(2,1)}, u32[]{:S(2)}, u32[]{:S(2)}) async-start(bf16[32,4,576]{2,1,0:T(4,128)(2,1)} %reshape.30), calls=%async_computation | async-start | bytes 327680 | tf_op jit(solution)/shard_map/all_to_all | solution.py:201
  122.8 2.8 %shard_map.86 = (f32[8,128,128]{2,1,0:T(8,128)S(1)}, f32[8,128,128]{2,1,0:T(8,128)S(1)}, f32[8,128,512]{2,1,0:T(8,128)S(1)}) custom-call(s32[9]{0:T(128)S(1)} %stack.39.refs_0_, s32[128,128]{1,0:T(8,128)S(1)} %get-tuple-element.10.refs_1_, s32[2,128]{1,0:T(2,128)S(1)} %copy-done.6, bf16[8,128,576]{2,1,0:T(8,128)(2,1)S(1)} %copy-done.4, ...), custom_call_target="tpu_custom_call" | custom-call | flops 883200000 | bytes 6000000 | tf_op jit(solution)/shard_map/pallas_call | solution.py:229
  125.7 4.8 %shard_map.87 = (f32[8,128,128]{2,1,0:T(8,128)S(1)}, f32[8,128,128]{2,1,0:T(8,128)S(1)}, f32[8,128,512]{2,1,0:T(8,128)S(1)}) custom-call(s32[9]{0:T(128)S(1)} %stack.39.refs_0_, s32[128,128]{1,0:T(8,128)S(1)} %get-tuple-element.10.refs_1_, s32[2,128]{1,0:T(2,128)S(1)} %copy-done.6, bf16[8,128,576]{2,1,0:T(8,128)(2,1)S(1)} %copy-done.4, ...), custom_call_target="tpu_custom_call" | custom-call | flops 1766400000 | bytes 6000000 | tf_op jit(solution)/shard_map/pallas_call | solution.py:229
  130.4 1.3 copy-done.7
  131.8 21.1 %all-to-all-done = bf16[32,4,576]{2,1,0:T(4,128)(2,1)} async-done(((bf16[32,4,576]{2,1,0:T(4,128)(2,1)}), bf16[32,4,576]{2,1,0:T(4,128)(2,1)}, u32[]{:S(2)}, u32[]{:S(2)}) %all-to-all-start) | async-done | bytes 147488 | tf_op jit(solution)/shard_map/all_to_all | solution.py:201
  154.2 1.6 copy-done.8
  155.8 7.2 %shard_map.88 = bf16[128,1024]{1,0:T(8,128)(2,1)} custom-call(s32[9]{0:T(128)S(1)} %stack.39.refs_0_, s32[128,128]{1,0:T(8,128)S(1)} %get-tuple-element.10.refs_1_, s32[2,128]{1,0:T(2,128)S(1)} %copy-done.6, bf16[8,128,576]{2,1,0:T(8,128)(2,1)S(1)} %copy-done.5, bf16[1024,576]{1,0:T(8,128)(2,1)} %bitcast.11.refs_4_, ...), custom_call_target="tpu_custom_call" | custom-call | flops 2355200000 | bytes 6000000 | tf_op jit(solution)/shard_map/pallas_call | solution.py:229
  163.1 1.6 copy.24
  (37 shorter events, 7.7 us)
Async XLA Ops:
  0.6 85.4 %copy-start.9 = (s32[128,1]{0,1:T(1,128)S(1)}, s32[128,1]{0,1:T(1,128)}, u32[]{:S(2)}) copy-start(s32[128,1]{0,1:T(1,128)} %param.10) | copy-start | bytes 1540
  1.7 29.6 %collective-permute-start = (bf16[16,576]{1,0:T(8,128)(2,1)S(1)}, bf16[16,576]{1,0:T(8,128)(2,1)S(1)}, u32[]{:S(2)}, u32[]{:S(2)}) collective-permute-start(bf16[16,576]{1,0:T(8,128)(2,1)S(1)} %constant_dynamic-slice_fusion), channel_id=1, source_target_pairs={{0,8},{8,16},{16,24},{24,32},{32,40},{40,48},{48,56},{56,64},{64,7... | collective-permute-start | bytes 55304 | tf_op jit(solution)/shard_map/ppermute | solution.py:189
  6.5 26.3 %collective-permute-start.1 = (bf16[16,576]{1,0:T(8,128)(2,1)S(1)}, bf16[16,576]{1,0:T(8,128)(2,1)S(1)}, u32[]{:S(2)}, u32[]{:S(2)}) collective-permute-start(bf16[16,576]{1,0:T(8,128)(2,1)S(1)} %constant_dynamic-slice_fusion), channel_id=1, source_target_pairs={{0,72},{8,80},{16,88},{24,96},{32,104},{40,112},{48,120},{56,128},... | collective-permute-start | bytes 55304 | tf_op jit(solution)/shard_map/ppermute | solution.py:189
  32.8 14.2 %collective-permute-start.2 = (bf16[32,576]{1,0:T(8,128)(2,1)S(1)}, bf16[32,576]{1,0:T(8,128)(2,1)S(1)}, u32[]{:S(2)}, u32[]{:S(2)}) collective-permute-start(bf16[32,576]{1,0:T(8,128)(2,1)S(1)} %constant_dynamic-update-slice_fusion), channel_id=1, source_target_pairs={{0,32},{8,40},{16,48},{24,56},{32,64},{40,72},{48,80},{56,88},{64,... | collective-permute-start | bytes 110600 | tf_op jit(solution)/shard_map/ppermute | solution.py:189
  47.0 10.2 %collective-permute-start.3 = (bf16[64,576]{1,0:T(8,128)(2,1)S(1)}, bf16[64,576]{1,0:T(8,128)(2,1)S(1)}, u32[]{:S(2)}, u32[]{:S(2)}) collective-permute-start(bf16[64,576]{1,0:T(8,128)(2,1)S(1)} %pad_maximum_fusion.3), channel_id=1, source_target_pairs={{0,16},{8,24},{16,32},{24,40},{32,48},{40,56},{48,64},{56,72},{64,... | collective-permute-start | bytes 221192 | tf_op jit(solution)/shard_map/ppermute | solution.py:189
  57.2 7.0 %collective-permute-start.4 = (bf16[128,576]{1,0:T(8,128)(2,1)S(1)}, bf16[128,576]{1,0:T(8,128)(2,1)S(1)}, u32[]{:S(2)}, u32[]{:S(2)}) collective-permute-start(bf16[128,576]{1,0:T(8,128)(2,1)S(1)} %pad_maximum_fusion.2), channel_id=1, source_target_pairs={{0,8},{8,16},{16,24},{24,32},{32,40},{40,48},{48,56},{56,64},{64,7... | collective-permute-start | bytes 442376 | tf_op jit(solution)/shard_map/ppermute | solution.py:189
  64.2 55.1 %copy-start = (bf16[8,128,512]{2,1,0:T(8,128)(2,1)S(1)}, bf16[8,128,512]{2,1,0:T(8,128)(2,1)}, u32[]{:S(2)}) copy-start(bf16[8,128,512]{2,1,0:T(8,128)(2,1)} %ak_ref.1) | copy-start | bytes 3145732
  64.3 55.1 %copy-start.1 = (bf16[128,1536]{1,0:T(8,128)(2,1)S(1)}, bf16[128,1536]{1,0:T(8,128)(2,1)}, u32[]{:S(2)}) copy-start(bf16[128,1536]{1,0:T(8,128)(2,1)} %q_ref.1) | copy-start | bytes 1179652
  64.3 55.1 %copy-start.2 = (s32[4096]{0:T(1024)S(1)}, s32[4096]{0:T(1024)}, u32[]{:S(2)}) copy-start(s32[4096]{0:T(1024)} %param.9) | copy-start | bytes 49156
  64.3 12.5 %collective-permute-start.5 = (bf16[256,576]{1,0:T(8,128)(2,1)S(1)}, bf16[256,576]{1,0:T(8,128)(2,1)S(1)}, u32[]{:S(2)}, u32[]{:S(2)}) collective-permute-start(bf16[256,576]{1,0:T(8,128)(2,1)S(1)} %pad_maximum_fusion.1.refs_4_), channel_id=1, source_target_pairs={{0,2},{2,4},{4,6},{6,0},{1,3},{3,5},{5,7},{7,1},{8,10},{10,12},{12... | collective-permute-start | bytes 884744 | tf_op jit(solution)/shard_map/ppermute | solution.py:206
  68.0 12.6 %collective-permute-start.6 = (bf16[256,576]{1,0:T(8,128)(2,1)S(1)}, bf16[256,576]{1,0:T(8,128)(2,1)S(1)}, u32[]{:S(2)}, u32[]{:S(2)}) collective-permute-start(bf16[256,576]{1,0:T(8,128)(2,1)S(1)} %pad_maximum_fusion.1.refs_4_), channel_id=1, source_target_pairs={{0,4},{2,6},{4,0},{6,2},{1,5},{3,7},{5,1},{7,3},{8,12},{10,14},{12... | collective-permute-start | bytes 884744 | tf_op jit(solution)/shard_map/ppermute | solution.py:206
  70.8 13.2 %collective-permute-start.7 = (bf16[256,576]{1,0:T(8,128)(2,1)S(1)}, bf16[256,576]{1,0:T(8,128)(2,1)S(1)}, u32[]{:S(2)}, u32[]{:S(2)}) collective-permute-start(bf16[256,576]{1,0:T(8,128)(2,1)S(1)} %pad_maximum_fusion.1.refs_4_), channel_id=1, source_target_pairs={{0,6},{2,0},{4,2},{6,4},{1,7},{3,1},{5,3},{7,5},{8,14},{10,8},{12,... | collective-permute-start | bytes 884744 | tf_op jit(solution)/shard_map/ppermute | solution.py:206
  84.1 37.4 %copy-start.6 = (s32[2,128]{1,0:T(2,128)S(1)}, s32[2,128]{1,0:T(2,128)}, u32[]{:S(2)}) copy-start(s32[2,128]{1,0:T(2,128)} %constant.63.clone.refs_2_) | copy-start | bytes 3076
  84.1 68.8 %collective-permute-start.8 = (bf16[4,16,16,576]{3,2,1,0:T(8,128)(2,1)S(1)}, bf16[4,16,16,576]{3,2,1,0:T(8,128)(2,1)}, u32[]{:S(2)}, u32[]{:S(2)}) collective-permute-start(bf16[4,16,16,576]{3,2,1,0:T(8,128)(2,1)S(1)} %bitcast.14), channel_id=1, source_target_pairs={{0,1},{1,0},{2,3},{3,2},{4,5},{5,4},{6,7},{7,6},{8,9},{9,8},{10,11... | collective-permute-start | bytes 3538952 | tf_op jit(solution)/shard_map/ppermute | solution.py:211
  87.3 65.6 %all-to-all-start = ((bf16[32,4,576]{2,1,0:T(4,128)(2,1)}), bf16[32,4,576]{2,1,0:T(4,128)(2,1)}, u32[]{:S(2)}, u32[]{:S(2)}) async-start(bf16[32,4,576]{2,1,0:T(4,128)(2,1)} %reshape.30), calls=%async_computation | async-start | bytes 327680 | tf_op jit(solution)/shard_map/all_to_all | solution.py:201
  120.3 1.1 copy-start.3
  121.5 1.3 copy-start.4
  130.4 1.3 copy-start.7
  152.9 1.3 copy-start.5
  154.2 1.6 copy-start.8

commit v7 on v6

--- a/solution.py
+++ b/solution.py
@@ -202,10 +202,12 @@
     late = shift(eight, 1)
 
     window = cat(eight, late)
-    others = [
-        lax.ppermute(window, "head", [(i, (i + k) % head_count) for i in range(head_count)])
-        for k in range(1, head_count)
-    ]
+
+    def turn(k):
+        return lax.ppermute(window, "head", [(i, (i + k) % head_count) for i in range(head_count)])
+
+    others = [turn(1)]
+    others += [turn(k) for k in range(2, head_count)]
     near_flat = cat(window, *others)
     near = near_flat.reshape(head_count, 2 * len(EARLY), share, WIDTH)
     far = lax.ppermute(near, "dec", [(i, (i + 1) % dec_count) for i in range(dec_count)])
@@ -238,9 +240,8 @@
                 transcendentals=1000 * count),
         )(meta, *inputs)
 
-    state = attend(window, (1,), own=(latent_rows,))
-    wide = window.shape[0]
-    state = attend(near_flat, (2, 3, 4), skip=wide, state=state)
+    state = attend(cat(window, others[0]), (1, 2), own=(latent_rows,))
+    state = attend(near_flat, (3, 4), skip=2 * window.shape[0], state=state)
     answer = attend(far.reshape(near_flat.shape), (5, 6, 7, 8), state=state,
                     values=(absorb_value,))
     return (answer, arrived[None])

time: 165 us -> 166 us (level)
    unnamed x24 -> x30, local copies, waits for them, and re-layouts: 9.47 us -> 10.7 us
where the time goes in v7:
time: 166 us; the launch traced here: 165 us
  starting transfers between devices  98.7 us (59%)
  waiting for transfers between devices  36.9 us (22%)
  Pallas kernels  15.7 us (9%)
  local copies, waits for them, and re-layouts  11.5 us (7%)
    ppermute x5, starting transfers between devices, shift(): return lax.ppermute(x, 'ctx', [(i, i + k) for i in range(ctx_count - k)])  54.4 us
    all_to_all x1, starting transfers between devices, program(): lax.all_to_all(outgoing, 'ctx', split_axis=0, concat_axis=0, tiled=True)  31.4 us
    all_to_all x1, waiting for transfers between devices, program(): lax.all_to_all(outgoing, 'ctx', split_axis=0, concat_axis=0, tiled=True)  20.3 us
    pallas_call x3, Pallas kernels, attend(): pl.pallas_call(lambda *refs: attend_kernel(*refs, scale=scale, group=grou...  14.4 us
    ppermute x3, starting transfers between devices, turn(): lax.ppermute(window, 'head', [(i, (i + k) % head_count) for i in range(he...  10.8 us
    unnamed x30, local copies, waits for them, and re-layouts  10.7 us
    ppermute x3, waiting for transfers between devices, turn(): lax.ppermute(window, 'head', [(i, (i + k) % head_count) for i in range(he...  8.7 us
    ppermute x5, waiting for transfers between devices, shift(): return lax.ppermute(x, 'ctx', [(i, i + k) for i in range(ctx_count - k)])  7.95 us
  transfers between devices with their start and end apart: 10, of which 8 were waited for; matrix products, arithmetic and copies ran while one was open for 1% of the time, Pallas kernels for 5%

profile of v7, /device:TPU:34, one launch (start us, length us, event | category | flops | bytes accessed | tf_op | source)
XLA Modules:
  0.0 165.5 jit_solution(9873856165028309158)
XLA Ops:
  1.7 4.7 %collective-permute-start = (bf16[16,576]{1,0:T(8,128)(2,1)S(1)}, bf16[16,576]{1,0:T(8,128)(2,1)S(1)}, u32[]{:S(2)}, u32[]{:S(2)}) collective-permute-start(bf16[16,576]{1,0:T(8,128)(2,1)S(1)} %constant_dynamic-slice_fusion), channel_id=1, source_target_pairs={{0,8},{8,16},{16,24},{24,32},{32,40},{40,48},{48,56},{56,64},{64,7... | collective-permute-start | bytes 55304 | tf_op jit(solution)/shard_map/ppermute | solution.py:189
  6.4 24.8 %collective-permute-start.1 = (bf16[16,576]{1,0:T(8,128)(2,1)S(1)}, bf16[16,576]{1,0:T(8,128)(2,1)S(1)}, u32[]{:S(2)}, u32[]{:S(2)}) collective-permute-start(bf16[16,576]{1,0:T(8,128)(2,1)S(1)} %constant_dynamic-slice_fusion), channel_id=1, source_target_pairs={{0,72},{8,80},{16,88},{24,96},{32,104},{40,112},{48,120},{56,128},... | collective-permute-start | bytes 55304 | tf_op jit(solution)/shard_map/ppermute | solution.py:189
  31.3 1.4 collective-permute-done.1
  32.8 12.5 %collective-permute-start.2 = (bf16[32,576]{1,0:T(8,128)(2,1)S(1)}, bf16[32,576]{1,0:T(8,128)(2,1)S(1)}, u32[]{:S(2)}, u32[]{:S(2)}) collective-permute-start(bf16[32,576]{1,0:T(8,128)(2,1)S(1)} %constant_dynamic-update-slice_fusion), channel_id=1, source_target_pairs={{0,32},{8,40},{16,48},{24,56},{32,64},{40,72},{48,80},{56,88},{64,... | collective-permute-start | bytes 110600 | tf_op jit(solution)/shard_map/ppermute | solution.py:189
  45.3 1.7 %collective-permute-done.2 = bf16[32,576]{1,0:T(8,128)(2,1)S(1)} collective-permute-done((bf16[32,576]{1,0:T(8,128)(2,1)S(1)}, bf16[32,576]{1,0:T(8,128)(2,1)S(1)}, u32[]{:S(2)}, u32[]{:S(2)}) %collective-permute-start.2) | collective-permute-done | bytes 36896 | tf_op jit(solution)/shard_map/ppermute | solution.py:189
  47.0 8.1 %collective-permute-start.3 = (bf16[64,576]{1,0:T(8,128)(2,1)S(1)}, bf16[64,576]{1,0:T(8,128)(2,1)S(1)}, u32[]{:S(2)}, u32[]{:S(2)}) collective-permute-start(bf16[64,576]{1,0:T(8,128)(2,1)S(1)} %pad_maximum_fusion.4), channel_id=1, source_target_pairs={{0,16},{8,24},{16,32},{24,40},{32,48},{40,56},{48,64},{56,72},{64,... | collective-permute-start | bytes 221192 | tf_op jit(solution)/shard_map/ppermute | solution.py:189
  55.1 2.0 %collective-permute-done.3 = bf16[64,576]{1,0:T(8,128)(2,1)S(1)} collective-permute-done((bf16[64,576]{1,0:T(8,128)(2,1)S(1)}, bf16[64,576]{1,0:T(8,128)(2,1)S(1)}, u32[]{:S(2)}, u32[]{:S(2)}) %collective-permute-start.3) | collective-permute-done | bytes 73760 | tf_op jit(solution)/shard_map/ppermute | solution.py:189
  57.2 4.2 %collective-permute-start.4 = (bf16[128,576]{1,0:T(8,128)(2,1)S(1)}, bf16[128,576]{1,0:T(8,128)(2,1)S(1)}, u32[]{:S(2)}, u32[]{:S(2)}) collective-permute-start(bf16[128,576]{1,0:T(8,128)(2,1)S(1)} %pad_maximum_fusion.3), channel_id=1, source_target_pairs={{0,8},{8,16},{16,24},{24,32},{32,40},{40,48},{48,56},{56,64},{64,7... | collective-permute-start | bytes 442376 | tf_op jit(solution)/shard_map/ppermute | solution.py:189
  61.4 2.8 %collective-permute-done.4 = bf16[128,576]{1,0:T(8,128)(2,1)S(1)} collective-permute-done((bf16[128,576]{1,0:T(8,128)(2,1)S(1)}, bf16[128,576]{1,0:T(8,128)(2,1)S(1)}, u32[]{:S(2)}, u32[]{:S(2)}) %collective-permute-start.4) | collective-permute-done | bytes 147488 | tf_op jit(solution)/shard_map/ppermute | solution.py:189
  64.2 3.6 %collective-permute-start.5 = (bf16[256,576]{1,0:T(8,128)(2,1)S(1)}, bf16[256,576]{1,0:T(8,128)(2,1)S(1)}, u32[]{:S(2)}, u32[]{:S(2)}) collective-permute-start(bf16[256,576]{1,0:T(8,128)(2,1)S(1)} %pad_maximum_fusion.2), channel_id=1, source_target_pairs={{0,2},{2,4},{4,6},{6,0},{1,3},{3,5},{5,7},{7,1},{8,10},{10,12},{12... | collective-permute-start | bytes 884744 | tf_op jit(solution)/shard_map/ppermute | solution.py:207
  67.8 2.8 %collective-permute-start.6 = (bf16[256,576]{1,0:T(8,128)(2,1)S(1)}, bf16[256,576]{1,0:T(8,128)(2,1)S(1)}, u32[]{:S(2)}, u32[]{:S(2)}) collective-permute-start(bf16[256,576]{1,0:T(8,128)(2,1)S(1)} %pad_maximum_fusion.2), channel_id=1, source_target_pairs={{0,4},{2,6},{4,0},{6,2},{1,5},{3,7},{5,1},{7,3},{8,12},{10,14},{12... | collective-permute-start | bytes 884744 | tf_op jit(solution)/shard_map/ppermute | solution.py:207
  70.6 4.5 %collective-permute-start.7 = (bf16[256,576]{1,0:T(8,128)(2,1)S(1)}, bf16[256,576]{1,0:T(8,128)(2,1)S(1)}, u32[]{:S(2)}, u32[]{:S(2)}) collective-permute-start(bf16[256,576]{1,0:T(8,128)(2,1)S(1)} %pad_maximum_fusion.2), channel_id=1, source_target_pairs={{0,6},{2,0},{4,2},{6,4},{1,7},{3,1},{5,3},{7,5},{8,14},{10,8},{12,... | collective-permute-start | bytes 884744 | tf_op jit(solution)/shard_map/ppermute | solution.py:207
  75.1 1.5 collective-permute-done.5
  76.7 3.8 %collective-permute-done.6 = bf16[256,576]{1,0:T(8,128)(2,1)S(1)} collective-permute-done((bf16[256,576]{1,0:T(8,128)(2,1)S(1)}, bf16[256,576]{1,0:T(8,128)(2,1)S(1)}, u32[]{:S(2)}, u32[]{:S(2)}) %collective-permute-start.6) | collective-permute-done | bytes 294944 | tf_op jit(solution)/shard_map/ppermute | solution.py:207
  80.4 3.4 %collective-permute-done.7 = bf16[256,576]{1,0:T(8,128)(2,1)S(1)} collective-permute-done((bf16[256,576]{1,0:T(8,128)(2,1)S(1)}, bf16[256,576]{1,0:T(8,128)(2,1)S(1)}, u32[]{:S(2)}, u32[]{:S(2)}) %collective-permute-start.7) | collective-permute-done | bytes 294944 | tf_op jit(solution)/shard_map/ppermute | solution.py:207
  84.0 2.1 %collective-permute-start.8 = (bf16[4,16,16,576]{3,2,1,0:T(8,128)(2,1)S(1)}, bf16[4,16,16,576]{3,2,1,0:T(8,128)(2,1)}, u32[]{:S(2)}, u32[]{:S(2)}) collective-permute-start(bf16[4,16,16,576]{3,2,1,0:T(8,128)(2,1)S(1)} %bitcast.14), channel_id=1, source_target_pairs={{0,1},{1,0},{2,3},{3,2},{4,5},{5,4},{6,7},{7,6},{8,9},{9,8},{10,11... | collective-permute-start | bytes 3538952 | tf_op jit(solution)/shard_map/ppermute | solution.py:213
  87.3 31.4 %all-to-all-start = ((bf16[32,4,576]{2,1,0:T(4,128)(2,1)}), bf16[32,4,576]{2,1,0:T(4,128)(2,1)}, u32[]{:S(2)}, u32[]{:S(2)}) async-start(bf16[32,4,576]{2,1,0:T(4,128)(2,1)} %reshape.30), calls=%async_computation | async-start | bytes 327680 | tf_op jit(solution)/shard_map/all_to_all | solution.py:201
  122.5 3.7 %shard_map.86 = (f32[8,128,128]{2,1,0:T(8,128)S(1)}, f32[8,128,128]{2,1,0:T(8,128)S(1)}, f32[8,128,512]{2,1,0:T(8,128)S(1)}) custom-call(s32[9]{0:T(128)S(1)} %stack.39.refs_0_, s32[128,128]{1,0:T(8,128)S(1)} %get-tuple-element.10.refs_1_, s32[2,128]{1,0:T(2,128)S(1)} %copy-done.3, bf16[8,128,576]{2,1,0:T(8,128)(2,1)S(1)} %get-tuple-element.11.refs_3_, ...), custom_call_target="tpu_custom_call" | custom-call | flops 1472000000 | bytes 6000000 | tf_op jit(solution)/shard_map/pallas_call | solution.py:231
  126.2 3.5 %shard_map.87 = (f32[8,128,128]{2,1,0:T(8,128)S(1)}, f32[8,128,128]{2,1,0:T(8,128)S(1)}, f32[8,128,512]{2,1,0:T(8,128)S(1)}) custom-call(s32[9]{0:T(128)S(1)} %stack.39.refs_0_, s32[128,128]{1,0:T(8,128)S(1)} %get-tuple-element.10.refs_1_, s32[2,128]{1,0:T(2,128)S(1)} %copy-done.3, bf16[8,128,576]{2,1,0:T(8,128)(2,1)S(1)} %get-tuple-element.11.refs_3_, ...), custom_call_target="tpu_custom_call" | custom-call | flops 1177600000 | bytes 6000000 | tf_op jit(solution)/shard_map/pallas_call | solution.py:231
  129.7 1.3 copy-done.4
  132.6 20.3 %all-to-all-done = bf16[32,4,576]{2,1,0:T(4,128)(2,1)} async-done(((bf16[32,4,576]{2,1,0:T(4,128)(2,1)}), bf16[32,4,576]{2,1,0:T(4,128)(2,1)}, u32[]{:S(2)}, u32[]{:S(2)}) %all-to-all-start) | async-done | bytes 147488 | tf_op jit(solution)/shard_map/all_to_all | solution.py:201
  152.9 1.6 copy-done.5
  156.6 7.2 %shard_map.88 = bf16[128,1024]{1,0:T(8,128)(2,1)} custom-call(s32[9]{0:T(128)S(1)} %stack.39.refs_0_, s32[128,128]{1,0:T(8,128)S(1)} %get-tuple-element.10.refs_1_, s32[2,128]{1,0:T(2,128)S(1)} %copy-done.3, bf16[8,128,576]{2,1,0:T(8,128)(2,1)S(1)} %get-tuple-element.11.refs_3_, bf16[1024,576]{1,0:T(8,128)(2,1)} %bitcast.11.refs_4_, ...), custom_call_target="tpu_custom_call" | custom-call | flops 2355200000 | bytes 6000000 | tf_op jit(solution)/shard_map/pallas_call | solution.py:231
  163.8 1.6 copy.24
  (44 shorter events, 9.9 us)
Async XLA Ops:
  1.7 29.6 %collective-permute-start = (bf16[16,576]{1,0:T(8,128)(2,1)S(1)}, bf16[16,576]{1,0:T(8,128)(2,1)S(1)}, u32[]{:S(2)}, u32[]{:S(2)}) collective-permute-start(bf16[16,576]{1,0:T(8,128)(2,1)S(1)} %constant_dynamic-slice_fusion), channel_id=1, source_target_pairs={{0,8},{8,16},{16,24},{24,32},{32,40},{40,48},{48,56},{56,64},{64,7... | collective-permute-start | bytes 55304 | tf_op jit(solution)/shard_map/ppermute | solution.py:189
  6.4 26.3 %collective-permute-start.1 = (bf16[16,576]{1,0:T(8,128)(2,1)S(1)}, bf16[16,576]{1,0:T(8,128)(2,1)S(1)}, u32[]{:S(2)}, u32[]{:S(2)}) collective-permute-start(bf16[16,576]{1,0:T(8,128)(2,1)S(1)} %constant_dynamic-slice_fusion), channel_id=1, source_target_pairs={{0,72},{8,80},{16,88},{24,96},{32,104},{40,112},{48,120},{56,128},... | collective-permute-start | bytes 55304 | tf_op jit(solution)/shard_map/ppermute | solution.py:189
  32.8 14.2 %collective-permute-start.2 = (bf16[32,576]{1,0:T(8,128)(2,1)S(1)}, bf16[32,576]{1,0:T(8,128)(2,1)S(1)}, u32[]{:S(2)}, u32[]{:S(2)}) collective-permute-start(bf16[32,576]{1,0:T(8,128)(2,1)S(1)} %constant_dynamic-update-slice_fusion), channel_id=1, source_target_pairs={{0,32},{8,40},{16,48},{24,56},{32,64},{40,72},{48,80},{56,88},{64,... | collective-permute-start | bytes 110600 | tf_op jit(solution)/shard_map/ppermute | solution.py:189
  47.0 36.8 %copy-start.11 = (bf16[32,576]{1,0:T(8,128)(2,1)}, bf16[32,576]{1,0:T(8,128)(2,1)S(1)}, u32[]{:S(2)}) copy-start(bf16[32,576]{1,0:T(8,128)(2,1)S(1)} %collective-permute-done.2) | copy-start | bytes 110596
  47.0 10.2 %collective-permute-start.3 = (bf16[64,576]{1,0:T(8,128)(2,1)S(1)}, bf16[64,576]{1,0:T(8,128)(2,1)S(1)}, u32[]{:S(2)}, u32[]{:S(2)}) collective-permute-start(bf16[64,576]{1,0:T(8,128)(2,1)S(1)} %pad_maximum_fusion.4), channel_id=1, source_target_pairs={{0,16},{8,24},{16,32},{24,40},{32,48},{40,56},{48,64},{56,72},{64,... | collective-permute-start | bytes 221192 | tf_op jit(solution)/shard_map/ppermute | solution.py:189
  57.2 7.0 %collective-permute-start.4 = (bf16[128,576]{1,0:T(8,128)(2,1)S(1)}, bf16[128,576]{1,0:T(8,128)(2,1)S(1)}, u32[]{:S(2)}, u32[]{:S(2)}) collective-permute-start(bf16[128,576]{1,0:T(8,128)(2,1)S(1)} %pad_maximum_fusion.3), channel_id=1, source_target_pairs={{0,8},{8,16},{16,24},{24,32},{32,40},{40,48},{48,56},{56,64},{64,7... | collective-permute-start | bytes 442376 | tf_op jit(solution)/shard_map/ppermute | solution.py:189
  64.2 21.8 %copy-start.12 = (s32[128,1]{0,1:T(1,128)S(1)}, s32[128,1]{0,1:T(1,128)}, u32[]{:S(2)}) copy-start(s32[128,1]{0,1:T(1,128)} %param.10) | copy-start | bytes 1540
  64.2 12.4 %collective-permute-start.5 = (bf16[256,576]{1,0:T(8,128)(2,1)S(1)}, bf16[256,576]{1,0:T(8,128)(2,1)S(1)}, u32[]{:S(2)}, u32[]{:S(2)}) collective-permute-start(bf16[256,576]{1,0:T(8,128)(2,1)S(1)} %pad_maximum_fusion.2), channel_id=1, source_target_pairs={{0,2},{2,4},{4,6},{6,0},{1,3},{3,5},{5,7},{7,1},{8,10},{10,12},{12... | collective-permute-start | bytes 884744 | tf_op jit(solution)/shard_map/ppermute | solution.py:207
  67.8 12.6 %collective-permute-start.6 = (bf16[256,576]{1,0:T(8,128)(2,1)S(1)}, bf16[256,576]{1,0:T(8,128)(2,1)S(1)}, u32[]{:S(2)}, u32[]{:S(2)}) collective-permute-start(bf16[256,576]{1,0:T(8,128)(2,1)S(1)} %pad_maximum_fusion.2), channel_id=1, source_target_pairs={{0,4},{2,6},{4,0},{6,2},{1,5},{3,7},{5,1},{7,3},{8,12},{10,14},{12... | collective-permute-start | bytes 884744 | tf_op jit(solution)/shard_map/ppermute | solution.py:207
  70.6 13.2 %collective-permute-start.7 = (bf16[256,576]{1,0:T(8,128)(2,1)S(1)}, bf16[256,576]{1,0:T(8,128)(2,1)S(1)}, u32[]{:S(2)}, u32[]{:S(2)}) collective-permute-start(bf16[256,576]{1,0:T(8,128)(2,1)S(1)} %pad_maximum_fusion.2), channel_id=1, source_target_pairs={{0,6},{2,0},{4,2},{6,4},{1,7},{3,1},{5,3},{7,5},{8,14},{10,8},{12,... | collective-permute-start | bytes 884744 | tf_op jit(solution)/shard_map/ppermute | solution.py:207
  76.7 7.2 %copy-start.10 = (bf16[256,576]{1,0:T(8,128)(2,1)}, bf16[256,576]{1,0:T(8,128)(2,1)S(1)}, u32[]{:S(2)}) copy-start(bf16[256,576]{1,0:T(8,128)(2,1)S(1)} %collective-permute-done.5) | copy-start | bytes 884740
  83.9 35.2 %copy-start.1 = (bf16[128,1536]{1,0:T(8,128)(2,1)S(1)}, bf16[128,1536]{1,0:T(8,128)(2,1)}, u32[]{:S(2)}) copy-start(bf16[128,1536]{1,0:T(8,128)(2,1)} %q_ref.1) | copy-start | bytes 1179652
  84.0 35.2 %copy-start.2 = (s32[4096]{0:T(1024)S(1)}, s32[4096]{0:T(1024)}, u32[]{:S(2)}) copy-start(s32[4096]{0:T(1024)} %param.9) | copy-start | bytes 49156
  84.0 68.9 %collective-permute-start.8 = (bf16[4,16,16,576]{3,2,1,0:T(8,128)(2,1)S(1)}, bf16[4,16,16,576]{3,2,1,0:T(8,128)(2,1)}, u32[]{:S(2)}, u32[]{:S(2)}) collective-permute-start(bf16[4,16,16,576]{3,2,1,0:T(8,128)(2,1)S(1)} %bitcast.14), channel_id=1, source_target_pairs={{0,1},{1,0},{2,3},{3,2},{4,5},{5,4},{6,7},{7,6},{8,9},{9,8},{10,11... | collective-permute-start | bytes 3538952 | tf_op jit(solution)/shard_map/ppermute | solution.py:213
  87.3 65.7 %all-to-all-start = ((bf16[32,4,576]{2,1,0:T(4,128)(2,1)}), bf16[32,4,576]{2,1,0:T(4,128)(2,1)}, u32[]{:S(2)}, u32[]{:S(2)}) async-start(bf16[32,4,576]{2,1,0:T(4,128)(2,1)} %reshape.30), calls=%async_computation | async-start | bytes 327680 | tf_op jit(solution)/shard_map/all_to_all | solution.py:201
  119.2 1.2 copy-start
  120.4 2.1 %copy-start.3 = (s32[2,128]{1,0:T(2,128)S(1)}, s32[2,128]{1,0:T(2,128)}, u32[]{:S(2)}) copy-start(s32[2,128]{1,0:T(2,128)} %constant.63.clone.refs_2_) | copy-start | bytes 3076
  129.7 1.3 copy-start.4
  131.0 0.8 copy-start.6
  131.8 0.8 copy-start.8
  152.9 1.6 copy-start.5
  154.5 1.0 copy-start.7
  155.5 1.0 copy-start.9
